TPU v7x, 256 devices: a 4x2x16 block of a 4x16x16 slice. The times are simulated.
256 devices in a mesh: group: 2 (over y), station: 16 (over z), tm: 4 (over x), chan: 2 (over core).
Axes of the slice: x: 4, y: 2, z: 16, core: 2. Of those that a mesh axis runs over, the one named last changes fastest.
The devices are a block of a 4x16x16 slice.
Arguments:
- voltages: bfloat16 [32, 128, 2, 96, 512], P(('group', 'station'), 'chan', None, None, 'tm'), parts along dimension 0, may hold values from -6 to 6
- delays: int32 [32], P(('group', 'station')), parts along dimension 0, may hold values from 0 to 16, as said below
- tap_sets: int32 [32, 128], P(('group', 'station'), 'chan'), parts along dimension 0, may hold values from 0 to 15
- tap_table: bfloat16 [16, 16], replicated, may hold values from -1.5 to 1.5
- weights: bfloat16 [32, 128, 2, 96, 128], P(('group', 'station'), 'chan'), parts along dimension 0, may hold values from -0.15625 to 0.15625
Outputs:
- array_beams: bfloat16 [256, 2, 128, 512], P(('group', 'chan', 'station'), None, None, 'tm'), parts along dimension 0
There are 2 independent parts, one for each index of `group`. A program takes and returns all parts, laid end to end along the dimension named above; an argument that names none is the same for every part. Nothing has to cross between parts.
Inputs may be any that keep to these rules, and one draw needn't show every extreme that they name: `delays`: every delay lies in 0 to 16, and some station has delay 16.
All inputs are finite; a program needn't handle non-finite values.
Results may differ from a plain program's by a relative error of at most 0.0049.
Values may be sent and summed in bfloat16 or wider, within the bound.
No kernel may reach another device: no remote copies, remote signals or barrier semaphores. Data moves between devices by JAX's collectives and lax.ppermute only.
A program may use at most 64 MiB of HBM per device.

v0:
```python
import jax
import jax.numpy as jnp
from jax import lax
from jax.sharding import PartitionSpec as P

TAPS = 16
MAXD = 16
BLOCK = 128


def passed_along(value, axis, steps):
    count = lax.axis_size(axis)
    leading, last = (max(0, -steps), min(count, count - steps))
    return lax.ppermute(value, axis, [(source, source + steps) for source in range(leading, last)])


def steering_matrix(weights):
    real_w = weights[:, :, 0]
    imag_w = weights[:, :, 1]
    upper_rows = jnp.concatenate([real_w, imag_w], axis=-1)
    lower_rows = jnp.concatenate([-imag_w, real_w], axis=-1)
    return jnp.concatenate([upper_rows, lower_rows], axis=2)


def body(voltages, delays, tap_sets, tap_table, weights):
    station_number, channel_total, pairing_total, antenna_total, time_length = voltages.shape
    set_count, tap_count = tap_table.shape
    halo_len = MAXD + TAPS - 1
    window_len = BLOCK + halo_len
    flat_voltages = voltages.reshape(
        station_number, channel_total, pairing_total * antenna_total, time_length
    )
    prev_rim = passed_along(flat_voltages[..., time_length - halo_len :], "tm", 1)
    extended = jnp.concatenate([prev_rim, flat_voltages], axis=-1)
    windows = jnp.stack([extended], axis=3)
    set_onehot = (tap_sets[..., None] == jnp.arange(set_count)[None, None, :]).astype(jnp.bfloat16)
    chosen_taps = jnp.einsum(
        "scm,mk->sck", set_onehot, tap_table, preferred_element_type=jnp.float32
    ).astype(jnp.bfloat16)
    window_pos = jnp.arange(window_len)[:, None]
    output_pos = jnp.arange(BLOCK)[None, :]
    lag_table = output_pos + halo_len - window_pos
    station_lag = lag_table[None, :, :] - delays[:, None, None]
    tap_onehot = (station_lag[..., None] == jnp.arange(tap_count)[None, None, None, :]).astype(
        jnp.bfloat16
    )
    band_matrix = jnp.einsum(
        "sck,sjuk->scju", chosen_taps, tap_onehot, preferred_element_type=jnp.float32
    ).astype(jnp.bfloat16)
    delayed_voltages = jnp.einsum(
        "scanj,scju->scanu", windows, band_matrix, preferred_element_type=jnp.float32
    ).astype(jnp.bfloat16)
    delayed_voltages = delayed_voltages.reshape(
        station_number, channel_total, pairing_total * antenna_total, time_length
    )
    station_axis_size = lax.axis_size("station")
    row_count = channel_total // station_axis_size
    stacked = steering_matrix(weights)
    summed = lax.psum_scatter(
        jnp.einsum("scan,scat->cnt", stacked, delayed_voltages, preferred_element_type=jnp.float32),
        "station",
        scatter_dimension=0,
        tiled=True,
    )
    beam_count = weights.shape[-1]
    return summed.astype(jnp.bfloat16).reshape(row_count, 2, beam_count, time_length)


def solution(mesh):
    return jax.shard_map(
        body,
        mesh=mesh,
        in_specs=(
            P(("group", "station"), "chan", None, None, "tm"),
            P(("group", "station")),
            P(("group", "station"), "chan"),
            P(),
            P(("group", "station"), "chan", None, None, None),
        ),
        out_specs=P(("group", "chan", "station"), None, None, "tm"),
        check_vma=False,
    )
```

profile of v0, /device:TPU:33, one launch (start us, length us, event | category | flops | bytes accessed | tf_op | source)
XLA Modules:
  0.0 187.2 jit_solution(5500585693136973122)
XLA Ops:
  6.5 0.0 copy-start
  6.6 0.0 reduce-scatter.2.cloned.1.call-start
  6.6 4.5 %slice.12 = bf16[1,64,192,31]{3,2,1,0:T(8,128)(2,1)} slice(bf16[1,64,192,128]{3,2,1,0:T(8,128)(2,1)} %bitcast.30), slice={[0:1], [0:64], [0:192], [97:128]} | slice | bytes 1523712 | tf_op jit(solution)/shard_map/slice | solution.py:33
  11.0 0.0 copy-start.4
  11.1 0.0 copy-start.1
  11.1 4.6 %copy.13 = bf16[1,64,192,31]{2,1,3,0:T(8,128)(2,1)} copy(bf16[1,64,192,31]{3,2,1,0:T(8,128)(2,1)} %slice.12) | data formatting | bytes 1523712 | tf_op jit(solution)/shard_map/slice | solution.py:33
  15.7 5.1 %collective-permute-start = (bf16[1,64,192,31]{2,1,3,0:T(8,128)(2,1)}, bf16[1,64,192,31]{2,1,3,0:T(8,128)(2,1)}, u32[]{:S(2)}, u32[]{:S(2)}) collective-permute-start(bf16[1,64,192,31]{2,1,3,0:T(8,128)(2,1)} %copy.13), channel_id=1, source_target_pairs={{0,2},{2,4},{4,6},{1,3},{3,5},{5,7},{8,10},{10,12},{12,14},{9,11},... | collective-permute-start | bytes 2285576 | tf_op jit(solution)/shard_map/ppermute | solution.py:14
  21.4 0.0 copy-done
  21.4 0.0 copy-done.4
  21.5 2.6 %convolution_convert_fusion = bf16[64,159,128]{2,0,1:T(8,128)(2,1)} fusion(s32[159,128]{1,0:T(8,128)S(1)} %subtract_subtract_fusion, bf16[16,16]{1,0:T(8,128)(2,1)S(1)} %copy-done, s32[64]{0:T(128)S(1)} %bitcast.32), kind=kOutput, calls=%fused_computation.14 | convolution fusion | flops 43343872 | bytes 2687232 | tf_op jit(solution)/shard_map/sck,sjuk->scju/dot_general | solution.py:47
  24.1 0.0 copy-done.1
  24.1 5.0 %copy.15 = bf16[1,64,192,128]{2,3,1,0:T(8,128)(2,1)} copy(bf16[1,64,192,128]{3,2,1,0:T(8,128)(2,1)S(1)} %bitcast.31) | data formatting | bytes 6291456 | tf_op jit(solution)/shard_map/reshape | solution.py:30
  29.0 0.0 copy-start.2
  29.0 2.9 %fusion.22 = bf16[1,64,96,128]{3,2,1,0:T(8,128)(2,1)} fusion(bf16[1,64,2,96,128]{4,3,2,1,0:T(8,128)(2,1)} %param.9), kind=kLoop, calls=%fused_computation.26 | loop fusion | flops 786432 | bytes 3145728 | tf_op jit(solution)/shard_map/neg | solution.py:21
  31.9 0.0 copy-done.2
  31.9 0.0 copy-start.3
  31.9 1.8 slice_bitcast_fusion
  33.8 0.0 collective-permute-done
  33.8 2.8 %copy.14 = bf16[1,64,192,31]{2,3,1,0:T(8,128)(2,1)} copy(bf16[1,64,192,31]{2,1,3,0:T(8,128)(2,1)} %collective-permute-done) | data formatting | bytes 1523712 | tf_op jit(solution)/shard_map/ppermute | solution.py:14
  36.6 0.0 copy-done.3
  36.6 14.7 %fusion = f32[64,256,128]{2,1,0:T(8,128)} fusion(bf16[1,64,96,128]{3,2,1,0:T(8,128)(2,1)} %get-tuple-element.6, bf16[1,64,96,128]{3,2,1,0:T(8,128)(2,1)} %fusion.22, bf16[1,64,96,128]{3,2,1,0:T(8,128)(2,1)} %get-tuple-element.5, bf16[1,64,192,128]{2,3,1,0:T(8,128)(2,1)} %copy.15, bf16[1,64,192,31]{2,3,1,0:T(8,128)(2,1)} %copy.14, ...), kind=kOutput, calls=%fused_computation.1 | convolution fusion | flops 1340030976 | bytes 19619840 | tf_op jit(solution)/shard_map/scan,scat->cnt/dot_general | solution.py:60
  51.3 0.1 reduce-scatter.2.cloned.1.call-update
  51.3 127.3 %reduce-scatter.2.cloned.1.call-done = f32[4,256,128]{2,1,0:T(8,128)} async-done(((f32[64,256,128]{2,1,0:T(8,128)}), f32[4,256,128]{2,1,0:T(8,128)}) %reduce-scatter.2.cloned.1.call-update) | async-done | bytes 524304 | tf_op jit(solution)/shard_map/reduce_scatter | solution.py:59
  178.6 1.8 convert_element_type.20
  (2 shorter events, 0.0 us)
Async XLA Ops:
  6.5 14.9 %copy-start = (bf16[16,16]{1,0:T(8,128)(2,1)S(1)}, bf16[16,16]{1,0:T(8,128)(2,1)}, u32[]{:S(2)}) copy-start(bf16[16,16]{1,0:T(8,128)(2,1)} %param.8) | copy-start | bytes 1540
  6.6 172.1 %reduce-scatter.2.cloned.1.call-start = ((), (), s32[]{:S(2)}) async-start(), calls=%async_computation.1 | async-start | bytes 8912896 | tf_op jit(solution)/shard_map/reduce_scatter | solution.py:59
  11.0 10.4 %copy-start.4 = (s32[1,64]{1,0:T(1,128)S(1)}, s32[1,64]{1,0:T(1,128)}, u32[]{:S(2)}) copy-start(s32[1,64]{1,0:T(1,128)} %param.7) | copy-start | bytes 772
  11.1 13.0 %copy-start.1 = (bf16[1,64,2,96,128]{4,3,2,1,0:T(8,128)(2,1)S(1)}, bf16[1,64,2,96,128]{4,3,2,1,0:T(8,128)(2,1)}, u32[]{:S(2)}) copy-start(bf16[1,64,2,96,128]{4,3,2,1,0:T(8,128)(2,1)} %param.5) | copy-start | bytes 9437188
  15.7 18.1 %collective-permute-start = (bf16[1,64,192,31]{2,1,3,0:T(8,128)(2,1)}, bf16[1,64,192,31]{2,1,3,0:T(8,128)(2,1)}, u32[]{:S(2)}, u32[]{:S(2)}) collective-permute-start(bf16[1,64,192,31]{2,1,3,0:T(8,128)(2,1)} %copy.13), channel_id=1, source_target_pairs={{0,2},{2,4},{4,6},{1,3},{3,5},{5,7},{8,10},{10,12},{12,14},{9,11},... | collective-permute-start | bytes 2285576 | tf_op jit(solution)/shard_map/ppermute | solution.py:14
  29.0 2.9 %copy-start.2 = (bf16[1,64,2,96,128]{4,3,2,1,0:T(8,128)(2,1)S(1)}, bf16[1,64,2,96,128]{4,3,2,1,0:T(8,128)(2,1)}, u32[]{:S(2)}) copy-start(bf16[1,64,2,96,128]{4,3,2,1,0:T(8,128)(2,1)} %param.9) | copy-start | bytes 9437188
  31.9 4.7 %copy-start.3 = (bf16[64,159,128]{2,0,1:T(8,128)(2,1)S(1)}, bf16[64,159,128]{2,0,1:T(8,128)(2,1)}, u32[]{:S(2)}) copy-start(bf16[64,159,128]{2,0,1:T(8,128)(2,1)} %convolution_convert_fusion) | copy-start | bytes 7815172
Sparse Core Ops, SparseCore 0:
  51.4 127.1 reduce-scatter.1
where the time goes:
time: 187 us
  waiting for transfers between devices  127 us (68%)
  local copies, waits for them, and re-layouts  18.8 us (10%)
  matrix products  17.3 us (9%)
  between operations  14.1 us (8%)
  starting transfers between devices  5.06 us (3%)
  other arithmetic  4.7 us (3%)
    reduce_scatter x1, waiting for transfers between devices, body(): lax.psum_scatter(jnp.einsum('scan,scat->cnt', stacked, delayed_voltages,...  127 us
    dot_general x1, matrix products, body(): jnp.einsum('scan,scat->cnt', stacked, delayed_voltages, preferred_element...  14.7 us
    slice x2, local copies, waits for them, and re-layouts, body(): flat_voltages[..., time_length - halo_len:]  9.14 us
    ppermute x1, starting transfers between devices, passed_along(): lax.ppermute(value, axis, [(source, source + steps) for source in range(l...  5.06 us
    reshape x1, local copies, waits for them, and re-layouts, body(): voltages.reshape(station_number, channel_total, pairing_total * antenna_t...  4.95 us
  transfers between devices with their start and end apart: 2, of which 1 were waited for; matrix products, arithmetic and copies ran while one was open for 7% of the time, Pallas kernels for 0%

commit v1 on v0

v1 whole, which is shorter than its diff:
```python
import functools

import jax
import jax.numpy as jnp
from jax import lax
from jax.experimental import pallas as pl
from jax.experimental.pallas import tpu as pltpu
from jax.sharding import PartitionSpec as P


TAPS = 16
HALO = 32


ANY = pl.BlockSpec(memory_space=pl.ANY)
VMEM = pl.BlockSpec(memory_space=pltpu.VMEM)
SMEM = pl.BlockSpec(memory_space=pltpu.SMEM)
PARAMS = pltpu.CompilerParams(vmem_limit_bytes=16 * 1024 * 1024)


def near(value, space=pltpu.VMEM):
    return pltpu.with_memory_space_constraint(value, space)


def passed_along(value, axis, step, wrap):
    count = lax.axis_size(axis)
    pairs = [(source, (source + step) % count) for source in range(count)]
    if not wrap:
        pairs = [(source, target) for source, target in pairs if target == source + step]
    return lax.ppermute(value, axis, pairs)


def chunk_index(offset, count):
    return lax.rem(lax.axis_index("station") + (offset % count), count)


def pack_near_kernel(offsets, count, x_ref, packed_ref):
    rows, _, length = x_ref.shape[1:]
    for i, offset in enumerate(offsets):
        chunk = chunk_index(offset, count)
        packed_ref[i] = jnp.concatenate(
            [x_ref[chunk, q, :, length - HALO :] for q in range(rows)], axis=-1
        )


def pack_kernel(offsets, count, x_ref, packed_ref, buf, sem):
    copies = [
        pltpu.make_async_copy(x_ref.at[chunk_index(offset, count)], buf.at[i], sem.at[i])
        for i, offset in enumerate(offsets)
    ]
    for copy in copies:
        copy.start()
    rows = buf.shape[1]
    length = buf.shape[-1]
    for i, copy in enumerate(copies):
        copy.wait()
        packed_ref[i] = jnp.concatenate(
            [buf[i, q, :, length - HALO :] for q in range(rows)], axis=-1
        )


def pack(x, offsets, direct):
    count, rows, height, length = x.shape
    shape = pltpu.VMEM((len(offsets), height, rows * HALO), x.dtype)
    if direct:
        return pl.pallas_call(
            functools.partial(pack_near_kernel, offsets, count),
            out_shape=shape,
            in_specs=[VMEM],
            out_specs=VMEM,
            compiler_params=PARAMS,
            name="pack",
        )(near(x))
    return pl.pallas_call(
        functools.partial(pack_kernel, offsets, count),
        out_shape=shape,
        in_specs=[ANY],
        out_specs=VMEM,
        scratch_shapes=[
            pltpu.VMEM((len(offsets), rows, height, length), x.dtype),
            pltpu.SemaphoreType.DMA((len(offsets),)),
        ],
        compiler_params=PARAMS,
        name="pack",
    )(near(x, pltpu.HBM))


def bank_kernel(table_ref, delay_ref, x_ref, w_ref, main_ref, halo_ref, near_x_ref, near_w_ref, sem):
    sets, length, _ = main_ref.shape
    delay = delay_ref[0]
    block = 16
    copies = [
        pltpu.make_async_copy(x_ref, near_x_ref, sem.at[0]),
        pltpu.make_async_copy(w_ref, near_w_ref, sem.at[1]),
    ]
    for copy in copies:
        copy.start()

    def fill(ref, start, shift):
        row = lax.broadcasted_iota(jnp.int32, (block, ref.shape[-1]), 0) + start
        lane = lax.broadcasted_iota(jnp.int32, (block, ref.shape[-1]), 1)
        lag = row - delay + shift(lane)
        rows = [jnp.zeros(lag.shape, jnp.float32) for _ in range(sets)]
        for k in range(TAPS):
            hit = lag == k
            for m in range(sets):
                rows[m] = jnp.where(hit, table_ref[m, k], rows[m])
        for m in range(sets):
            ref[m, pl.ds(start, block), :] = rows[m].astype(ref.dtype)

    @pl.loop(0, length // block)
    def _(i):
        fill(main_ref, pl.multiple_of(i * block, block), lambda lane: -lane)

    @pl.loop(0, HALO // block)
    def _(i):
        fill(halo_ref, pl.multiple_of(i * block, block), lambda lane: HALO - lax.rem(lane, HALO))

    for copy in copies:
        copy.wait()


def bank(table, delays, x, w):
    length = x.shape[-1]
    sets = table.shape[0]
    return pl.pallas_call(
        bank_kernel,
        out_shape=(
            pltpu.VMEM((sets, length, length), jnp.bfloat16),
            pltpu.VMEM((sets, HALO, length), jnp.bfloat16),
            pltpu.VMEM(x.shape, x.dtype),
            pltpu.VMEM(w.shape, w.dtype),
        ),
        in_specs=[SMEM, SMEM, ANY, ANY],
        out_specs=(VMEM,) * 4,
        scratch_shapes=[pltpu.SemaphoreType.DMA((2,))],
        compiler_params=PARAMS,
        name="bank",
    )(near(table.astype(jnp.float32), pltpu.SMEM), near(delays, pltpu.SMEM), near(x, pltpu.HBM), near(w, pltpu.HBM))


def beam_kernel(parts, count, sets_ref, x_ref, w_ref, main_ref, edge_ref, halo_ref, *outs):
    _, rows, _, length = x_ref.shape
    lane_block = lax.broadcasted_iota(jnp.int32, (HALO, length), 1) // HALO
    nt = (((1,), (1,)), ((), ()))
    for offset, place, where in parts:
        chunk = chunk_index(offset, count)
        chosen = [sets_ref[0, chunk * rows + q] for q in range(rows)]
        edge = jnp.concatenate(
            [
                jnp.where(lane_block == q, edge_ref[chosen[q]], jnp.zeros((), jnp.bfloat16))
                for q in range(rows)
            ],
            axis=0,
        )
        early = lax.dot_general(edge, halo_ref[place], nt, preferred_element_type=jnp.float32)
        for q in range(rows):
            late = lax.dot_general(
                main_ref[chosen[q]], x_ref[chunk, q], nt, preferred_element_type=jnp.float32
            )
            delayed = jnp.concatenate(
                [late[:HALO] + early[q * HALO : (q + 1) * HALO], late[HALO:]], axis=0
            ).astype(jnp.bfloat16)
            real_w = w_ref[chunk, q, 0]
            imag_w = w_ref[chunk, q, 1]
            steer = jnp.concatenate(
                [
                    jnp.concatenate([real_w, imag_w], axis=-1),
                    jnp.concatenate([-imag_w, real_w], axis=-1),
                ],
                axis=0,
            )
            beams = jnp.dot(delayed, steer, preferred_element_type=jnp.float32)
            out, spot = where[q]
            outs[out][spot] = beams.astype(outs[out].dtype)


def beams_of(parts, out_rows, dtype, tap_sets, x, w, banks, halo):
    count, rows, height, length = x.shape
    beam_count = w.shape[-1]
    n_out = max(where[0] for part in parts for where in part[2]) + 1
    return pl.pallas_call(
        functools.partial(beam_kernel, parts, count),
        out_shape=(pltpu.VMEM((out_rows, length, 2 * beam_count), dtype),) * n_out,
        in_specs=[SMEM] + [VMEM] * 5,
        out_specs=(VMEM,) * n_out,
        cost_estimate=pl.CostEstimate(
            flops=len(parts) * rows * 2 * length * height * (length + 2 * beam_count),
            bytes_accessed=len(parts) * rows * height * (length + beam_count) * 2,
            transcendentals=0,
        ),
        compiler_params=PARAMS,
        name="beams",
    )(near(tap_sets, pltpu.SMEM), near(x), near(w), near(banks[0]), near(banks[1]), near(halo))


def join_kernel(right_ref, left_ref, own_right_ref, own_left_ref, to_right_ref, to_left_ref):
    split = right_ref.shape[0]
    whole = own_right_ref.shape[0]
    for q in range(whole):
        value = own_right_ref[q]
        if q < split:
            value = value + right_ref[q].astype(jnp.float32)
        to_right_ref[q] = value.astype(to_right_ref.dtype)
        value = own_left_ref[q]
        if q >= whole - left_ref.shape[0]:
            value = value + left_ref[q - whole + left_ref.shape[0]].astype(jnp.float32)
        to_left_ref[q] = value.astype(to_left_ref.dtype)


def join(right, left, own_right, own_left):
    shape = pltpu.VMEM(own_right.shape, right.dtype)
    return pl.pallas_call(
        join_kernel,
        out_shape=(shape, shape),
        in_specs=[VMEM] * 4,
        out_specs=(VMEM, VMEM),
        compiler_params=PARAMS,
        name="join",
    )(near(right), near(left), near(own_right), near(own_left))


def finish_kernel(right_ref, left_ref, own_ref, out_ref):
    rows, _, width = own_ref.shape
    half = width // 2
    for q in range(rows):
        total = (
            right_ref[q].astype(jnp.float32) + left_ref[q].astype(jnp.float32) + own_ref[q]
        )
        for part in range(2):
            out_ref[q, part] = total[:, part * half : (part + 1) * half].T.astype(out_ref.dtype)


def finish(right, left, own):
    rows, length, width = own.shape
    return pl.pallas_call(
        finish_kernel,
        out_shape=jax.ShapeDtypeStruct((rows, 2, width // 2, length), jnp.bfloat16),
        in_specs=[VMEM] * 3,
        out_specs=VMEM,
        compiler_params=PARAMS,
        name="finish",
    )(near(right), near(left), near(own))


def ring(voltages, delays, tap_sets, tap_table, weights):
    _, channels, pair, antennas, length = voltages.shape
    beam_count = weights.shape[-1]
    count = lax.axis_size("station")
    rows = channels // count
    half = count // 2
    split = rows // 2
    x = voltages.reshape(count, rows, pair * antennas, length)
    w = weights.reshape(count, rows, pair, antennas, beam_count)

    def around(s):
        return [half - s, s - half]

    pieces = [[half] + around(1)]
    pieces.append([o for s in range(2, 5) for o in around(s)])
    pieces.append([o for s in range(5, half) for o in around(s)] + [0])
    halos = {}

    def send_piece(i):
        packed = pack(near_x if i else x, pieces[i], i > 0)
        got = passed_along(packed, "tm", 1, False)
        halos.update({o: (got, place) for place, o in enumerate(pieces[i])})

    def own(offsets, split_rows, dtype):
        parts = []
        for j, o in enumerate(offsets):
            spots = [(j, q) for q in range(rows)]
            if split_rows:
                spots = [(0, q) if q < split else (1, q - split) for q in range(rows)]
            parts.append((o, halos[o][1], spots))
        return beams_of(
            parts, split if split_rows else rows, dtype, tap_sets, near_x, near_w, banks, halos[o][0]
        )

    send_piece(0)
    *banks, near_x, near_w = bank(tap_table, delays, x, w)
    right, left = own([half], True, jnp.bfloat16)
    send_piece(1)
    send_piece(2)
    for s in range(1, half + 1):
        right = passed_along(right, "station", 1, True)
        left = passed_along(left, "station", -1, True)
        if s == half:
            return finish(right, left, own([0], False, jnp.float32)[0])
        own_right, own_left = own(around(s), False, jnp.float32)
        if s == 1:
            right, left = join(right, left, own_right, own_left)
        else:
            right = (right.astype(jnp.float32) + own_right).astype(jnp.bfloat16)
            left = (left.astype(jnp.float32) + own_left).astype(jnp.bfloat16)


def solution(mesh):
    return jax.shard_map(
        ring,
        mesh=mesh,
        in_specs=(
            P(("group", "station"), "chan", None, None, "tm"),
            P(("group", "station")),
            P(("group", "station"), "chan"),
            P(),
            P(("group", "station"), "chan", None, None, None),
        ),
        out_specs=P(("group", "chan", "station"), None, None, "tm"),
        check_vma=False,
    )
```

time: 187 us -> 107 us (0.57)
  the two profiles are of different devices: /device:TPU:33 before, /device:TPU:42 now
where the time goes in v1:
time: 107 us
  starting transfers between devices  56.9 us (53%)
  waiting for transfers between devices  27.8 us (26%)
  Pallas kernels  20.3 us (19%)
    ppermute x19, starting transfers between devices, passed_along(): return lax.ppermute(value, axis, pairs)  56.9 us
    ppermute x19, waiting for transfers between devices, passed_along(): return lax.ppermute(value, axis, pairs)  27.8 us
    pallas_call x9, Pallas kernels, beams_of(): pl.pallas_call(functools.partial(beam_kernel, parts, count), out_shape=(p...  14 us
    pallas_call x1, Pallas kernels, bank(): pl.pallas_call(bank_kernel, out_shape=(pltpu.VMEM((sets, length, length),...  3.53 us
  transfers between devices with their start and end apart: 19, of which 8 were waited for; matrix products, arithmetic and copies ran while one was open for 1% of the time, Pallas kernels for 16%

profile of v1, /device:TPU:42, one launch (start us, length us, event | category | flops | bytes accessed | tf_op | source)
XLA Modules:
  0.0 106.9 jit_solution(1634123263693840939)
XLA Ops:
  0.0 1.3 %pack.3 = bf16[3,192,128]{2,1,0:T(8,128)(2,1)S(1)} custom-call(bf16[16,4,192,128]{3,2,1,0:T(8,128)(2,1)} %bitcast.2), custom_call_target="tpu_custom_call" | custom-call | tf_op jit(solution)/shard_map/pack/pallas_call | solution.py:74
  1.3 3.6 %collective-permute-start = (bf16[3,192,128]{2,1,0:T(8,128)(2,1)S(1)}, bf16[3,192,128]{2,1,0:T(8,128)(2,1)S(1)}, u32[]{:S(2)}, u32[]{:S(2)}) collective-permute-start(bf16[3,192,128]{2,1,0:T(8,128)(2,1)S(1)} %pack.3), channel_id=1, source_target_pairs={{0,2},{2,4},{4,6},{1,3},{3,5},{5,7},{8,10},{10,12},{12,14},{9,11},... | collective-permute-start | bytes 442376 | tf_op jit(solution)/shard_map/ppermute | solution.py:30
  5.6 3.5 %bank.1 = (bf16[16,128,128]{2,1,0:T(8,128)(2,1)S(1)}, bf16[16,32,128]{2,1,0:T(8,128)(2,1)S(1)}, bf16[16,4,192,128]{3,2,1,0:T(8,128)(2,1)S(1)}, bf16[16,4,2,96,128]{4,3,2,1,0:T(8,128)(2,1)S(1)}) custom-call(f32[16,16]{1,0:T(8,128)S(1)} %convert_element_type.75.table_ref, s32[1]{0:T(128)S(6)} %copy.6.delay_ref, bf16[16,4,192,128]{3,2,1,0:T(8,128)(2,1)} %bitcast.3, ...), custom_call_target="tpu_custom_call" | custom-call | tf_op jit(solution)/shard_map/bank/pallas_call | solution.py:126
  9.1 1.0 beams.9
  10.2 2.9 %collective-permute-start.1 = (bf16[2,128,256]{2,1,0:T(8,128)(2,1)S(1)}, bf16[2,128,256]{2,1,0:T(8,128)(2,1)S(1)}, u32[]{:S(2)}, u32[]{:S(2)}) collective-permute-start(bf16[2,128,256]{2,1,0:T(8,128)(2,1)S(1)} %get-tuple-element.31), channel_id=1, source_target_pairs={{0,8},{8,16},{16,24},{24,32},{32,40},{40,48},{48,56},{56,64},{64,7... | collective-permute-start | bytes 393224 | tf_op jit(solution)/shard_map/ppermute | solution.py:30
  13.0 19.7 %collective-permute-start.2 = (bf16[2,128,256]{2,1,0:T(8,128)(2,1)S(1)}, bf16[2,128,256]{2,1,0:T(8,128)(2,1)S(1)}, u32[]{:S(2)}, u32[]{:S(2)}) collective-permute-start(bf16[2,128,256]{2,1,0:T(8,128)(2,1)S(1)} %get-tuple-element.32), channel_id=1, source_target_pairs={{0,120},{8,0},{16,8},{24,16},{32,24},{40,32},{48,40},{56,48},{64,5... | collective-permute-start | bytes 393224 | tf_op jit(solution)/shard_map/ppermute | solution.py:30
  32.8 0.3 pack.4
  33.1 3.3 %collective-permute-start.4 = (bf16[6,192,128]{2,1,0:T(8,128)(2,1)S(1)}, bf16[6,192,128]{2,1,0:T(8,128)(2,1)S(1)}, u32[]{:S(2)}, u32[]{:S(2)}) collective-permute-start(bf16[6,192,128]{2,1,0:T(8,128)(2,1)S(1)} %pack.4), channel_id=1, source_target_pairs={{0,2},{2,4},{4,6},{1,3},{3,5},{5,7},{8,10},{10,12},{12,14},{9,11},... | collective-permute-start | bytes 884744 | tf_op jit(solution)/shard_map/ppermute | solution.py:30
  36.4 1.7 %beams.10 = (f32[4,128,256]{2,1,0:T(8,128)S(1)}, f32[4,128,256]{2,1,0:T(8,128)S(1)}) custom-call(s32[1,64]{1,0:T(1,128)S(1)} %copy-done, bf16[16,4,192,128]{3,2,1,0:T(8,128)(2,1)S(1)} %get-tuple-element.27.x_ref, bf16[16,4,2,96,128]{4,3,2,1,0:T(8,128)(2,1)S(1)} %get-tuple-element.28.w_ref, bf16[16,128,128]{2,1,0:T(8,128)(2,1)S(1)} %get-tuple-element.29.main_ref, ...), custom_call_target="tpu_custom_call" | custom-call | flops 150994944 | bytes 786432 | tf_op jit(solution)/shard_map/beams/pallas_call | solution.py:182
  38.1 0.1 join.1
  38.2 2.0 %collective-permute-start.12 = (bf16[4,128,256]{2,1,0:T(8,128)(2,1)S(1)}, bf16[4,128,256]{2,1,0:T(8,128)(2,1)S(1)}, u32[]{:S(2)}, u32[]{:S(2)}) collective-permute-start(bf16[4,128,256]{2,1,0:T(8,128)(2,1)S(1)} %get-tuple-element.42), channel_id=1, source_target_pairs={{0,120},{8,0},{16,8},{24,16},{32,24},{40,32},{48,40},{56,48},{64,5... | collective-permute-start | bytes 786440 | tf_op jit(solution)/shard_map/ppermute | solution.py:30
  40.2 0.3 pack.5
  40.6 3.3 %collective-permute-start.8 = (bf16[7,192,128]{2,1,0:T(8,128)(2,1)S(1)}, bf16[7,192,128]{2,1,0:T(8,128)(2,1)S(1)}, u32[]{:S(2)}, u32[]{:S(2)}) collective-permute-start(bf16[7,192,128]{2,1,0:T(8,128)(2,1)S(1)} %pack.5), channel_id=1, source_target_pairs={{0,2},{2,4},{4,6},{1,3},{3,5},{5,7},{8,10},{10,12},{12,14},{9,11},... | collective-permute-start | bytes 1032200 | tf_op jit(solution)/shard_map/ppermute | solution.py:30
  43.8 0.3 collective-permute-start.3
  44.1 1.7 %beams.11 = (f32[4,128,256]{2,1,0:T(8,128)S(1)}, f32[4,128,256]{2,1,0:T(8,128)S(1)}) custom-call(s32[1,64]{1,0:T(1,128)S(1)} %copy-done, bf16[16,4,192,128]{3,2,1,0:T(8,128)(2,1)S(1)} %get-tuple-element.27.x_ref, bf16[16,4,2,96,128]{4,3,2,1,0:T(8,128)(2,1)S(1)} %get-tuple-element.28.w_ref, bf16[16,128,128]{2,1,0:T(8,128)(2,1)S(1)} %get-tuple-element.29.main_ref, ...), custom_call_target="tpu_custom_call" | custom-call | flops 150994944 | bytes 786432 | tf_op jit(solution)/shard_map/beams/pallas_call | solution.py:182
  45.8 0.1 add_convert_fusion.5
  45.9 3.2 %collective-permute-start.13 = (bf16[4,128,256]{2,1,0:T(8,128)(2,1)S(1)}, bf16[4,128,256]{2,1,0:T(8,128)(2,1)S(1)}, u32[]{:S(2)}, u32[]{:S(2)}) collective-permute-start(bf16[4,128,256]{2,1,0:T(8,128)(2,1)S(1)} %add_convert_fusion.5), channel_id=1, source_target_pairs={{0,120},{8,0},{16,8},{24,16},{32,24},{40,32},{48,40},{56,48},{64,5... | collective-permute-start | bytes 786440 | tf_op jit(solution)/shard_map/ppermute | solution.py:30
  49.1 2.4 %collective-permute-done.3 = bf16[4,128,256]{2,1,0:T(8,128)(2,1)S(1)} collective-permute-done((bf16[4,128,256]{2,1,0:T(8,128)(2,1)S(1)}, bf16[4,128,256]{2,1,0:T(8,128)(2,1)S(1)}, u32[]{:S(2)}, u32[]{:S(2)}) %collective-permute-start.3) | collective-permute-done | bytes 262176 | tf_op jit(solution)/shard_map/ppermute | solution.py:30
  51.6 0.1 collective-permute-start.5
  51.8 1.7 %beams.12 = (f32[4,128,256]{2,1,0:T(8,128)S(1)}, f32[4,128,256]{2,1,0:T(8,128)S(1)}) custom-call(s32[1,64]{1,0:T(1,128)S(1)} %copy-done, bf16[16,4,192,128]{3,2,1,0:T(8,128)(2,1)S(1)} %get-tuple-element.27.x_ref, bf16[16,4,2,96,128]{4,3,2,1,0:T(8,128)(2,1)S(1)} %get-tuple-element.28.w_ref, bf16[16,128,128]{2,1,0:T(8,128)(2,1)S(1)} %get-tuple-element.29.main_ref, ...), custom_call_target="tpu_custom_call" | custom-call | flops 150994944 | bytes 786432 | tf_op jit(solution)/shard_map/beams/pallas_call | solution.py:182
  53.5 0.1 add_convert_fusion.4
  53.5 3.3 %collective-permute-start.14 = (bf16[4,128,256]{2,1,0:T(8,128)(2,1)S(1)}, bf16[4,128,256]{2,1,0:T(8,128)(2,1)S(1)}, u32[]{:S(2)}, u32[]{:S(2)}) collective-permute-start(bf16[4,128,256]{2,1,0:T(8,128)(2,1)S(1)} %add_convert_fusion.4), channel_id=1, source_target_pairs={{0,120},{8,0},{16,8},{24,16},{32,24},{40,32},{48,40},{56,48},{64,5... | collective-permute-start | bytes 786440 | tf_op jit(solution)/shard_map/ppermute | solution.py:30
  56.9 3.1 %collective-permute-done.5 = bf16[4,128,256]{2,1,0:T(8,128)(2,1)S(1)} collective-permute-done((bf16[4,128,256]{2,1,0:T(8,128)(2,1)S(1)}, bf16[4,128,256]{2,1,0:T(8,128)(2,1)S(1)}, u32[]{:S(2)}, u32[]{:S(2)}) %collective-permute-start.5) | collective-permute-done | bytes 262176 | tf_op jit(solution)/shard_map/ppermute | solution.py:30
  60.0 0.1 add_convert_fusion.10
  60.0 0.1 collective-permute-start.6
  60.2 1.7 %beams.13 = (f32[4,128,256]{2,1,0:T(8,128)S(1)}, f32[4,128,256]{2,1,0:T(8,128)S(1)}) custom-call(s32[1,64]{1,0:T(1,128)S(1)} %copy-done, bf16[16,4,192,128]{3,2,1,0:T(8,128)(2,1)S(1)} %get-tuple-element.27.x_ref, bf16[16,4,2,96,128]{4,3,2,1,0:T(8,128)(2,1)S(1)} %get-tuple-element.28.w_ref, bf16[16,128,128]{2,1,0:T(8,128)(2,1)S(1)} %get-tuple-element.29.main_ref, ...), custom_call_target="tpu_custom_call" | custom-call | flops 150994944 | bytes 786432 | tf_op jit(solution)/shard_map/beams/pallas_call | solution.py:182
  61.9 0.1 add_convert_fusion.3
  62.0 3.6 %collective-permute-start.15 = (bf16[4,128,256]{2,1,0:T(8,128)(2,1)S(1)}, bf16[4,128,256]{2,1,0:T(8,128)(2,1)S(1)}, u32[]{:S(2)}, u32[]{:S(2)}) collective-permute-start(bf16[4,128,256]{2,1,0:T(8,128)(2,1)S(1)} %add_convert_fusion.3), channel_id=1, source_target_pairs={{0,120},{8,0},{16,8},{24,16},{32,24},{40,32},{48,40},{56,48},{64,5... | collective-permute-start | bytes 786440 | tf_op jit(solution)/shard_map/ppermute | solution.py:30
  65.6 3.8 %collective-permute-done.6 = bf16[4,128,256]{2,1,0:T(8,128)(2,1)S(1)} collective-permute-done((bf16[4,128,256]{2,1,0:T(8,128)(2,1)S(1)}, bf16[4,128,256]{2,1,0:T(8,128)(2,1)S(1)}, u32[]{:S(2)}, u32[]{:S(2)}) %collective-permute-start.6) | collective-permute-done | bytes 262176 | tf_op jit(solution)/shard_map/ppermute | solution.py:30
  69.4 0.3 collective-permute-start.7
  69.8 1.7 %beams.14 = (f32[4,128,256]{2,1,0:T(8,128)S(1)}, f32[4,128,256]{2,1,0:T(8,128)S(1)}) custom-call(s32[1,64]{1,0:T(1,128)S(1)} %copy-done, bf16[16,4,192,128]{3,2,1,0:T(8,128)(2,1)S(1)} %get-tuple-element.27.x_ref, bf16[16,4,2,96,128]{4,3,2,1,0:T(8,128)(2,1)S(1)} %get-tuple-element.28.w_ref, bf16[16,128,128]{2,1,0:T(8,128)(2,1)S(1)} %get-tuple-element.29.main_ref, ...), custom_call_target="tpu_custom_call" | custom-call | flops 150994944 | bytes 786432 | tf_op jit(solution)/shard_map/beams/pallas_call | solution.py:182
  71.5 0.1 collective-permute-done.15
  71.6 3.8 %collective-permute-start.16 = (bf16[4,128,256]{2,1,0:T(8,128)(2,1)S(1)}, bf16[4,128,256]{2,1,0:T(8,128)(2,1)S(1)}, u32[]{:S(2)}, u32[]{:S(2)}) collective-permute-start(bf16[4,128,256]{2,1,0:T(8,128)(2,1)S(1)} %add_convert_fusion.2), channel_id=1, source_target_pairs={{0,120},{8,0},{16,8},{24,16},{32,24},{40,32},{48,40},{56,48},{64,5... | collective-permute-start | bytes 786440 | tf_op jit(solution)/shard_map/ppermute | solution.py:30
  75.4 4.5 %collective-permute-done.7 = bf16[4,128,256]{2,1,0:T(8,128)(2,1)S(1)} collective-permute-done((bf16[4,128,256]{2,1,0:T(8,128)(2,1)S(1)}, bf16[4,128,256]{2,1,0:T(8,128)(2,1)S(1)}, u32[]{:S(2)}, u32[]{:S(2)}) %collective-permute-start.7) | collective-permute-done | bytes 262176 | tf_op jit(solution)/shard_map/ppermute | solution.py:30
  80.1 0.1 collective-permute-start.9
  80.2 1.7 %beams.15 = (f32[4,128,256]{2,1,0:T(8,128)S(1)}, f32[4,128,256]{2,1,0:T(8,128)S(1)}) custom-call(s32[1,64]{1,0:T(1,128)S(1)} %copy-done, bf16[16,4,192,128]{3,2,1,0:T(8,128)(2,1)S(1)} %get-tuple-element.27.x_ref, bf16[16,4,2,96,128]{4,3,2,1,0:T(8,128)(2,1)S(1)} %get-tuple-element.28.w_ref, bf16[16,128,128]{2,1,0:T(8,128)(2,1)S(1)} %get-tuple-element.29.main_ref, ...), custom_call_target="tpu_custom_call" | custom-call | flops 150994944 | bytes 786432 | tf_op jit(solution)/shard_map/beams/pallas_call | solution.py:182
  81.9 0.1 add_convert_fusion.1
  82.0 3.6 %collective-permute-start.17 = (bf16[4,128,256]{2,1,0:T(8,128)(2,1)S(1)}, bf16[4,128,256]{2,1,0:T(8,128)(2,1)S(1)}, u32[]{:S(2)}, u32[]{:S(2)}) collective-permute-start(bf16[4,128,256]{2,1,0:T(8,128)(2,1)S(1)} %add_convert_fusion.1), channel_id=1, source_target_pairs={{0,120},{8,0},{16,8},{24,16},{32,24},{40,32},{48,40},{56,48},{64,5... | collective-permute-start | bytes 786440 | tf_op jit(solution)/shard_map/ppermute | solution.py:30
  85.6 4.0 %collective-permute-done.9 = bf16[4,128,256]{2,1,0:T(8,128)(2,1)S(1)} collective-permute-done((bf16[4,128,256]{2,1,0:T(8,128)(2,1)S(1)}, bf16[4,128,256]{2,1,0:T(8,128)(2,1)S(1)}, u32[]{:S(2)}, u32[]{:S(2)}) %collective-permute-start.9) | collective-permute-done | bytes 262176 | tf_op jit(solution)/shard_map/ppermute | solution.py:30
  89.6 0.1 collective-permute-start.10
  89.7 1.7 %beams.16 = (f32[4,128,256]{2,1,0:T(8,128)S(1)}, f32[4,128,256]{2,1,0:T(8,128)S(1)}) custom-call(s32[1,64]{1,0:T(1,128)S(1)} %copy-done, bf16[16,4,192,128]{3,2,1,0:T(8,128)(2,1)S(1)} %get-tuple-element.27.x_ref, bf16[16,4,2,96,128]{4,3,2,1,0:T(8,128)(2,1)S(1)} %get-tuple-element.28.w_ref, bf16[16,128,128]{2,1,0:T(8,128)(2,1)S(1)} %get-tuple-element.29.main_ref, ...), custom_call_target="tpu_custom_call" | custom-call | flops 150994944 | bytes 786432 | tf_op jit(solution)/shard_map/beams/pallas_call | solution.py:182
  91.5 0.1 add_convert_fusion
  91.5 3.3 %collective-permute-start.18 = (bf16[4,128,256]{2,1,0:T(8,128)(2,1)S(1)}, bf16[4,128,256]{2,1,0:T(8,128)(2,1)S(1)}, u32[]{:S(2)}, u32[]{:S(2)}) collective-permute-start(bf16[4,128,256]{2,1,0:T(8,128)(2,1)S(1)} %add_convert_fusion), channel_id=1, source_target_pairs={{0,120},{8,0},{16,8},{24,16},{32,24},{40,32},{48,40},{56,48},{64,5... | collective-permute-start | bytes 786440 | tf_op jit(solution)/shard_map/ppermute | solution.py:30
  94.9 3.4 %collective-permute-done.10 = bf16[4,128,256]{2,1,0:T(8,128)(2,1)S(1)} collective-permute-done((bf16[4,128,256]{2,1,0:T(8,128)(2,1)S(1)}, bf16[4,128,256]{2,1,0:T(8,128)(2,1)S(1)}, u32[]{:S(2)}, u32[]{:S(2)}) %collective-permute-start.10) | collective-permute-done | bytes 262176 | tf_op jit(solution)/shard_map/ppermute | solution.py:30
  98.3 0.1 collective-permute-start.11
  98.4 1.0 beams.17.own_ref
  99.5 6.5 %collective-permute-done.11.right_ref = bf16[4,128,256]{2,1,0:T(8,128)(2,1)S(1)} collective-permute-done((bf16[4,128,256]{2,1,0:T(8,128)(2,1)S(1)}, bf16[4,128,256]{2,1,0:T(8,128)(2,1)S(1)}, u32[]{:S(2)}, u32[]{:S(2)}) %collective-permute-start.11) | collective-permute-done | bytes 262176 | tf_op jit(solution)/shard_map/ppermute | solution.py:30
  106.0 0.9 finish.1
  (22 shorter events, 0.5 us)
Async XLA Ops:
  0.0 4.9 %copy-start.1 = (bf16[16,16]{1,0:T(8,128)(2,1)S(1)}, bf16[16,16]{1,0:T(8,128)(2,1)}, u32[]{:S(2)}) copy-start(bf16[16,16]{1,0:T(8,128)(2,1)} %param.8) | copy-start | bytes 1540
  1.3 7.8 %collective-permute-start = (bf16[3,192,128]{2,1,0:T(8,128)(2,1)S(1)}, bf16[3,192,128]{2,1,0:T(8,128)(2,1)S(1)}, u32[]{:S(2)}, u32[]{:S(2)}) collective-permute-start(bf16[3,192,128]{2,1,0:T(8,128)(2,1)S(1)} %pack.3), channel_id=1, source_target_pairs={{0,2},{2,4},{4,6},{1,3},{3,5},{5,7},{8,10},{10,12},{12,14},{9,11},... | collective-permute-start | bytes 442376 | tf_op jit(solution)/shard_map/ppermute | solution.py:30
  5.5 3.6 %copy-start = (s32[1,64]{1,0:T(1,128)S(1)}, s32[1,64]{1,0:T(1,128)}, u32[]{:S(2)}) copy-start(s32[1,64]{1,0:T(1,128)} %sets_ref.17) | copy-start | bytes 772
  10.2 28.0 %collective-permute-start.1 = (bf16[2,128,256]{2,1,0:T(8,128)(2,1)S(1)}, bf16[2,128,256]{2,1,0:T(8,128)(2,1)S(1)}, u32[]{:S(2)}, u32[]{:S(2)}) collective-permute-start(bf16[2,128,256]{2,1,0:T(8,128)(2,1)S(1)} %get-tuple-element.31), channel_id=1, source_target_pairs={{0,8},{8,16},{16,24},{24,32},{32,40},{40,48},{48,56},{56,64},{64,7... | collective-permute-start | bytes 393224 | tf_op jit(solution)/shard_map/ppermute | solution.py:30
  13.0 25.1 %collective-permute-start.2 = (bf16[2,128,256]{2,1,0:T(8,128)(2,1)S(1)}, bf16[2,128,256]{2,1,0:T(8,128)(2,1)S(1)}, u32[]{:S(2)}, u32[]{:S(2)}) collective-permute-start(bf16[2,128,256]{2,1,0:T(8,128)(2,1)S(1)} %get-tuple-element.32), channel_id=1, source_target_pairs={{0,120},{8,0},{16,8},{24,16},{32,24},{40,32},{48,40},{56,48},{64,5... | collective-permute-start | bytes 393224 | tf_op jit(solution)/shard_map/ppermute | solution.py:30
  33.1 11.0 %collective-permute-start.4 = (bf16[6,192,128]{2,1,0:T(8,128)(2,1)S(1)}, bf16[6,192,128]{2,1,0:T(8,128)(2,1)S(1)}, u32[]{:S(2)}, u32[]{:S(2)}) collective-permute-start(bf16[6,192,128]{2,1,0:T(8,128)(2,1)S(1)} %pack.4), channel_id=1, source_target_pairs={{0,2},{2,4},{4,6},{1,3},{3,5},{5,7},{8,10},{10,12},{12,14},{9,11},... | collective-permute-start | bytes 884744 | tf_op jit(solution)/shard_map/ppermute | solution.py:30
  38.2 7.6 %collective-permute-start.12 = (bf16[4,128,256]{2,1,0:T(8,128)(2,1)S(1)}, bf16[4,128,256]{2,1,0:T(8,128)(2,1)S(1)}, u32[]{:S(2)}, u32[]{:S(2)}) collective-permute-start(bf16[4,128,256]{2,1,0:T(8,128)(2,1)S(1)} %get-tuple-element.42), channel_id=1, source_target_pairs={{0,120},{8,0},{16,8},{24,16},{32,24},{40,32},{48,40},{56,48},{64,5... | collective-permute-start | bytes 786440 | tf_op jit(solution)/shard_map/ppermute | solution.py:30
  40.6 29.2 %collective-permute-start.8 = (bf16[7,192,128]{2,1,0:T(8,128)(2,1)S(1)}, bf16[7,192,128]{2,1,0:T(8,128)(2,1)S(1)}, u32[]{:S(2)}, u32[]{:S(2)}) collective-permute-start(bf16[7,192,128]{2,1,0:T(8,128)(2,1)S(1)} %pack.5), channel_id=1, source_target_pairs={{0,2},{2,4},{4,6},{1,3},{3,5},{5,7},{8,10},{10,12},{12,14},{9,11},... | collective-permute-start | bytes 1032200 | tf_op jit(solution)/shard_map/ppermute | solution.py:30
  43.8 7.7 %collective-permute-start.3 = (bf16[4,128,256]{2,1,0:T(8,128)(2,1)S(1)}, bf16[4,128,256]{2,1,0:T(8,128)(2,1)S(1)}, u32[]{:S(2)}, u32[]{:S(2)}) collective-permute-start(bf16[4,128,256]{2,1,0:T(8,128)(2,1)S(1)} %get-tuple-element.35), channel_id=1, source_target_pairs={{0,8},{8,16},{16,24},{24,32},{32,40},{40,48},{48,56},{56,64},{64,7... | collective-permute-start | bytes 786440 | tf_op jit(solution)/shard_map/ppermute | solution.py:30
  45.9 7.6 %collective-permute-start.13 = (bf16[4,128,256]{2,1,0:T(8,128)(2,1)S(1)}, bf16[4,128,256]{2,1,0:T(8,128)(2,1)S(1)}, u32[]{:S(2)}, u32[]{:S(2)}) collective-permute-start(bf16[4,128,256]{2,1,0:T(8,128)(2,1)S(1)} %add_convert_fusion.5), channel_id=1, source_target_pairs={{0,120},{8,0},{16,8},{24,16},{32,24},{40,32},{48,40},{56,48},{64,5... | collective-permute-start | bytes 786440 | tf_op jit(solution)/shard_map/ppermute | solution.py:30
  51.6 8.4 %collective-permute-start.5 = (bf16[4,128,256]{2,1,0:T(8,128)(2,1)S(1)}, bf16[4,128,256]{2,1,0:T(8,128)(2,1)S(1)}, u32[]{:S(2)}, u32[]{:S(2)}) collective-permute-start(bf16[4,128,256]{2,1,0:T(8,128)(2,1)S(1)} %add_convert_fusion.11), channel_id=1, source_target_pairs={{0,8},{8,16},{16,24},{24,32},{32,40},{40,48},{48,56},{56,64},{64,7... | collective-permute-start | bytes 786440 | tf_op jit(solution)/shard_map/ppermute | solution.py:30
  53.5 8.3 %collective-permute-start.14 = (bf16[4,128,256]{2,1,0:T(8,128)(2,1)S(1)}, bf16[4,128,256]{2,1,0:T(8,128)(2,1)S(1)}, u32[]{:S(2)}, u32[]{:S(2)}) collective-permute-start(bf16[4,128,256]{2,1,0:T(8,128)(2,1)S(1)} %add_convert_fusion.4), channel_id=1, source_target_pairs={{0,120},{8,0},{16,8},{24,16},{32,24},{40,32},{48,40},{56,48},{64,5... | collective-permute-start | bytes 786440 | tf_op jit(solution)/shard_map/ppermute | solution.py:30
  60.0 9.3 %collective-permute-start.6 = (bf16[4,128,256]{2,1,0:T(8,128)(2,1)S(1)}, bf16[4,128,256]{2,1,0:T(8,128)(2,1)S(1)}, u32[]{:S(2)}, u32[]{:S(2)}) collective-permute-start(bf16[4,128,256]{2,1,0:T(8,128)(2,1)S(1)} %add_convert_fusion.10), channel_id=1, source_target_pairs={{0,8},{8,16},{16,24},{24,32},{32,40},{40,48},{48,56},{56,64},{64,7... | collective-permute-start | bytes 786440 | tf_op jit(solution)/shard_map/ppermute | solution.py:30
  62.0 9.6 %collective-permute-start.15 = (bf16[4,128,256]{2,1,0:T(8,128)(2,1)S(1)}, bf16[4,128,256]{2,1,0:T(8,128)(2,1)S(1)}, u32[]{:S(2)}, u32[]{:S(2)}) collective-permute-start(bf16[4,128,256]{2,1,0:T(8,128)(2,1)S(1)} %add_convert_fusion.3), channel_id=1, source_target_pairs={{0,120},{8,0},{16,8},{24,16},{32,24},{40,32},{48,40},{56,48},{64,5... | collective-permute-start | bytes 786440 | tf_op jit(solution)/shard_map/ppermute | solution.py:30
  69.4 10.5 %collective-permute-start.7 = (bf16[4,128,256]{2,1,0:T(8,128)(2,1)S(1)}, bf16[4,128,256]{2,1,0:T(8,128)(2,1)S(1)}, u32[]{:S(2)}, u32[]{:S(2)}) collective-permute-start(bf16[4,128,256]{2,1,0:T(8,128)(2,1)S(1)} %add_convert_fusion.9), channel_id=1, source_target_pairs={{0,8},{8,16},{16,24},{24,32},{32,40},{40,48},{48,56},{56,64},{64,7... | collective-permute-start | bytes 786440 | tf_op jit(solution)/shard_map/ppermute | solution.py:30
  71.6 10.3 %collective-permute-start.16 = (bf16[4,128,256]{2,1,0:T(8,128)(2,1)S(1)}, bf16[4,128,256]{2,1,0:T(8,128)(2,1)S(1)}, u32[]{:S(2)}, u32[]{:S(2)}) collective-permute-start(bf16[4,128,256]{2,1,0:T(8,128)(2,1)S(1)} %add_convert_fusion.2), channel_id=1, source_target_pairs={{0,120},{8,0},{16,8},{24,16},{32,24},{40,32},{48,40},{56,48},{64,5... | collective-permute-start | bytes 786440 | tf_op jit(solution)/shard_map/ppermute | solution.py:30
  80.1 9.5 %collective-permute-start.9 = (bf16[4,128,256]{2,1,0:T(8,128)(2,1)S(1)}, bf16[4,128,256]{2,1,0:T(8,128)(2,1)S(1)}, u32[]{:S(2)}, u32[]{:S(2)}) collective-permute-start(bf16[4,128,256]{2,1,0:T(8,128)(2,1)S(1)} %add_convert_fusion.8), channel_id=1, source_target_pairs={{0,8},{8,16},{16,24},{24,32},{32,40},{40,48},{48,56},{56,64},{64,7... | collective-permute-start | bytes 786440 | tf_op jit(solution)/shard_map/ppermute | solution.py:30
  82.0 9.5 %collective-permute-start.17 = (bf16[4,128,256]{2,1,0:T(8,128)(2,1)S(1)}, bf16[4,128,256]{2,1,0:T(8,128)(2,1)S(1)}, u32[]{:S(2)}, u32[]{:S(2)}) collective-permute-start(bf16[4,128,256]{2,1,0:T(8,128)(2,1)S(1)} %add_convert_fusion.1), channel_id=1, source_target_pairs={{0,120},{8,0},{16,8},{24,16},{32,24},{40,32},{48,40},{56,48},{64,5... | collective-permute-start | bytes 786440 | tf_op jit(solution)/shard_map/ppermute | solution.py:30
  89.6 8.6 %collective-permute-start.10 = (bf16[4,128,256]{2,1,0:T(8,128)(2,1)S(1)}, bf16[4,128,256]{2,1,0:T(8,128)(2,1)S(1)}, u32[]{:S(2)}, u32[]{:S(2)}) collective-permute-start(bf16[4,128,256]{2,1,0:T(8,128)(2,1)S(1)} %add_convert_fusion.7), channel_id=1, source_target_pairs={{0,8},{8,16},{16,24},{24,32},{32,40},{40,48},{48,56},{56,64},{64,7... | collective-permute-start | bytes 786440 | tf_op jit(solution)/shard_map/ppermute | solution.py:30
  91.5 8.0 %collective-permute-start.18 = (bf16[4,128,256]{2,1,0:T(8,128)(2,1)S(1)}, bf16[4,128,256]{2,1,0:T(8,128)(2,1)S(1)}, u32[]{:S(2)}, u32[]{:S(2)}) collective-permute-start(bf16[4,128,256]{2,1,0:T(8,128)(2,1)S(1)} %add_convert_fusion), channel_id=1, source_target_pairs={{0,120},{8,0},{16,8},{24,16},{32,24},{40,32},{48,40},{56,48},{64,5... | collective-permute-start | bytes 786440 | tf_op jit(solution)/shard_map/ppermute | solution.py:30
  98.3 7.7 %collective-permute-start.11 = (bf16[4,128,256]{2,1,0:T(8,128)(2,1)S(1)}, bf16[4,128,256]{2,1,0:T(8,128)(2,1)S(1)}, u32[]{:S(2)}, u32[]{:S(2)}) collective-permute-start(bf16[4,128,256]{2,1,0:T(8,128)(2,1)S(1)} %add_convert_fusion.6), channel_id=1, source_target_pairs={{0,8},{8,16},{16,24},{24,32},{32,40},{40,48},{48,56},{56,64},{64,7... | collective-permute-start | bytes 786440 | tf_op jit(solution)/shard_map/ppermute | solution.py:30

commit v2 on v1

v2 whole, which is shorter than its diff:
```python
import functools

import jax
import jax.numpy as jnp
from jax import lax
from jax.experimental import pallas as pl
from jax.experimental.pallas import tpu as pltpu
from jax.sharding import PartitionSpec as P


TAPS = 16
HALO = 32


ANY = pl.BlockSpec(memory_space=pl.ANY)
VMEM = pl.BlockSpec(memory_space=pltpu.VMEM)
SMEM = pl.BlockSpec(memory_space=pltpu.SMEM)
PARAMS = pltpu.CompilerParams(vmem_limit_bytes=6 * 1024 * 1024)


def near(value, space=pltpu.VMEM):
    return pltpu.with_memory_space_constraint(value, space)


def from_earlier(value):
    return lax.ppermute(value, "tm", [(i, i + 1) for i in range(lax.axis_size("tm") - 1)])


def onward(value):
    count, cores = lax.axis_size("station"), lax.axis_size("chan")
    pairs = []
    for station in range(count):
        for core in range(cores):
            step = 1 if core % 2 == 0 else -1
            pairs.append((station * cores + core, (station + step) % count * cores + core))
    return lax.ppermute(value, ("station", "chan"), pairs)


def across_cores(value):
    cores = lax.axis_size("chan")
    return lax.ppermute(value, "chan", [(i, (i + 1) % cores) for i in range(cores)])


def chunk_index(offset, count):
    up = lax.rem(lax.axis_index("chan"), 2) == 0
    signed = jnp.where(up, offset % count, -offset % count)
    return lax.rem(lax.axis_index("station") + signed, count)


def side_by_side(channels):
    return jnp.concatenate([one[:, one.shape[-1] - HALO :] for one in channels], axis=-1)


def pack_near_kernel(offsets, count, x_ref, packed_ref):
    for i, offset in enumerate(offsets):
        chunk = chunk_index(offset, count)
        packed_ref[i] = side_by_side([x_ref[chunk, q] for q in range(x_ref.shape[1])])


def pack_kernel(offsets, count, x_ref, packed_ref, buf, sem):
    copies = [
        pltpu.make_async_copy(x_ref.at[chunk_index(offset, count)], buf.at[i], sem.at[i])
        for i, offset in enumerate(offsets)
    ]
    for copy in copies:
        copy.start()
    for i, copy in enumerate(copies):
        copy.wait()
        packed_ref[i] = side_by_side([buf[i, q] for q in range(buf.shape[1])])


def pack(x, offsets, direct):
    count, rows, height, length = x.shape
    shape = pltpu.VMEM((len(offsets), height, rows * HALO), x.dtype)
    if direct:
        return pl.pallas_call(
            functools.partial(pack_near_kernel, offsets, count),
            out_shape=shape,
            in_specs=[VMEM],
            out_specs=VMEM,
            compiler_params=PARAMS,
            name="pack",
        )(near(x))
    return pl.pallas_call(
        functools.partial(pack_kernel, offsets, count),
        out_shape=shape,
        in_specs=[ANY],
        out_specs=VMEM,
        scratch_shapes=[
            pltpu.VMEM((len(offsets), rows, height, length), x.dtype),
            pltpu.SemaphoreType.DMA((len(offsets),)),
        ],
        compiler_params=PARAMS,
        name="pack",
    )(near(x, pltpu.HBM))


def bank_kernel(
    offsets, count, delay_ref, table_ref, x_ref, w_ref,
    main_ref, edge_ref, near_x_ref, near_w_ref, packed_ref, sem,
):
    sets, length, _ = main_ref.shape
    copies = [
        pltpu.make_async_copy(x_ref, near_x_ref, sem.at[0]),
        pltpu.make_async_copy(w_ref, near_w_ref, sem.at[1]),
    ]
    for copy in copies:
        copy.start()
    tap = lax.broadcasted_iota(jnp.int32, (TAPS, length), 0)
    lane = lax.broadcasted_iota(jnp.int32, (TAPS, length), 1)
    back = delay_ref[0] + lane + tap
    hit = ((back == 0) | (back == length)).astype(jnp.bfloat16)
    first_rows = jnp.dot(table_ref[...], hit, preferred_element_type=jnp.float32)
    row = lax.broadcasted_iota(jnp.int32, (length, length), 0)
    own = lax.broadcasted_iota(jnp.int32, (length, length), 1) <= row
    lanes = lax.broadcasted_iota(jnp.int32, (HALO, length), 1)
    for m in range(sets):
        band = jnp.broadcast_to(first_rows[m : m + 1], (length, length))
        band = pltpu.roll(band, 0, 1, stride=1, stride_axis=0)
        main_ref[m] = jnp.where(own, band, 0.0).astype(main_ref.dtype)
        edge = jnp.where(lanes >= length - HALO, band[:HALO], 0.0)
        spread = edge
        for q in range(1, length // HALO):
            spread = spread + pltpu.roll(edge, q * HALO, 1)
        edge_ref[m] = spread.astype(edge_ref.dtype)
    for copy in copies:
        copy.wait()
    pack_near_kernel(offsets, count, near_x_ref, packed_ref)


def bank(table, delays, x, w, offsets):
    _, rows, height, length = x.shape
    sets = table.shape[0]
    return pl.pallas_call(
        functools.partial(bank_kernel, offsets, x.shape[0]),
        out_shape=(
            pltpu.VMEM((sets, length, length), jnp.bfloat16),
            pltpu.VMEM((sets, HALO, length), jnp.bfloat16),
            pltpu.VMEM(x.shape, x.dtype),
            pltpu.VMEM(w.shape, w.dtype),
            pltpu.VMEM((len(offsets), height, rows * HALO), x.dtype),
        ),
        in_specs=[SMEM, VMEM, ANY, ANY],
        out_specs=(VMEM,) * 5,
        scratch_shapes=[pltpu.SemaphoreType.DMA((2,))],
        compiler_params=PARAMS,
        name="bank",
    )(near(delays, pltpu.SMEM), table, near(x, pltpu.HBM), near(w, pltpu.HBM))


def settle_kernel(offsets, count, value_ref, *refs):
    out_ref, sem = refs[-2:]
    if offsets:
        copies = [
            pltpu.make_async_copy(value_ref.at[chunk_index(o, count)], out_ref.at[i], sem.at[i])
            for i, o in enumerate(offsets)
        ]
    else:
        copies = [pltpu.make_async_copy(value_ref, out_ref, sem.at[0])]
    for copy in copies:
        copy.start()
    for copy in copies:
        copy.wait()


def settle(value, offsets=(), after=()):
    shape = (len(offsets),) + value.shape[1:] if offsets else value.shape
    return pl.pallas_call(
        functools.partial(settle_kernel, offsets, value.shape[0]),
        out_shape=pltpu.VMEM(shape, value.dtype),
        in_specs=[ANY] + [VMEM] * len(after),
        out_specs=VMEM,
        scratch_shapes=[pltpu.SemaphoreType.DMA((max(1, len(offsets)),))],
        compiler_params=PARAMS,
        name="settle",
    )(value, *[near(one) for one in after])


FILTER, STEER, BOTH = range(3)


def work_kernel(jobs, count, rows, names, *refs):
    held = dict(zip(names, refs))
    outs = refs[len(names) :]
    nt = (((1,), (1,)), ((), ()))
    filters = 0
    for i, (what, offset, place) in enumerate(jobs):
        out = outs[-1].at[filters] if what == FILTER else outs[i]
        filters += what == FILTER
        chunk = chunk_index(offset, count)
        if what != STEER:
            x_ref = held["x"].at[chunk]
            length = x_ref.shape[-1]
            lane_block = lax.broadcasted_iota(jnp.int32, (HALO, length), 1) // HALO
            chosen = [held["sets"][0, chunk * rows + q] for q in range(rows)]
            edge = jnp.concatenate(
                [
                    jnp.where(lane_block == q, held["edge"][m], jnp.zeros((), jnp.bfloat16))
                    for q, m in enumerate(chosen)
                ],
                axis=0,
            )
            early = lax.dot_general(
                edge, held["halo"][place], nt, preferred_element_type=jnp.float32
            )
        w_ref = None
        if what == BOTH:
            w_ref = held["w"].at[chunk]
        elif what == STEER:
            w_ref = held["other_w"].at[held["other_w"].shape[0] - offset]
        for q in range(rows):
            if what == STEER:
                delayed = held["given"][place, q, :, : 2 * w_ref.shape[-2]]
            else:
                late = lax.dot_general(
                    held["main"][chosen[q]], x_ref[q], nt, preferred_element_type=jnp.float32
                )
                delayed = jnp.concatenate(
                    [late[:HALO] + early[q * HALO : (q + 1) * HALO], late[HALO:]], axis=0
                ).astype(jnp.bfloat16)
            if what == FILTER:
                spare = jnp.zeros((delayed.shape[0], out.shape[-1] - delayed.shape[1]), out.dtype)
                out[q] = jnp.concatenate([delayed, spare], axis=-1)
                continue
            real_w = w_ref[q, 0]
            imag_w = w_ref[q, 1]
            steer = jnp.concatenate(
                [
                    jnp.concatenate([real_w, imag_w], axis=-1),
                    jnp.concatenate([-imag_w, real_w], axis=-1),
                ],
                axis=0,
            )
            out[q] = jnp.dot(delayed, steer, preferred_element_type=jnp.float32).astype(out.dtype)


def work(jobs, dtypes, rows, count, length, height, width, **arrays):
    names = tuple(arrays)
    shapes = [pltpu.VMEM((rows, length, width), dtype) for dtype in dtypes]
    filters = sum(what == FILTER for what, _, _ in jobs)
    if filters:
        lanes = (height + 127) // 128 * 128
        shapes.append(pltpu.VMEM((filters, rows, length, lanes), jnp.bfloat16))
    flops = 0
    for what, _, _ in jobs:
        flops += 2 * rows * length * height * (
            (0 if what == STEER else length) + (0 if what == FILTER else width)
        )
    return pl.pallas_call(
        functools.partial(work_kernel, jobs, count, rows, names),
        out_shape=tuple(shapes),
        in_specs=[SMEM if name == "sets" else VMEM for name in names],
        out_specs=(VMEM,) * len(shapes),
        cost_estimate=pl.CostEstimate(flops=flops, bytes_accessed=flops // 256, transcendentals=0),
        compiler_params=PARAMS,
        name="work",
    )(*[near(value, pltpu.SMEM if name == "sets" else pltpu.VMEM) for name, value in arrays.items()])


def finish_kernel(right_ref, left_ref, own_ref, out_ref):
    rows, _, width = own_ref.shape
    half = width // 2
    for q in range(rows):
        total = (
            right_ref[q].astype(jnp.float32) + left_ref[q].astype(jnp.float32) + own_ref[q]
        )
        for part in range(2):
            out_ref[q, part] = total[:, part * half : (part + 1) * half].T.astype(out_ref.dtype)


def finish(right, left, own):
    rows, length, width = own.shape
    return pl.pallas_call(
        finish_kernel,
        out_shape=jax.ShapeDtypeStruct((rows, 2, width // 2, length), jnp.bfloat16),
        in_specs=[VMEM] * 3,
        out_specs=VMEM,
        compiler_params=PARAMS,
        name="finish",
    )(near(right), near(left), near(own))


def ring(voltages, delays, tap_sets, tap_table, weights):
    _, channels, pair, antennas, length = voltages.shape
    beam_count = weights.shape[-1]
    count = lax.axis_size("station")
    rows = channels // count
    half = count // 2
    height = pair * antennas
    x = voltages.reshape(count, rows, height, length)
    w = weights.reshape(count, rows, pair, antennas, beam_count)
    sizes = (rows, count, length, height, 2 * beam_count)
    wide, thin = jnp.float32, jnp.bfloat16

    pieces = [[half, half - 1, 1 - half]]
    pieces.append([o for s in (2, 3) for o in (half - s, s - half)])
    pieces.append([o for s in range(4, half) for o in (half - s, s - half)] + [0])
    halos = {}

    def use_piece(i, got, after=()):
        if after:
            got = settle(got, (), after)
        halos.update({o: (got, place) for place, o in enumerate(pieces[i])})

    packed = pack(x, pieces[0], False)
    use_piece(0, from_earlier(packed))
    main, edge, near_x, near_w, packed = bank(tap_table, delays, x, w, pieces[1])
    other_w = across_cores(w)
    second = packed
    common = {"sets": tap_sets, "main": main, "edge": edge, "x": near_x, "w": near_w}

    def filtered(offsets):
        jobs = tuple((FILTER, o, halos[o][1]) for o in offsets)
        return work(jobs, [], *sizes, **common, halo=halos[offsets[0]][0])[0]

    halo, place = halos[half]
    a, handed = work(
        ((BOTH, half, place), (FILTER, 1 - half, halos[1 - half][1])), [thin],
        *sizes, **common, halo=halo,
    )
    a_got = onward(a)
    given = {1: (across_cores(handed), 0)}
    other_w = settle(other_w, tuple(half - s for s in range(1, half)))
    halo, place = halos[half - 1]
    (own,) = work(((BOTH, half - 1, place),), [wide], *sizes, **common, halo=halo)
    second = from_earlier(second)
    packed = pack(near_x, pieces[2], True)
    (b,) = work(
        ((STEER, half - 1, 0),), [thin], *sizes, given=given[1][0], other_w=other_w
    )

    def send_filtered(first, last):
        over = filtered([s - half for s in range(first, last)])
        got = across_cores(over)
        got = settle(got)
        given.update({s: (got, s - first) for s in range(first, last)})

    for s in range(1, half):
        b_got = onward(b)
        a = (a_got.astype(wide) + own).astype(thin)
        a_got = onward(a)
        if s == 1:
            use_piece(1, second, (b,))
            send_filtered(2, 4)
            third = from_earlier(packed)
        elif s == 3:
            use_piece(2, third, (a, b))
            send_filtered(4, half)
        halo, place = halos[half - s - 1]
        if s == half - 1:
            (own,) = work(((BOTH, 0, place),), [wide], *sizes, **common, halo=halo)
            break
        job = (BOTH, half - s - 1, place)
        if s != 3:
            own, other = work(
                (job, (STEER, half - s - 1, given[s + 1][1])), [wide, wide], *sizes, **common,
                halo=halo, given=given[s + 1][0], other_w=other_w,
            )
        else:
            (own,) = work((job,), [wide], *sizes, **common, halo=halo)
            (other,) = work(
                ((STEER, half - s - 1, given[s + 1][1]),), [wide], *sizes,
                given=given[s + 1][0], other_w=other_w,
            )
        b = (b_got.astype(wide) + other).astype(thin)
    back = across_cores(b_got)
    return finish(a_got, back, own)


def solution(mesh):
    return jax.shard_map(
        ring,
        mesh=mesh,
        in_specs=(
            P(("group", "station"), "chan", None, None, "tm"),
            P(("group", "station")),
            P(("group", "station"), "chan"),
            P(),
            P(("group", "station"), "chan", None, None, None),
        ),
        out_specs=P(("group", "chan", "station"), None, None, "tm"),
        check_vma=False,
    )
```

time: 107 us -> 109 us (1.019)
  the two profiles are of different devices: /device:TPU:42 before, /device:TPU:33 now
where the time goes in v2:
time: 109 us; the launch traced here: 108 us
  starting transfers between devices  69.6 us (64%)
  Pallas kernels  22.1 us (20%)
  waiting for transfers between devices  14.7 us (13%)
    ppermute x5, starting transfers between devices, across_cores(): lax.ppermute(value, 'chan', [(i, (i + 1) % cores) for i in range(cores)])  31.8 us
    ppermute x15, starting transfers between devices, onward(): return lax.ppermute(value, ('station', 'chan'), pairs)  28.7 us
    pallas_call x13, Pallas kernels, work(): pl.pallas_call(functools.partial(work_kernel, jobs, count, rows, names),...  13.2 us
    ppermute x15, waiting for transfers between devices, onward(): return lax.ppermute(value, ('station', 'chan'), pairs)  12.5 us
    ppermute x3, starting transfers between devices, from_earlier(): lax.ppermute(value, 'tm', [(i, i + 1) for i in range(lax.axis_size('tm')...  9.1 us
    pallas_call x1, Pallas kernels, bank(): pl.pallas_call(functools.partial(bank_kernel, offsets, x.shape[0]), out_s...  3.83 us
    pallas_call x5, Pallas kernels, settle(): pl.pallas_call(functools.partial(settle_kernel, offsets, value.shape[0]),...  2.5 us
  transfers between devices with their start and end apart: 23, of which 11 were waited for; matrix products, arithmetic and copies ran while one was open for 1% of the time, Pallas kernels for 17%

profile of v2, /device:TPU:33, one launch (start us, length us, event | category | flops | bytes accessed | tf_op | source)
XLA Modules:
  0.0 108.2 jit_solution(15368911549616393712)
XLA Ops:
  0.0 20.4 %collective-permute-start.5 = (bf16[16,4,2,96,128]{4,3,2,1,0:T(8,128)(2,1)}, bf16[16,4,2,96,128]{4,3,2,1,0:T(8,128)(2,1)S(1)}, u32[]{:S(2)}, u32[]{:S(2)}) collective-permute-start(bf16[16,4,2,96,128]{4,3,2,1,0:T(8,128)(2,1)} %bitcast.4), channel_id=1, source_target_pairs={{0,1},{1,0},{2,3},{3,2},{4,5},{5,4},{6,7},{7,6},{8,9},{9,8},{10,11... | collective-permute-start | bytes 9437192 | tf_op jit(solution)/shard_map/ppermute | solution.py:41
  20.4 1.3 %pack.2 = bf16[3,192,128]{2,1,0:T(8,128)(2,1)S(1)} custom-call(bf16[16,4,192,128]{3,2,1,0:T(8,128)(2,1)} %bitcast.2), custom_call_target="tpu_custom_call" | custom-call | tf_op jit(solution)/shard_map/pack/pallas_call | solution.py:84
  21.7 1.3 %collective-permute-start = (bf16[3,192,128]{2,1,0:T(8,128)(2,1)S(1)}, bf16[3,192,128]{2,1,0:T(8,128)(2,1)S(1)}, u32[]{:S(2)}, u32[]{:S(2)}) collective-permute-start(bf16[3,192,128]{2,1,0:T(8,128)(2,1)S(1)} %pack.2), channel_id=1, source_target_pairs={{0,2},{2,4},{4,6},{1,3},{3,5},{5,7},{8,10},{10,12},{12,14},{9,11},... | collective-permute-start | bytes 442376 | tf_op jit(solution)/shard_map/ppermute | solution.py:26
  23.7 3.8 %bank.1 = (bf16[16,128,128]{2,1,0:T(8,128)(2,1)S(1)}, bf16[16,32,128]{2,1,0:T(8,128)(2,1)S(1)}, bf16[16,4,192,128]{3,2,1,0:T(8,128)(2,1)S(1)}, bf16[16,4,2,96,12...) custom-call(s32[1]{0:T(128)S(6)} %copy.6.delay_ref, bf16[16,16]{1,0:T(8,128)(2,1)S(1)} %copy-done.1, ...), custom_call_target="tpu_custom_call" | custom-call | tf_op jit(solution)/shard_map/bank/pallas_call | solution.py:134
  27.5 1.3 %work.13 = (bf16[4,128,256]{2,1,0:T(8,128)(2,1)S(1)}, bf16[1,4,128,256]{3,2,1,0:T(8,128)(2,1)S(1)}) custom-call(s32[1,64]{1,0:T(1,128)S(1)} %copy-done, bf16[16,128,128]{2,1,0:T(8,128)(2,1)S(1)} %get-tuple-element.22.refs_1_, bf16[16,32,128]{2,1,0:T(8,128)(2,1)S(1)} %get-tuple-element.23.refs_2_, ...), custom_call_target="tpu_custom_call" | custom-call | flops 100663296 | bytes 393216 | tf_op jit(solution)/shard_map/work/pallas_call | solution.py:249
  29.0 3.6 %collective-permute-start.3 = (bf16[4,192,128]{2,1,0:T(8,128)(2,1)S(1)}, bf16[4,192,128]{2,1,0:T(8,128)(2,1)S(1)}, u32[]{:S(2)}, u32[]{:S(2)}) collective-permute-start(bf16[4,192,128]{2,1,0:T(8,128)(2,1)S(1)} %get-tuple-element.27), channel_id=1, source_target_pairs={{0,2},{2,4},{4,6},{1,3},{3,5},{5,7},{8,10},{10,12},{12,14},{9,11},... | collective-permute-start | bytes 589832 | tf_op jit(solution)/shard_map/ppermute | solution.py:26
  32.6 1.9 %settle.5.refs_1_.refs_7_ = bf16[7,4,2,96,128]{4,3,2,1,0:T(8,128)(2,1)S(1)} custom-call(bf16[16,4,2,96,128]{4,3,2,1,0:T(8,128)(2,1)S(1)} %collective-permute-done.5.value_ref), custom_call_target="tpu_custom_call" | custom-call | tf_op jit(solution)/shard_map/settle/pallas_call | solution.py:168
  34.8 2.1 %collective-permute-done.3.value_ref = bf16[4,192,128]{2,1,0:T(8,128)(2,1)S(1)} collective-permute-done((bf16[4,192,128]{2,1,0:T(8,128)(2,1)S(1)}, bf16[4,192,128]{2,1,0:T(8,128)(2,1)S(1)}, u32[]{:S(2)}, u32[]{:S(2)}) %collective-permute-start.3) | collective-permute-done | bytes 196640 | tf_op jit(solution)/shard_map/ppermute | solution.py:26
  37.0 1.0 work.16
  38.1 1.0 collective-permute-start.6
  39.1 5.1 %collective-permute-start.1 = (bf16[4,128,256]{2,1,0:T(8,128)(2,1)S(1)}, bf16[4,128,256]{2,1,0:T(8,128)(2,1)S(1)}, u32[]{:S(2)}, u32[]{:S(2)}) collective-permute-start(bf16[4,128,256]{2,1,0:T(8,128)(2,1)S(1)} %get-tuple-element.26), channel_id=1, source_target_pairs={{0,8},{1,121},{8,16},{9,1},{16,24},{17,9},{24,32},{25,17},{32,40},... | collective-permute-start | bytes 786440 | tf_op jit(solution)/shard_map/ppermute | solution.py:36
  44.2 0.4 pack.3
  44.6 4.2 %collective-permute-start.9 = (bf16[9,192,128]{2,1,0:T(8,128)(2,1)S(1)}, bf16[9,192,128]{2,1,0:T(8,128)(2,1)S(1)}, u32[]{:S(2)}, u32[]{:S(2)}) collective-permute-start(bf16[9,192,128]{2,1,0:T(8,128)(2,1)S(1)} %pack.3), channel_id=1, source_target_pairs={{0,2},{2,4},{4,6},{1,3},{3,5},{5,7},{8,10},{10,12},{12,14},{9,11},... | collective-permute-start | bytes 1327112 | tf_op jit(solution)/shard_map/ppermute | solution.py:26
  48.8 1.0 work.14
  50.0 0.8 collective-permute-start.2
  50.8 1.2 %work.17 = (f32[4,128,256]{2,1,0:T(8,128)S(1)}, f32[4,128,256]{2,1,0:T(8,128)S(1)}) custom-call(s32[1,64]{1,0:T(1,128)S(1)} %copy-done, bf16[16,128,128]{2,1,0:T(8,128)(2,1)S(1)} %get-tuple-element.22.refs_1_, bf16[16,32,128]{2,1,0:T(8,128)(2,1)S(1)} %get-tuple-element.23.refs_2_, bf16[16,4,192,128]{3,2,1,0:T(8,128)(2,1)S(1)} %get-tuple-element.24.refs_3_.x_ref, ...), custom_call_target="tpu_custom_call" | custom-call | flops 125829120 | bytes 491520 | tf_op jit(solution)/shard_map/work/pallas_call | solution.py:249
  52.1 3.4 %collective-permute-done.10 = bf16[4,128,256]{2,1,0:T(8,128)(2,1)S(1)} collective-permute-done((bf16[4,128,256]{2,1,0:T(8,128)(2,1)S(1)}, bf16[4,128,256]{2,1,0:T(8,128)(2,1)S(1)}, u32[]{:S(2)}, u32[]{:S(2)}) %collective-permute-start.10) | collective-permute-done | bytes 262176 | tf_op jit(solution)/shard_map/ppermute | solution.py:36
  55.5 1.0 collective-permute-start.11
  56.5 1.4 %collective-permute-done.2 = bf16[4,128,256]{2,1,0:T(8,128)(2,1)S(1)} collective-permute-done((bf16[4,128,256]{2,1,0:T(8,128)(2,1)S(1)}, bf16[4,128,256]{2,1,0:T(8,128)(2,1)S(1)}, u32[]{:S(2)}, u32[]{:S(2)}) %collective-permute-start.2) | collective-permute-done | bytes 262176 | tf_op jit(solution)/shard_map/ppermute | solution.py:36
  58.0 1.3 %collective-permute-start.7 = (bf16[4,128,256]{2,1,0:T(8,128)(2,1)S(1)}, bf16[4,128,256]{2,1,0:T(8,128)(2,1)S(1)}, u32[]{:S(2)}, u32[]{:S(2)}) collective-permute-start(bf16[4,128,256]{2,1,0:T(8,128)(2,1)S(1)} %add_convert_fusion.11), channel_id=1, source_target_pairs={{0,8},{1,121},{8,16},{9,1},{16,24},{17,9},{24,32},{25,17},{32,40},... | collective-permute-start | bytes 786440 | tf_op jit(solution)/shard_map/ppermute | solution.py:36
  59.4 1.2 %work.18 = (f32[4,128,256]{2,1,0:T(8,128)S(1)}, f32[4,128,256]{2,1,0:T(8,128)S(1)}) custom-call(s32[1,64]{1,0:T(1,128)S(1)} %copy-done, bf16[16,128,128]{2,1,0:T(8,128)(2,1)S(1)} %get-tuple-element.22.refs_1_, bf16[16,32,128]{2,1,0:T(8,128)(2,1)S(1)} %get-tuple-element.23.refs_2_, bf16[16,4,192,128]{3,2,1,0:T(8,128)(2,1)S(1)} %get-tuple-element.24.refs_3_.x_ref, ...), custom_call_target="tpu_custom_call" | custom-call | flops 125829120 | bytes 491520 | tf_op jit(solution)/shard_map/work/pallas_call | solution.py:249
  60.6 0.6 collective-permute-done.11
  61.2 2.7 %collective-permute-done.7 = bf16[4,128,256]{2,1,0:T(8,128)(2,1)S(1)} collective-permute-done((bf16[4,128,256]{2,1,0:T(8,128)(2,1)S(1)}, bf16[4,128,256]{2,1,0:T(8,128)(2,1)S(1)}, u32[]{:S(2)}, u32[]{:S(2)}) %collective-permute-start.7) | collective-permute-done | bytes 262176 | tf_op jit(solution)/shard_map/ppermute | solution.py:36
  64.0 0.3 settle.8.refs_5_
  64.3 1.4 %work.20 = bf16[4,4,128,256]{3,2,1,0:T(8,128)(2,1)S(1)} custom-call(s32[1,64]{1,0:T(1,128)S(1)} %copy-done, bf16[16,128,128]{2,1,0:T(8,128)(2,1)S(1)} %get-tuple-element.22.refs_1_, bf16[16,32,128]{2,1,0:T(8,128)(2,1)S(1)} %get-tuple-element.23.refs_2_, bf16[16,4,192,128]{3,2,1,0:T(8,128)(2,1)S(1)} %get-tuple-element.24.refs_3_.x_ref, ...), custom_call_target="tpu_custom_call" | custom-call | flops 100663296 | bytes 393216 | tf_op jit(solution)/shard_map/work/pallas_call | solution.py:249
  65.6 1.8 %collective-permute-start.13 = (bf16[4,4,128,256]{3,2,1,0:T(8,128)(2,1)S(1)}, bf16[4,4,128,256]{3,2,1,0:T(8,128)(2,1)S(1)}, u32[]{:S(2)}, u32[]{:S(2)}) collective-permute-start(bf16[4,4,128,256]{3,2,1,0:T(8,128)(2,1)S(1)} %work.20), channel_id=1, source_target_pairs={{0,1},{1,0},{2,3},{3,2},{4,5},{5,4},{6,7},{7,6},{8,9},{9,8},{10,11... | collective-permute-start | bytes 3145736 | tf_op jit(solution)/shard_map/ppermute | solution.py:41
  67.4 0.5 collective-permute-start.17
  67.9 1.7 %collective-permute-start.8 = (bf16[4,128,256]{2,1,0:T(8,128)(2,1)S(1)}, bf16[4,128,256]{2,1,0:T(8,128)(2,1)S(1)}, u32[]{:S(2)}, u32[]{:S(2)}) collective-permute-start(bf16[4,128,256]{2,1,0:T(8,128)(2,1)S(1)} %add_convert_fusion.10.refs_0_), channel_id=1, source_target_pairs={{0,8},{1,121},{8,16},{9,1},{16,24},{17,9},{24,32},{25,17},{32,40},... | collective-permute-start | bytes 786440 | tf_op jit(solution)/shard_map/ppermute | solution.py:36
  69.6 1.0 work.19
  71.0 1.9 %collective-permute-done.17 = bf16[4,128,256]{2,1,0:T(8,128)(2,1)S(1)} collective-permute-done((bf16[4,128,256]{2,1,0:T(8,128)(2,1)S(1)}, bf16[4,128,256]{2,1,0:T(8,128)(2,1)S(1)}, u32[]{:S(2)}, u32[]{:S(2)}) %collective-permute-start.17) | collective-permute-done | bytes 262176 | tf_op jit(solution)/shard_map/ppermute | solution.py:36
  73.0 1.5 %collective-permute-start.18 = (bf16[4,128,256]{2,1,0:T(8,128)(2,1)S(1)}, bf16[4,128,256]{2,1,0:T(8,128)(2,1)S(1)}, u32[]{:S(2)}, u32[]{:S(2)}) collective-permute-start(bf16[4,128,256]{2,1,0:T(8,128)(2,1)S(1)} %add_convert_fusion.3), channel_id=1, source_target_pairs={{0,8},{1,121},{8,16},{9,1},{16,24},{17,9},{24,32},{25,17},{32,40},... | collective-permute-start | bytes 786440 | tf_op jit(solution)/shard_map/ppermute | solution.py:36
  74.5 1.2 %collective-permute-done.8 = bf16[4,128,256]{2,1,0:T(8,128)(2,1)S(1)} collective-permute-done((bf16[4,128,256]{2,1,0:T(8,128)(2,1)S(1)}, bf16[4,128,256]{2,1,0:T(8,128)(2,1)S(1)}, u32[]{:S(2)}, u32[]{:S(2)}) %collective-permute-start.8) | collective-permute-done | bytes 262176 | tf_op jit(solution)/shard_map/ppermute | solution.py:36
  75.8 1.5 %collective-permute-start.12 = (bf16[4,128,256]{2,1,0:T(8,128)(2,1)S(1)}, bf16[4,128,256]{2,1,0:T(8,128)(2,1)S(1)}, u32[]{:S(2)}, u32[]{:S(2)}) collective-permute-start(bf16[4,128,256]{2,1,0:T(8,128)(2,1)S(1)} %add_convert_fusion.7), channel_id=1, source_target_pairs={{0,8},{1,121},{8,16},{9,1},{16,24},{17,9},{24,32},{25,17},{32,40},... | collective-permute-start | bytes 786440 | tf_op jit(solution)/shard_map/ppermute | solution.py:36
  77.4 1.2 %work.21 = (f32[4,128,256]{2,1,0:T(8,128)S(1)}, f32[4,128,256]{2,1,0:T(8,128)S(1)}) custom-call(s32[1,64]{1,0:T(1,128)S(1)} %copy-done, bf16[16,128,128]{2,1,0:T(8,128)(2,1)S(1)} %get-tuple-element.22.refs_1_, bf16[16,32,128]{2,1,0:T(8,128)(2,1)S(1)} %get-tuple-element.23.refs_2_, bf16[16,4,192,128]{3,2,1,0:T(8,128)(2,1)S(1)} %get-tuple-element.24.refs_3_.x_ref, ...), custom_call_target="tpu_custom_call" | custom-call | flops 125829120 | bytes 491520 | tf_op jit(solution)/shard_map/work/pallas_call | solution.py:249
  78.6 2.5 %collective-permute-start.19 = (bf16[4,128,256]{2,1,0:T(8,128)(2,1)S(1)}, bf16[4,128,256]{2,1,0:T(8,128)(2,1)S(1)}, u32[]{:S(2)}, u32[]{:S(2)}) collective-permute-start(bf16[4,128,256]{2,1,0:T(8,128)(2,1)S(1)} %add_convert_fusion.2), channel_id=1, source_target_pairs={{0,8},{1,121},{8,16},{9,1},{16,24},{17,9},{24,32},{25,17},{32,40},... | collective-permute-start | bytes 786440 | tf_op jit(solution)/shard_map/ppermute | solution.py:36
  81.2 0.3 collective-permute-done.12
  81.5 2.5 %collective-permute-start.14 = (bf16[4,128,256]{2,1,0:T(8,128)(2,1)S(1)}, bf16[4,128,256]{2,1,0:T(8,128)(2,1)S(1)}, u32[]{:S(2)}, u32[]{:S(2)}) collective-permute-start(bf16[4,128,256]{2,1,0:T(8,128)(2,1)S(1)} %add_convert_fusion.6), channel_id=1, source_target_pairs={{0,8},{1,121},{8,16},{9,1},{16,24},{17,9},{24,32},{25,17},{32,40},... | collective-permute-start | bytes 786440 | tf_op jit(solution)/shard_map/ppermute | solution.py:36
  84.0 1.2 %work.22 = (f32[4,128,256]{2,1,0:T(8,128)S(1)}, f32[4,128,256]{2,1,0:T(8,128)S(1)}) custom-call(s32[1,64]{1,0:T(1,128)S(1)} %copy-done, bf16[16,128,128]{2,1,0:T(8,128)(2,1)S(1)} %get-tuple-element.22.refs_1_, bf16[16,32,128]{2,1,0:T(8,128)(2,1)S(1)} %get-tuple-element.23.refs_2_, bf16[16,4,192,128]{3,2,1,0:T(8,128)(2,1)S(1)} %get-tuple-element.24.refs_3_.x_ref, ...), custom_call_target="tpu_custom_call" | custom-call | flops 125829120 | bytes 491520 | tf_op jit(solution)/shard_map/work/pallas_call | solution.py:249
  85.3 2.5 %collective-permute-start.20 = (bf16[4,128,256]{2,1,0:T(8,128)(2,1)S(1)}, bf16[4,128,256]{2,1,0:T(8,128)(2,1)S(1)}, u32[]{:S(2)}, u32[]{:S(2)}) collective-permute-start(bf16[4,128,256]{2,1,0:T(8,128)(2,1)S(1)} %add_convert_fusion.1), channel_id=1, source_target_pairs={{0,8},{1,121},{8,16},{9,1},{16,24},{17,9},{24,32},{25,17},{32,40},... | collective-permute-start | bytes 786440 | tf_op jit(solution)/shard_map/ppermute | solution.py:36
  87.8 1.2 %work.23 = (f32[4,128,256]{2,1,0:T(8,128)S(1)}, f32[4,128,256]{2,1,0:T(8,128)S(1)}) custom-call(s32[1,64]{1,0:T(1,128)S(1)} %copy-done, bf16[16,128,128]{2,1,0:T(8,128)(2,1)S(1)} %get-tuple-element.22.refs_1_, bf16[16,32,128]{2,1,0:T(8,128)(2,1)S(1)} %get-tuple-element.23.refs_2_, bf16[16,4,192,128]{3,2,1,0:T(8,128)(2,1)S(1)} %get-tuple-element.24.refs_3_.x_ref, ...), custom_call_target="tpu_custom_call" | custom-call | flops 125829120 | bytes 491520 | tf_op jit(solution)/shard_map/work/pallas_call | solution.py:249
  89.1 1.5 %collective-permute-start.15 = (bf16[4,128,256]{2,1,0:T(8,128)(2,1)S(1)}, bf16[4,128,256]{2,1,0:T(8,128)(2,1)S(1)}, u32[]{:S(2)}, u32[]{:S(2)}) collective-permute-start(bf16[4,128,256]{2,1,0:T(8,128)(2,1)S(1)} %add_convert_fusion.5), channel_id=1, source_target_pairs={{0,8},{1,121},{8,16},{9,1},{16,24},{17,9},{24,32},{25,17},{32,40},... | collective-permute-start | bytes 786440 | tf_op jit(solution)/shard_map/ppermute | solution.py:36
  90.6 0.5 collective-permute-done.20
  91.1 3.2 %collective-permute-start.21 = (bf16[4,128,256]{2,1,0:T(8,128)(2,1)S(1)}, bf16[4,128,256]{2,1,0:T(8,128)(2,1)S(1)}, u32[]{:S(2)}, u32[]{:S(2)}) collective-permute-start(bf16[4,128,256]{2,1,0:T(8,128)(2,1)S(1)} %add_convert_fusion), channel_id=1, source_target_pairs={{0,8},{1,121},{8,16},{9,1},{16,24},{17,9},{24,32},{25,17},{32,40},... | collective-permute-start | bytes 786440 | tf_op jit(solution)/shard_map/ppermute | solution.py:36
  94.5 2.7 %collective-permute-start.16 = (bf16[4,128,256]{2,1,0:T(8,128)(2,1)S(1)}, bf16[4,128,256]{2,1,0:T(8,128)(2,1)S(1)}, u32[]{:S(2)}, u32[]{:S(2)}) collective-permute-start(bf16[4,128,256]{2,1,0:T(8,128)(2,1)S(1)} %add_convert_fusion.4), channel_id=1, source_target_pairs={{0,8},{1,121},{8,16},{9,1},{16,24},{17,9},{24,32},{25,17},{32,40},... | collective-permute-start | bytes 786440 | tf_op jit(solution)/shard_map/ppermute | solution.py:36
  97.2 0.5 collective-permute-done.21
  97.7 8.5 %collective-permute-start.22 = (bf16[4,128,256]{2,1,0:T(8,128)(2,1)S(1)}, bf16[4,128,256]{2,1,0:T(8,128)(2,1)S(1)}, u32[]{:S(2)}, u32[]{:S(2)}) collective-permute-start(bf16[4,128,256]{2,1,0:T(8,128)(2,1)S(1)} %collective-permute-done.21), channel_id=1, source_target_pairs={{0,1},{1,0},{2,3},{3,2},{4,5},{5,4},{6,7},{7,6},{8,9},{9,8},{10,11... | collective-permute-start | bytes 786440 | tf_op jit(solution)/shard_map/ppermute | solution.py:41
  106.2 1.0 work.25.own_ref
  107.3 0.9 finish.1
  (37 shorter events, 2.1 us)
Async XLA Ops:
  0.0 23.7 %copy-start.1 = (bf16[16,16]{1,0:T(8,128)(2,1)S(1)}, bf16[16,16]{1,0:T(8,128)(2,1)}, u32[]{:S(2)}) copy-start(bf16[16,16]{1,0:T(8,128)(2,1)} %table_ref.1) | copy-start | bytes 1540
  0.0 32.6 %collective-permute-start.5 = (bf16[16,4,2,96,128]{4,3,2,1,0:T(8,128)(2,1)}, bf16[16,4,2,96,128]{4,3,2,1,0:T(8,128)(2,1)S(1)}, u32[]{:S(2)}, u32[]{:S(2)}) collective-permute-start(bf16[16,4,2,96,128]{4,3,2,1,0:T(8,128)(2,1)} %bitcast.4), channel_id=1, source_target_pairs={{0,1},{1,0},{2,3},{3,2},{4,5},{5,4},{6,7},{7,6},{8,9},{9,8},{10,11... | collective-permute-start | bytes 9437192 | tf_op jit(solution)/shard_map/ppermute | solution.py:41
  21.7 5.8 %collective-permute-start = (bf16[3,192,128]{2,1,0:T(8,128)(2,1)S(1)}, bf16[3,192,128]{2,1,0:T(8,128)(2,1)S(1)}, u32[]{:S(2)}, u32[]{:S(2)}) collective-permute-start(bf16[3,192,128]{2,1,0:T(8,128)(2,1)S(1)} %pack.2), channel_id=1, source_target_pairs={{0,2},{2,4},{4,6},{1,3},{3,5},{5,7},{8,10},{10,12},{12,14},{9,11},... | collective-permute-start | bytes 442376 | tf_op jit(solution)/shard_map/ppermute | solution.py:26
  23.7 3.9 %copy-start = (s32[1,64]{1,0:T(1,128)S(1)}, s32[1,64]{1,0:T(1,128)}, u32[]{:S(2)}) copy-start(s32[1,64]{1,0:T(1,128)} %refs_0_.21) | copy-start | bytes 772
  28.8 5.7 %collective-permute-start.4 = (bf16[1,4,128,256]{3,2,1,0:T(8,128)(2,1)S(1)}, bf16[1,4,128,256]{3,2,1,0:T(8,128)(2,1)S(1)}, u32[]{:S(2)}, u32[]{:S(2)}) collective-permute-start(bf16[1,4,128,256]{3,2,1,0:T(8,128)(2,1)S(1)} %get-tuple-element.28), channel_id=1, source_target_pairs={{0,1},{1,0},{2,3},{3,2},{4,5},{5,4},{6,7},{7,6},{8,9},{9,8},{10,11... | collective-permute-start | bytes 786440 | tf_op jit(solution)/shard_map/ppermute | solution.py:41
  29.0 7.8 %collective-permute-start.3 = (bf16[4,192,128]{2,1,0:T(8,128)(2,1)S(1)}, bf16[4,192,128]{2,1,0:T(8,128)(2,1)S(1)}, u32[]{:S(2)}, u32[]{:S(2)}) collective-permute-start(bf16[4,192,128]{2,1,0:T(8,128)(2,1)S(1)} %get-tuple-element.27), channel_id=1, source_target_pairs={{0,2},{2,4},{4,6},{1,3},{3,5},{5,7},{8,10},{10,12},{12,14},{9,11},... | collective-permute-start | bytes 589832 | tf_op jit(solution)/shard_map/ppermute | solution.py:26
  38.1 12.7 %collective-permute-start.6 = (bf16[2,4,128,256]{3,2,1,0:T(8,128)(2,1)S(1)}, bf16[2,4,128,256]{3,2,1,0:T(8,128)(2,1)S(1)}, u32[]{:S(2)}, u32[]{:S(2)}) collective-permute-start(bf16[2,4,128,256]{3,2,1,0:T(8,128)(2,1)S(1)} %work.16), channel_id=1, source_target_pairs={{0,1},{1,0},{2,3},{3,2},{4,5},{5,4},{6,7},{7,6},{8,9},{9,8},{10,11... | collective-permute-start | bytes 1572872 | tf_op jit(solution)/shard_map/ppermute | solution.py:41
  39.1 10.9 %collective-permute-start.1 = (bf16[4,128,256]{2,1,0:T(8,128)(2,1)S(1)}, bf16[4,128,256]{2,1,0:T(8,128)(2,1)S(1)}, u32[]{:S(2)}, u32[]{:S(2)}) collective-permute-start(bf16[4,128,256]{2,1,0:T(8,128)(2,1)S(1)} %get-tuple-element.26), channel_id=1, source_target_pairs={{0,8},{1,121},{8,16},{9,1},{16,24},{17,9},{24,32},{25,17},{32,40},... | collective-permute-start | bytes 786440 | tf_op jit(solution)/shard_map/ppermute | solution.py:36
  44.6 19.4 %collective-permute-start.9 = (bf16[9,192,128]{2,1,0:T(8,128)(2,1)S(1)}, bf16[9,192,128]{2,1,0:T(8,128)(2,1)S(1)}, u32[]{:S(2)}, u32[]{:S(2)}) collective-permute-start(bf16[9,192,128]{2,1,0:T(8,128)(2,1)S(1)} %pack.3), channel_id=1, source_target_pairs={{0,2},{2,4},{4,6},{1,3},{3,5},{5,7},{8,10},{10,12},{12,14},{9,11},... | collective-permute-start | bytes 1327112 | tf_op jit(solution)/shard_map/ppermute | solution.py:26
  49.8 5.6 %collective-permute-start.10 = (bf16[4,128,256]{2,1,0:T(8,128)(2,1)S(1)}, bf16[4,128,256]{2,1,0:T(8,128)(2,1)S(1)}, u32[]{:S(2)}, u32[]{:S(2)}) collective-permute-start(bf16[4,128,256]{2,1,0:T(8,128)(2,1)S(1)} %work.15.refs_0_), channel_id=1, source_target_pairs={{0,8},{1,121},{8,16},{9,1},{16,24},{17,9},{24,32},{25,17},{32,40},... | collective-permute-start | bytes 786440 | tf_op jit(solution)/shard_map/ppermute | solution.py:36
  50.0 7.9 %collective-permute-start.2 = (bf16[4,128,256]{2,1,0:T(8,128)(2,1)S(1)}, bf16[4,128,256]{2,1,0:T(8,128)(2,1)S(1)}, u32[]{:S(2)}, u32[]{:S(2)}) collective-permute-start(bf16[4,128,256]{2,1,0:T(8,128)(2,1)S(1)} %add_convert_fusion.12), channel_id=1, source_target_pairs={{0,8},{1,121},{8,16},{9,1},{16,24},{17,9},{24,32},{25,17},{32,40},... | collective-permute-start | bytes 786440 | tf_op jit(solution)/shard_map/ppermute | solution.py:36
  55.5 5.6 %collective-permute-start.11 = (bf16[4,128,256]{2,1,0:T(8,128)(2,1)S(1)}, bf16[4,128,256]{2,1,0:T(8,128)(2,1)S(1)}, u32[]{:S(2)}, u32[]{:S(2)}) collective-permute-start(bf16[4,128,256]{2,1,0:T(8,128)(2,1)S(1)} %add_convert_fusion.9), channel_id=1, source_target_pairs={{0,8},{1,121},{8,16},{9,1},{16,24},{17,9},{24,32},{25,17},{32,40},... | collective-permute-start | bytes 786440 | tf_op jit(solution)/shard_map/ppermute | solution.py:36
  58.0 5.9 %collective-permute-start.7 = (bf16[4,128,256]{2,1,0:T(8,128)(2,1)S(1)}, bf16[4,128,256]{2,1,0:T(8,128)(2,1)S(1)}, u32[]{:S(2)}, u32[]{:S(2)}) collective-permute-start(bf16[4,128,256]{2,1,0:T(8,128)(2,1)S(1)} %add_convert_fusion.11), channel_id=1, source_target_pairs={{0,8},{1,121},{8,16},{9,1},{16,24},{17,9},{24,32},{25,17},{32,40},... | collective-permute-start | bytes 786440 | tf_op jit(solution)/shard_map/ppermute | solution.py:36
  65.6 5.0 %collective-permute-start.13 = (bf16[4,4,128,256]{3,2,1,0:T(8,128)(2,1)S(1)}, bf16[4,4,128,256]{3,2,1,0:T(8,128)(2,1)S(1)}, u32[]{:S(2)}, u32[]{:S(2)}) collective-permute-start(bf16[4,4,128,256]{3,2,1,0:T(8,128)(2,1)S(1)} %work.20), channel_id=1, source_target_pairs={{0,1},{1,0},{2,3},{3,2},{4,5},{5,4},{6,7},{7,6},{8,9},{9,8},{10,11... | collective-permute-start | bytes 3145736 | tf_op jit(solution)/shard_map/ppermute | solution.py:41
  67.4 5.5 %collective-permute-start.17 = (bf16[4,128,256]{2,1,0:T(8,128)(2,1)S(1)}, bf16[4,128,256]{2,1,0:T(8,128)(2,1)S(1)}, u32[]{:S(2)}, u32[]{:S(2)}) collective-permute-start(bf16[4,128,256]{2,1,0:T(8,128)(2,1)S(1)} %add_convert_fusion.8.refs_1_), channel_id=1, source_target_pairs={{0,8},{1,121},{8,16},{9,1},{16,24},{17,9},{24,32},{25,17},{32,40},... | collective-permute-start | bytes 786440 | tf_op jit(solution)/shard_map/ppermute | solution.py:36
  67.9 7.8 %collective-permute-start.8 = (bf16[4,128,256]{2,1,0:T(8,128)(2,1)S(1)}, bf16[4,128,256]{2,1,0:T(8,128)(2,1)S(1)}, u32[]{:S(2)}, u32[]{:S(2)}) collective-permute-start(bf16[4,128,256]{2,1,0:T(8,128)(2,1)S(1)} %add_convert_fusion.10.refs_0_), channel_id=1, source_target_pairs={{0,8},{1,121},{8,16},{9,1},{16,24},{17,9},{24,32},{25,17},{32,40},... | collective-permute-start | bytes 786440 | tf_op jit(solution)/shard_map/ppermute | solution.py:36
  73.0 5.6 %collective-permute-start.18 = (bf16[4,128,256]{2,1,0:T(8,128)(2,1)S(1)}, bf16[4,128,256]{2,1,0:T(8,128)(2,1)S(1)}, u32[]{:S(2)}, u32[]{:S(2)}) collective-permute-start(bf16[4,128,256]{2,1,0:T(8,128)(2,1)S(1)} %add_convert_fusion.3), channel_id=1, source_target_pairs={{0,8},{1,121},{8,16},{9,1},{16,24},{17,9},{24,32},{25,17},{32,40},... | collective-permute-start | bytes 786440 | tf_op jit(solution)/shard_map/ppermute | solution.py:36
  75.8 5.6 %collective-permute-start.12 = (bf16[4,128,256]{2,1,0:T(8,128)(2,1)S(1)}, bf16[4,128,256]{2,1,0:T(8,128)(2,1)S(1)}, u32[]{:S(2)}, u32[]{:S(2)}) collective-permute-start(bf16[4,128,256]{2,1,0:T(8,128)(2,1)S(1)} %add_convert_fusion.7), channel_id=1, source_target_pairs={{0,8},{1,121},{8,16},{9,1},{16,24},{17,9},{24,32},{25,17},{32,40},... | collective-permute-start | bytes 786440 | tf_op jit(solution)/shard_map/ppermute | solution.py:36
  78.6 6.5 %collective-permute-start.19 = (bf16[4,128,256]{2,1,0:T(8,128)(2,1)S(1)}, bf16[4,128,256]{2,1,0:T(8,128)(2,1)S(1)}, u32[]{:S(2)}, u32[]{:S(2)}) collective-permute-start(bf16[4,128,256]{2,1,0:T(8,128)(2,1)S(1)} %add_convert_fusion.2), channel_id=1, source_target_pairs={{0,8},{1,121},{8,16},{9,1},{16,24},{17,9},{24,32},{25,17},{32,40},... | collective-permute-start | bytes 786440 | tf_op jit(solution)/shard_map/ppermute | solution.py:36
  81.5 7.5 %collective-permute-start.14 = (bf16[4,128,256]{2,1,0:T(8,128)(2,1)S(1)}, bf16[4,128,256]{2,1,0:T(8,128)(2,1)S(1)}, u32[]{:S(2)}, u32[]{:S(2)}) collective-permute-start(bf16[4,128,256]{2,1,0:T(8,128)(2,1)S(1)} %add_convert_fusion.6), channel_id=1, source_target_pairs={{0,8},{1,121},{8,16},{9,1},{16,24},{17,9},{24,32},{25,17},{32,40},... | collective-permute-start | bytes 786440 | tf_op jit(solution)/shard_map/ppermute | solution.py:36
  85.3 5.8 %collective-permute-start.20 = (bf16[4,128,256]{2,1,0:T(8,128)(2,1)S(1)}, bf16[4,128,256]{2,1,0:T(8,128)(2,1)S(1)}, u32[]{:S(2)}, u32[]{:S(2)}) collective-permute-start(bf16[4,128,256]{2,1,0:T(8,128)(2,1)S(1)} %add_convert_fusion.1), channel_id=1, source_target_pairs={{0,8},{1,121},{8,16},{9,1},{16,24},{17,9},{24,32},{25,17},{32,40},... | collective-permute-start | bytes 786440 | tf_op jit(solution)/shard_map/ppermute | solution.py:36
  89.1 5.3 %collective-permute-start.15 = (bf16[4,128,256]{2,1,0:T(8,128)(2,1)S(1)}, bf16[4,128,256]{2,1,0:T(8,128)(2,1)S(1)}, u32[]{:S(2)}, u32[]{:S(2)}) collective-permute-start(bf16[4,128,256]{2,1,0:T(8,128)(2,1)S(1)} %add_convert_fusion.5), channel_id=1, source_target_pairs={{0,8},{1,121},{8,16},{9,1},{16,24},{17,9},{24,32},{25,17},{32,40},... | collective-permute-start | bytes 786440 | tf_op jit(solution)/shard_map/ppermute | solution.py:36
  91.1 6.5 %collective-permute-start.21 = (bf16[4,128,256]{2,1,0:T(8,128)(2,1)S(1)}, bf16[4,128,256]{2,1,0:T(8,128)(2,1)S(1)}, u32[]{:S(2)}, u32[]{:S(2)}) collective-permute-start(bf16[4,128,256]{2,1,0:T(8,128)(2,1)S(1)} %add_convert_fusion), channel_id=1, source_target_pairs={{0,8},{1,121},{8,16},{9,1},{16,24},{17,9},{24,32},{25,17},{32,40},... | collective-permute-start | bytes 786440 | tf_op jit(solution)/shard_map/ppermute | solution.py:36
  94.5 12.8 %collective-permute-start.16 = (bf16[4,128,256]{2,1,0:T(8,128)(2,1)S(1)}, bf16[4,128,256]{2,1,0:T(8,128)(2,1)S(1)}, u32[]{:S(2)}, u32[]{:S(2)}) collective-permute-start(bf16[4,128,256]{2,1,0:T(8,128)(2,1)S(1)} %add_convert_fusion.4), channel_id=1, source_target_pairs={{0,8},{1,121},{8,16},{9,1},{16,24},{17,9},{24,32},{25,17},{32,40},... | collective-permute-start | bytes 786440 | tf_op jit(solution)/shard_map/ppermute | solution.py:36
  97.7 9.6 %collective-permute-start.22 = (bf16[4,128,256]{2,1,0:T(8,128)(2,1)S(1)}, bf16[4,128,256]{2,1,0:T(8,128)(2,1)S(1)}, u32[]{:S(2)}, u32[]{:S(2)}) collective-permute-start(bf16[4,128,256]{2,1,0:T(8,128)(2,1)S(1)} %collective-permute-done.21), channel_id=1, source_target_pairs={{0,1},{1,0},{2,3},{3,2},{4,5},{5,4},{6,7},{7,6},{8,9},{9,8},{10,11... | collective-permute-start | bytes 786440 | tf_op jit(solution)/shard_map/ppermute | solution.py:41

commit v3 on v2

--- a/solution.py
+++ b/solution.py
@@ -96,16 +96,12 @@
 
 
 def bank_kernel(
-    offsets, count, delay_ref, table_ref, x_ref, w_ref,
-    main_ref, edge_ref, near_x_ref, near_w_ref, packed_ref, sem,
+    offsets, count, delay_ref, table_ref, x_ref,
+    main_ref, edge_ref, near_x_ref, packed_ref, sem,
 ):
     sets, length, _ = main_ref.shape
-    copies = [
-        pltpu.make_async_copy(x_ref, near_x_ref, sem.at[0]),
-        pltpu.make_async_copy(w_ref, near_w_ref, sem.at[1]),
-    ]
-    for copy in copies:
-        copy.start()
+    copy = pltpu.make_async_copy(x_ref, near_x_ref, sem)
+    copy.start()
     tap = lax.broadcasted_iota(jnp.int32, (TAPS, length), 0)
     lane = lax.broadcasted_iota(jnp.int32, (TAPS, length), 1)
     back = delay_ref[0] + lane + tap
@@ -123,12 +119,11 @@
         for q in range(1, length // HALO):
             spread = spread + pltpu.roll(edge, q * HALO, 1)
         edge_ref[m] = spread.astype(edge_ref.dtype)
-    for copy in copies:
-        copy.wait()
+    copy.wait()
     pack_near_kernel(offsets, count, near_x_ref, packed_ref)
 
 
-def bank(table, delays, x, w, offsets):
+def bank(table, delays, x, offsets):
     _, rows, height, length = x.shape
     sets = table.shape[0]
     return pl.pallas_call(
@@ -137,40 +132,30 @@
             pltpu.VMEM((sets, length, length), jnp.bfloat16),
             pltpu.VMEM((sets, HALO, length), jnp.bfloat16),
             pltpu.VMEM(x.shape, x.dtype),
-            pltpu.VMEM(w.shape, w.dtype),
             pltpu.VMEM((len(offsets), height, rows * HALO), x.dtype),
         ),
-        in_specs=[SMEM, VMEM, ANY, ANY],
-        out_specs=(VMEM,) * 5,
-        scratch_shapes=[pltpu.SemaphoreType.DMA((2,))],
+        in_specs=[SMEM, VMEM, ANY],
+        out_specs=(VMEM,) * 4,
+        scratch_shapes=[pltpu.SemaphoreType.DMA],
         compiler_params=PARAMS,
         name="bank",
-    )(near(delays, pltpu.SMEM), table, near(x, pltpu.HBM), near(w, pltpu.HBM))
-
-
-def settle_kernel(offsets, count, value_ref, *refs):
+    )(near(delays, pltpu.SMEM), table, near(x, pltpu.HBM))
+
+
+def settle_kernel(value_ref, *refs):
     out_ref, sem = refs[-2:]
-    if offsets:
-        copies = [
-            pltpu.make_async_copy(value_ref.at[chunk_index(o, count)], out_ref.at[i], sem.at[i])
-            for i, o in enumerate(offsets)
-        ]
-    else:
-        copies = [pltpu.make_async_copy(value_ref, out_ref, sem.at[0])]
-    for copy in copies:
-        copy.start()
-    for copy in copies:
-        copy.wait()
-
-
-def settle(value, offsets=(), after=()):
-    shape = (len(offsets),) + value.shape[1:] if offsets else value.shape
-    return pl.pallas_call(
-        functools.partial(settle_kernel, offsets, value.shape[0]),
-        out_shape=pltpu.VMEM(shape, value.dtype),
+    copy = pltpu.make_async_copy(value_ref, out_ref, sem)
+    copy.start()
+    copy.wait()
+
+
+def settle(value, after=()):
+    return pl.pallas_call(
+        settle_kernel,
+        out_shape=pltpu.VMEM(value.shape, value.dtype),
         in_specs=[ANY] + [VMEM] * len(after),
         out_specs=VMEM,
-        scratch_shapes=[pltpu.SemaphoreType.DMA((max(1, len(offsets)),))],
+        scratch_shapes=[pltpu.SemaphoreType.DMA],
         compiler_params=PARAMS,
         name="settle",
     )(value, *[near(one) for one in after])
@@ -179,9 +164,18 @@
 FILTER, STEER, BOTH = range(3)
 
 
-def work_kernel(jobs, count, rows, names, *refs):
+def work_kernel(jobs, count, rows, names, fetch, *refs):
     held = dict(zip(names, refs))
     outs = refs[len(names) :]
+    copies = []
+    if fetch:
+        *outs, near_ref, sem = outs
+        copies = [
+            pltpu.make_async_copy(held["raw"].at[chunk_index(o, count)], near_ref.at[i], sem.at[i])
+            for i, o in enumerate(fetch)
+        ]
+        for copy in copies:
+            copy.start()
     nt = (((1,), (1,)), ((), ()))
     filters = 0
     for i, (what, offset, place) in enumerate(jobs):
@@ -232,29 +226,39 @@
                 axis=0,
             )
             out[q] = jnp.dot(delayed, steer, preferred_element_type=jnp.float32).astype(out.dtype)
-
-
-def work(jobs, dtypes, rows, count, length, height, width, **arrays):
+    for copy in copies:
+        copy.wait()
+
+
+def work(jobs, dtypes, rows, count, length, height, width, fetch=(), **arrays):
     names = tuple(arrays)
     shapes = [pltpu.VMEM((rows, length, width), dtype) for dtype in dtypes]
     filters = sum(what == FILTER for what, _, _ in jobs)
     if filters:
         lanes = (height + 127) // 128 * 128
         shapes.append(pltpu.VMEM((filters, rows, length, lanes), jnp.bfloat16))
+    if fetch:
+        shapes.append(pltpu.VMEM((len(fetch),) + arrays["raw"].shape[1:], arrays["raw"].dtype))
     flops = 0
     for what, _, _ in jobs:
         flops += 2 * rows * length * height * (
             (0 if what == STEER else length) + (0 if what == FILTER else width)
         )
     return pl.pallas_call(
-        functools.partial(work_kernel, jobs, count, rows, names),
+        functools.partial(work_kernel, jobs, count, rows, names, fetch),
         out_shape=tuple(shapes),
-        in_specs=[SMEM if name == "sets" else VMEM for name in names],
+        in_specs=[{"sets": SMEM, "raw": ANY}.get(name, VMEM) for name in names],
         out_specs=(VMEM,) * len(shapes),
+        scratch_shapes=[pltpu.SemaphoreType.DMA((len(fetch),))] if fetch else [],
         cost_estimate=pl.CostEstimate(flops=flops, bytes_accessed=flops // 256, transcendentals=0),
         compiler_params=PARAMS,
         name="work",
-    )(*[near(value, pltpu.SMEM if name == "sets" else pltpu.VMEM) for name, value in arrays.items()])
+    )(
+        *[
+            value if name == "raw" else near(value, pltpu.SMEM if name == "sets" else pltpu.VMEM)
+            for name, value in arrays.items()
+        ]
+    )
 
 
 def finish_kernel(right_ref, left_ref, own_ref, out_ref):
@@ -299,15 +303,15 @@
 
     def use_piece(i, got, after=()):
         if after:
-            got = settle(got, (), after)
+            got = settle(got, after)
         halos.update({o: (got, place) for place, o in enumerate(pieces[i])})
 
     packed = pack(x, pieces[0], False)
     use_piece(0, from_earlier(packed))
-    main, edge, near_x, near_w, packed = bank(tap_table, delays, x, w, pieces[1])
+    main, edge, near_x, packed = bank(tap_table, delays, x, pieces[1])
     other_w = across_cores(w)
     second = packed
-    common = {"sets": tap_sets, "main": main, "edge": edge, "x": near_x, "w": near_w}
+    common = {"sets": tap_sets, "main": main, "edge": edge, "x": near_x, "w": w}
 
     def filtered(offsets):
         jobs = tuple((FILTER, o, halos[o][1]) for o in offsets)
@@ -320,9 +324,11 @@
     )
     a_got = onward(a)
     given = {1: (across_cores(handed), 0)}
-    other_w = settle(other_w, tuple(half - s for s in range(1, half)))
     halo, place = halos[half - 1]
-    (own,) = work(((BOTH, half - 1, place),), [wide], *sizes, **common, halo=halo)
+    own, other_w = work(
+        ((BOTH, half - 1, place),), [wide], *sizes, **common, halo=halo,
+        fetch=tuple(half - s for s in range(1, half)), raw=other_w,
+    )
     second = from_earlier(second)
     packed = pack(near_x, pieces[2], True)
     (b,) = work(
@@ -340,7 +346,7 @@
         a = (a_got.astype(wide) + own).astype(thin)
         a_got = onward(a)
         if s == 1:
-            use_piece(1, second, (b,))
+            use_piece(1, second, (a, b))
             send_filtered(2, 4)
             third = from_earlier(packed)
         elif s == 3:

time: 109 us -> 106 us (0.972)
  waiting for transfers between devices: 14.7 us -> 11.7 us
    ppermute x3, waiting for transfers between devices: 2.06 us -> 0.01 us  [from_earlier(): lax.ppermute(value, 'tm', [(i, i + 1) for i in range(lax.axis_size('tm')...]
    pallas_call x18 -> x17, Pallas kernels: 15.7 us -> 15.8 us  [the longest x13 15.1 us: work(): pl.pallas_call(functools.partial(work_kernel, jobs, count, rows, names, f...]
  transfers between devices with their start and end apart: 23 -> 23, of which waited for: 11 -> 9; matrix products, arithmetic and copies ran while one was open for 1% -> 1% of each run, Pallas kernels for 17% -> 17%
where the time goes in v3:
time: 106 us; the launch traced here: 105 us
  starting transfers between devices  70.3 us (66%)
  Pallas kernels  21.3 us (20%)
  waiting for transfers between devices  11.7 us (11%)
    ppermute x5, starting transfers between devices, across_cores(): lax.ppermute(value, 'chan', [(i, (i + 1) % cores) for i in range(cores)])  32.1 us
    ppermute x15, starting transfers between devices, onward(): return lax.ppermute(value, ('station', 'chan'), pairs)  28.6 us
    pallas_call x13, Pallas kernels, work(): pl.pallas_call(functools.partial(work_kernel, jobs, count, rows, names, f...  15.1 us
    ppermute x15, waiting for transfers between devices, onward(): return lax.ppermute(value, ('station', 'chan'), pairs)  11.6 us
    ppermute x3, starting transfers between devices, from_earlier(): lax.ppermute(value, 'tm', [(i, i + 1) for i in range(lax.axis_size('tm')...  9.61 us
    pallas_call x1, Pallas kernels, bank(): pl.pallas_call(functools.partial(bank_kernel, offsets, x.shape[0]), out_s...  2.86 us
  transfers between devices with their start and end apart: 23, of which 9 were waited for; matrix products, arithmetic and copies ran while one was open for 1% of the time, Pallas kernels for 17%

profile of v3, /device:TPU:33, one launch (start us, length us, event | category | flops | bytes accessed | tf_op | source)
XLA Modules:
  0.0 105.2 jit_solution(5096792521583396014)
XLA Ops:
  0.0 20.4 %collective-permute-start.2 = (bf16[16,4,2,96,128]{4,3,2,1,0:T(8,128)(2,1)}, bf16[16,4,2,96,128]{4,3,2,1,0:T(8,128)(2,1)S(1)}, u32[]{:S(2)}, u32[]{:S(2)}) collective-permute-start(bf16[16,4,2,96,128]{4,3,2,1,0:T(8,128)(2,1)} %bitcast.2), channel_id=1, source_target_pairs={{0,1},{1,0},{2,3},{3,2},{4,5},{5,4},{6,7},{7,6},{8,9},{9,8},{10,11... | collective-permute-start | bytes 9437192 | tf_op jit(solution)/shard_map/ppermute | solution.py:41
  20.4 1.4 %pack.2 = bf16[3,192,128]{2,1,0:T(8,128)(2,1)S(1)} custom-call(bf16[16,4,192,128]{3,2,1,0:T(8,128)(2,1)} %bitcast.14), custom_call_target="tpu_custom_call" | custom-call | tf_op jit(solution)/shard_map/pack/pallas_call | solution.py:84
  21.9 1.3 %collective-permute-start = (bf16[3,192,128]{2,1,0:T(8,128)(2,1)S(1)}, bf16[3,192,128]{2,1,0:T(8,128)(2,1)S(1)}, u32[]{:S(2)}, u32[]{:S(2)}) collective-permute-start(bf16[3,192,128]{2,1,0:T(8,128)(2,1)S(1)} %pack.2), channel_id=1, source_target_pairs={{0,2},{2,4},{4,6},{1,3},{3,5},{5,7},{8,10},{10,12},{12,14},{9,11},... | collective-permute-start | bytes 442376 | tf_op jit(solution)/shard_map/ppermute | solution.py:26
  23.8 2.9 %bank.1 = (bf16[16,128,128]{2,1,0:T(8,128)(2,1)S(1)}, bf16[16,32,128]{2,1,0:T(8,128)(2,1)S(1)}, bf16[16,4,192,128]{3,2,1,0:T(8,128)(2,1)S(1)}, bf16[4,192,128]{2,1,0:T(8,128)(2,1)S(1)}) custom-call(s32[1]{0:T(128)S(6)} %copy.6.delay_ref, bf16[16,16]{1,0:T(8,128)(2,1)S(1)} %copy-done.2, bf16[16,4,192,128]{3,2,1,0:T(8,128)(2,1)} %bitcast.15), custom_call_target="tpu_custom_call" | custom-call | tf_op jit(solution)/shard_map/bank/pallas_call | solution.py:129
  26.7 1.3 %work.13 = (bf16[4,128,256]{2,1,0:T(8,128)(2,1)S(1)}, bf16[1,4,128,256]{3,2,1,0:T(8,128)(2,1)S(1)}) custom-call(s32[1,64]{1,0:T(1,128)S(1)} %copy-done.1, bf16[16,128,128]{2,1,0:T(8,128)(2,1)S(1)} %get-tuple-element.23.refs_1_, bf16[16,32,128]{2,1,0:T(8,128)(2,1)S(1)} %get-tuple-element.24.refs_2_, ...), custom_call_target="tpu_custom_call" | custom-call | flops 100663296 | bytes 393216 | tf_op jit(solution)/shard_map/work/pallas_call | solution.py:247
  28.0 0.6 collective-permute-start.5
  28.6 5.1 %collective-permute-start.1 = (bf16[4,128,256]{2,1,0:T(8,128)(2,1)S(1)}, bf16[4,128,256]{2,1,0:T(8,128)(2,1)S(1)}, u32[]{:S(2)}, u32[]{:S(2)}) collective-permute-start(bf16[4,128,256]{2,1,0:T(8,128)(2,1)S(1)} %get-tuple-element.26), channel_id=1, source_target_pairs={{0,8},{1,121},{8,16},{9,1},{16,24},{17,9},{24,32},{25,17},{32,40},... | collective-permute-start | bytes 786440 | tf_op jit(solution)/shard_map/ppermute | solution.py:36
  33.7 4.1 %collective-permute-start.4 = (bf16[4,192,128]{2,1,0:T(8,128)(2,1)S(1)}, bf16[4,192,128]{2,1,0:T(8,128)(2,1)S(1)}, u32[]{:S(2)}, u32[]{:S(2)}) collective-permute-start(bf16[4,192,128]{2,1,0:T(8,128)(2,1)S(1)} %get-tuple-element.28), channel_id=1, source_target_pairs={{0,2},{2,4},{4,6},{1,3},{3,5},{5,7},{8,10},{10,12},{12,14},{9,11},... | collective-permute-start | bytes 589832 | tf_op jit(solution)/shard_map/ppermute | solution.py:26
  37.9 2.9 %work.14 = (f32[4,128,256]{2,1,0:T(8,128)S(1)}, bf16[7,4,2,96,128]{4,3,2,1,0:T(8,128)(2,1)S(1)}) custom-call(s32[1,64]{1,0:T(1,128)S(1)} %copy-done.1, bf16[16,128,128]{2,1,0:T(8,128)(2,1)S(1)} %get-tuple-element.23.refs_1_, bf16[16,32,128]{2,1,0:T(8,128)(2,1)S(1)} %get-tuple-element.24.refs_2_, ...), custom_call_target="tpu_custom_call" | custom-call | flops 75497472 | bytes 294912 | tf_op jit(solution)/shard_map/work/pallas_call | solution.py:247
  40.8 0.2 work.15.refs_1_
  41.1 0.3 settle.4.refs_5_
  41.4 1.0 work.16
  42.6 1.8 %collective-permute-start.10 = (bf16[4,128,256]{2,1,0:T(8,128)(2,1)S(1)}, bf16[4,128,256]{2,1,0:T(8,128)(2,1)S(1)}, u32[]{:S(2)}, u32[]{:S(2)}) collective-permute-start(bf16[4,128,256]{2,1,0:T(8,128)(2,1)S(1)} %work.15.refs_1_), channel_id=1, source_target_pairs={{0,8},{1,121},{8,16},{9,1},{16,24},{17,9},{24,32},{25,17},{32,40},... | collective-permute-start | bytes 786440 | tf_op jit(solution)/shard_map/ppermute | solution.py:36
  44.3 0.4 pack.3
  44.7 4.2 %collective-permute-start.9 = (bf16[9,192,128]{2,1,0:T(8,128)(2,1)S(1)}, bf16[9,192,128]{2,1,0:T(8,128)(2,1)S(1)}, u32[]{:S(2)}, u32[]{:S(2)}) collective-permute-start(bf16[9,192,128]{2,1,0:T(8,128)(2,1)S(1)} %pack.3), channel_id=1, source_target_pairs={{0,2},{2,4},{4,6},{1,3},{3,5},{5,7},{8,10},{10,12},{12,14},{9,11},... | collective-permute-start | bytes 1327112 | tf_op jit(solution)/shard_map/ppermute | solution.py:26
  48.9 0.4 collective-permute-start.3
  49.3 1.2 %work.17 = (f32[4,128,256]{2,1,0:T(8,128)S(1)}, f32[4,128,256]{2,1,0:T(8,128)S(1)}) custom-call(s32[1,64]{1,0:T(1,128)S(1)} %copy-done.1, bf16[16,128,128]{2,1,0:T(8,128)(2,1)S(1)} %get-tuple-element.23.refs_1_, bf16[16,32,128]{2,1,0:T(8,128)(2,1)S(1)} %get-tuple-element.24.refs_2_, bf16[16,4,192,128]{3,2,1,0:T(8,128)(2,1)S(1)} %get-tuple-element.25.refs_3_.x_ref, ...), custom_call_target="tpu_custom_call" | custom-call | flops 125829120 | bytes 491520 | tf_op jit(solution)/shard_map/work/pallas_call | solution.py:247
  50.6 0.3 collective-permute-start.11
  50.9 3.4 %collective-permute-done.3 = bf16[4,128,256]{2,1,0:T(8,128)(2,1)S(1)} collective-permute-done((bf16[4,128,256]{2,1,0:T(8,128)(2,1)S(1)}, bf16[4,128,256]{2,1,0:T(8,128)(2,1)S(1)}, u32[]{:S(2)}, u32[]{:S(2)}) %collective-permute-start.3) | collective-permute-done | bytes 262176 | tf_op jit(solution)/shard_map/ppermute | solution.py:36
  54.4 1.4 %collective-permute-start.7 = (bf16[4,128,256]{2,1,0:T(8,128)(2,1)S(1)}, bf16[4,128,256]{2,1,0:T(8,128)(2,1)S(1)}, u32[]{:S(2)}, u32[]{:S(2)}) collective-permute-start(bf16[4,128,256]{2,1,0:T(8,128)(2,1)S(1)} %add_convert_fusion.11), channel_id=1, source_target_pairs={{0,8},{1,121},{8,16},{9,1},{16,24},{17,9},{24,32},{25,17},{32,40},... | collective-permute-start | bytes 786440 | tf_op jit(solution)/shard_map/ppermute | solution.py:36
  55.9 1.2 %work.18 = (f32[4,128,256]{2,1,0:T(8,128)S(1)}, f32[4,128,256]{2,1,0:T(8,128)S(1)}) custom-call(s32[1,64]{1,0:T(1,128)S(1)} %copy-done.1, bf16[16,128,128]{2,1,0:T(8,128)(2,1)S(1)} %get-tuple-element.23.refs_1_, bf16[16,32,128]{2,1,0:T(8,128)(2,1)S(1)} %get-tuple-element.24.refs_2_, bf16[16,4,192,128]{3,2,1,0:T(8,128)(2,1)S(1)} %get-tuple-element.25.refs_3_.x_ref, ...), custom_call_target="tpu_custom_call" | custom-call | flops 125829120 | bytes 491520 | tf_op jit(solution)/shard_map/work/pallas_call | solution.py:247
  57.1 0.3 collective-permute-done.11
  57.4 2.7 %collective-permute-done.7 = bf16[4,128,256]{2,1,0:T(8,128)(2,1)S(1)} collective-permute-done((bf16[4,128,256]{2,1,0:T(8,128)(2,1)S(1)}, bf16[4,128,256]{2,1,0:T(8,128)(2,1)S(1)}, u32[]{:S(2)}, u32[]{:S(2)}) %collective-permute-start.7) | collective-permute-done | bytes 262176 | tf_op jit(solution)/shard_map/ppermute | solution.py:36
  60.2 0.3 settle.6.refs_5_
  60.5 1.4 %work.20 = bf16[4,4,128,256]{3,2,1,0:T(8,128)(2,1)S(1)} custom-call(s32[1,64]{1,0:T(1,128)S(1)} %copy-done.1, bf16[16,128,128]{2,1,0:T(8,128)(2,1)S(1)} %get-tuple-element.23.refs_1_, bf16[16,32,128]{2,1,0:T(8,128)(2,1)S(1)} %get-tuple-element.24.refs_2_, bf16[16,4,192,128]{3,2,1,0:T(8,128)(2,1)S(1)} %get-tuple-element.25.refs_3_.x_ref, ...), custom_call_target="tpu_custom_call" | custom-call | flops 100663296 | bytes 393216 | tf_op jit(solution)/shard_map/work/pallas_call | solution.py:247
  61.9 2.5 %collective-permute-start.13 = (bf16[4,4,128,256]{3,2,1,0:T(8,128)(2,1)S(1)}, bf16[4,4,128,256]{3,2,1,0:T(8,128)(2,1)S(1)}, u32[]{:S(2)}, u32[]{:S(2)}) collective-permute-start(bf16[4,4,128,256]{3,2,1,0:T(8,128)(2,1)S(1)} %work.20), channel_id=1, source_target_pairs={{0,1},{1,0},{2,3},{3,2},{4,5},{5,4},{6,7},{7,6},{8,9},{9,8},{10,11... | collective-permute-start | bytes 3145736 | tf_op jit(solution)/shard_map/ppermute | solution.py:41
  64.4 0.5 collective-permute-start.17
  64.9 1.1 %collective-permute-start.8 = (bf16[4,128,256]{2,1,0:T(8,128)(2,1)S(1)}, bf16[4,128,256]{2,1,0:T(8,128)(2,1)S(1)}, u32[]{:S(2)}, u32[]{:S(2)}) collective-permute-start(bf16[4,128,256]{2,1,0:T(8,128)(2,1)S(1)} %add_convert_fusion.10.refs_0_), channel_id=1, source_target_pairs={{0,8},{1,121},{8,16},{9,1},{16,24},{17,9},{24,32},{25,17},{32,40},... | collective-permute-start | bytes 786440 | tf_op jit(solution)/shard_map/ppermute | solution.py:36
  65.9 1.0 work.19
  67.3 2.6 %collective-permute-done.17 = bf16[4,128,256]{2,1,0:T(8,128)(2,1)S(1)} collective-permute-done((bf16[4,128,256]{2,1,0:T(8,128)(2,1)S(1)}, bf16[4,128,256]{2,1,0:T(8,128)(2,1)S(1)}, u32[]{:S(2)}, u32[]{:S(2)}) %collective-permute-start.17) | collective-permute-done | bytes 262176 | tf_op jit(solution)/shard_map/ppermute | solution.py:36
  69.9 1.5 %collective-permute-start.18 = (bf16[4,128,256]{2,1,0:T(8,128)(2,1)S(1)}, bf16[4,128,256]{2,1,0:T(8,128)(2,1)S(1)}, u32[]{:S(2)}, u32[]{:S(2)}) collective-permute-start(bf16[4,128,256]{2,1,0:T(8,128)(2,1)S(1)} %add_convert_fusion.3), channel_id=1, source_target_pairs={{0,8},{1,121},{8,16},{9,1},{16,24},{17,9},{24,32},{25,17},{32,40},... | collective-permute-start | bytes 786440 | tf_op jit(solution)/shard_map/ppermute | solution.py:36
  71.5 1.2 %collective-permute-done.8 = bf16[4,128,256]{2,1,0:T(8,128)(2,1)S(1)} collective-permute-done((bf16[4,128,256]{2,1,0:T(8,128)(2,1)S(1)}, bf16[4,128,256]{2,1,0:T(8,128)(2,1)S(1)}, u32[]{:S(2)}, u32[]{:S(2)}) %collective-permute-start.8) | collective-permute-done | bytes 262176 | tf_op jit(solution)/shard_map/ppermute | solution.py:36
  72.8 1.5 %collective-permute-start.12 = (bf16[4,128,256]{2,1,0:T(8,128)(2,1)S(1)}, bf16[4,128,256]{2,1,0:T(8,128)(2,1)S(1)}, u32[]{:S(2)}, u32[]{:S(2)}) collective-permute-start(bf16[4,128,256]{2,1,0:T(8,128)(2,1)S(1)} %add_convert_fusion.7), channel_id=1, source_target_pairs={{0,8},{1,121},{8,16},{9,1},{16,24},{17,9},{24,32},{25,17},{32,40},... | collective-permute-start | bytes 786440 | tf_op jit(solution)/shard_map/ppermute | solution.py:36
  74.3 1.2 %work.21 = (f32[4,128,256]{2,1,0:T(8,128)S(1)}, f32[4,128,256]{2,1,0:T(8,128)S(1)}) custom-call(s32[1,64]{1,0:T(1,128)S(1)} %copy-done.1, bf16[16,128,128]{2,1,0:T(8,128)(2,1)S(1)} %get-tuple-element.23.refs_1_, bf16[16,32,128]{2,1,0:T(8,128)(2,1)S(1)} %get-tuple-element.24.refs_2_, bf16[16,4,192,128]{3,2,1,0:T(8,128)(2,1)S(1)} %get-tuple-element.25.refs_3_.x_ref, ...), custom_call_target="tpu_custom_call" | custom-call | flops 125829120 | bytes 491520 | tf_op jit(solution)/shard_map/work/pallas_call | solution.py:247
  75.6 2.5 %collective-permute-start.19 = (bf16[4,128,256]{2,1,0:T(8,128)(2,1)S(1)}, bf16[4,128,256]{2,1,0:T(8,128)(2,1)S(1)}, u32[]{:S(2)}, u32[]{:S(2)}) collective-permute-start(bf16[4,128,256]{2,1,0:T(8,128)(2,1)S(1)} %add_convert_fusion.2), channel_id=1, source_target_pairs={{0,8},{1,121},{8,16},{9,1},{16,24},{17,9},{24,32},{25,17},{32,40},... | collective-permute-start | bytes 786440 | tf_op jit(solution)/shard_map/ppermute | solution.py:36
  78.1 0.3 collective-permute-done.12
  78.5 2.5 %collective-permute-start.14 = (bf16[4,128,256]{2,1,0:T(8,128)(2,1)S(1)}, bf16[4,128,256]{2,1,0:T(8,128)(2,1)S(1)}, u32[]{:S(2)}, u32[]{:S(2)}) collective-permute-start(bf16[4,128,256]{2,1,0:T(8,128)(2,1)S(1)} %add_convert_fusion.6), channel_id=1, source_target_pairs={{0,8},{1,121},{8,16},{9,1},{16,24},{17,9},{24,32},{25,17},{32,40},... | collective-permute-start | bytes 786440 | tf_op jit(solution)/shard_map/ppermute | solution.py:36
  80.9 1.2 %work.22 = (f32[4,128,256]{2,1,0:T(8,128)S(1)}, f32[4,128,256]{2,1,0:T(8,128)S(1)}) custom-call(s32[1,64]{1,0:T(1,128)S(1)} %copy-done.1, bf16[16,128,128]{2,1,0:T(8,128)(2,1)S(1)} %get-tuple-element.23.refs_1_, bf16[16,32,128]{2,1,0:T(8,128)(2,1)S(1)} %get-tuple-element.24.refs_2_, bf16[16,4,192,128]{3,2,1,0:T(8,128)(2,1)S(1)} %get-tuple-element.25.refs_3_.x_ref, ...), custom_call_target="tpu_custom_call" | custom-call | flops 125829120 | bytes 491520 | tf_op jit(solution)/shard_map/work/pallas_call | solution.py:247
  82.2 2.5 %collective-permute-start.20 = (bf16[4,128,256]{2,1,0:T(8,128)(2,1)S(1)}, bf16[4,128,256]{2,1,0:T(8,128)(2,1)S(1)}, u32[]{:S(2)}, u32[]{:S(2)}) collective-permute-start(bf16[4,128,256]{2,1,0:T(8,128)(2,1)S(1)} %add_convert_fusion.1), channel_id=1, source_target_pairs={{0,8},{1,121},{8,16},{9,1},{16,24},{17,9},{24,32},{25,17},{32,40},... | collective-permute-start | bytes 786440 | tf_op jit(solution)/shard_map/ppermute | solution.py:36
  84.7 1.2 %work.23 = (f32[4,128,256]{2,1,0:T(8,128)S(1)}, f32[4,128,256]{2,1,0:T(8,128)S(1)}) custom-call(s32[1,64]{1,0:T(1,128)S(1)} %copy-done.1, bf16[16,128,128]{2,1,0:T(8,128)(2,1)S(1)} %get-tuple-element.23.refs_1_, bf16[16,32,128]{2,1,0:T(8,128)(2,1)S(1)} %get-tuple-element.24.refs_2_, bf16[16,4,192,128]{3,2,1,0:T(8,128)(2,1)S(1)} %get-tuple-element.25.refs_3_.x_ref, ...), custom_call_target="tpu_custom_call" | custom-call | flops 125829120 | bytes 491520 | tf_op jit(solution)/shard_map/work/pallas_call | solution.py:247
  86.0 1.5 %collective-permute-start.15 = (bf16[4,128,256]{2,1,0:T(8,128)(2,1)S(1)}, bf16[4,128,256]{2,1,0:T(8,128)(2,1)S(1)}, u32[]{:S(2)}, u32[]{:S(2)}) collective-permute-start(bf16[4,128,256]{2,1,0:T(8,128)(2,1)S(1)} %add_convert_fusion.5), channel_id=1, source_target_pairs={{0,8},{1,121},{8,16},{9,1},{16,24},{17,9},{24,32},{25,17},{32,40},... | collective-permute-start | bytes 786440 | tf_op jit(solution)/shard_map/ppermute | solution.py:36
  87.5 0.5 collective-permute-done.20
  88.1 3.2 %collective-permute-start.21 = (bf16[4,128,256]{2,1,0:T(8,128)(2,1)S(1)}, bf16[4,128,256]{2,1,0:T(8,128)(2,1)S(1)}, u32[]{:S(2)}, u32[]{:S(2)}) collective-permute-start(bf16[4,128,256]{2,1,0:T(8,128)(2,1)S(1)} %add_convert_fusion), channel_id=1, source_target_pairs={{0,8},{1,121},{8,16},{9,1},{16,24},{17,9},{24,32},{25,17},{32,40},... | collective-permute-start | bytes 786440 | tf_op jit(solution)/shard_map/ppermute | solution.py:36
  91.4 2.7 %collective-permute-start.16 = (bf16[4,128,256]{2,1,0:T(8,128)(2,1)S(1)}, bf16[4,128,256]{2,1,0:T(8,128)(2,1)S(1)}, u32[]{:S(2)}, u32[]{:S(2)}) collective-permute-start(bf16[4,128,256]{2,1,0:T(8,128)(2,1)S(1)} %add_convert_fusion.4), channel_id=1, source_target_pairs={{0,8},{1,121},{8,16},{9,1},{16,24},{17,9},{24,32},{25,17},{32,40},... | collective-permute-start | bytes 786440 | tf_op jit(solution)/shard_map/ppermute | solution.py:36
  94.1 0.5 collective-permute-done.21
  94.6 8.5 %collective-permute-start.22 = (bf16[4,128,256]{2,1,0:T(8,128)(2,1)S(1)}, bf16[4,128,256]{2,1,0:T(8,128)(2,1)S(1)}, u32[]{:S(2)}, u32[]{:S(2)}) collective-permute-start(bf16[4,128,256]{2,1,0:T(8,128)(2,1)S(1)} %collective-permute-done.21), channel_id=1, source_target_pairs={{0,1},{1,0},{2,3},{3,2},{4,5},{5,4},{6,7},{7,6},{8,9},{9,8},{10,11... | collective-permute-start | bytes 786440 | tf_op jit(solution)/shard_map/ppermute | solution.py:41
  103.1 1.0 work.25.own_ref
  104.3 0.9 finish.1
  (38 shorter events, 1.5 us)
Async XLA Ops:
  0.0 23.8 %copy-start.2 = (bf16[16,16]{1,0:T(8,128)(2,1)S(1)}, bf16[16,16]{1,0:T(8,128)(2,1)}, u32[]{:S(2)}) copy-start(bf16[16,16]{1,0:T(8,128)(2,1)} %table_ref.1) | copy-start | bytes 1540
  0.0 37.9 %collective-permute-start.2 = (bf16[16,4,2,96,128]{4,3,2,1,0:T(8,128)(2,1)}, bf16[16,4,2,96,128]{4,3,2,1,0:T(8,128)(2,1)S(1)}, u32[]{:S(2)}, u32[]{:S(2)}) collective-permute-start(bf16[16,4,2,96,128]{4,3,2,1,0:T(8,128)(2,1)} %bitcast.2), channel_id=1, source_target_pairs={{0,1},{1,0},{2,3},{3,2},{4,5},{5,4},{6,7},{7,6},{8,9},{9,8},{10,11... | collective-permute-start | bytes 9437192 | tf_op jit(solution)/shard_map/ppermute | solution.py:41
  20.4 6.3 %copy-start = (bf16[1,64,2,96,128]{4,3,2,1,0:T(8,128)(2,1)S(1)}, bf16[1,64,2,96,128]{4,3,2,1,0:T(8,128)(2,1)}, u32[]{:S(2)}) copy-start(bf16[1,64,2,96,128]{4,3,2,1,0:T(8,128)(2,1)} %param.9) | copy-start | bytes 9437188
  20.4 6.3 %copy-start.1 = (s32[1,64]{1,0:T(1,128)S(1)}, s32[1,64]{1,0:T(1,128)}, u32[]{:S(2)}) copy-start(s32[1,64]{1,0:T(1,128)} %refs_0_.21) | copy-start | bytes 772
  21.9 4.9 %collective-permute-start = (bf16[3,192,128]{2,1,0:T(8,128)(2,1)S(1)}, bf16[3,192,128]{2,1,0:T(8,128)(2,1)S(1)}, u32[]{:S(2)}, u32[]{:S(2)}) collective-permute-start(bf16[3,192,128]{2,1,0:T(8,128)(2,1)S(1)} %pack.2), channel_id=1, source_target_pairs={{0,2},{2,4},{4,6},{1,3},{3,5},{5,7},{8,10},{10,12},{12,14},{9,11},... | collective-permute-start | bytes 442376 | tf_op jit(solution)/shard_map/ppermute | solution.py:26
  28.0 12.8 %collective-permute-start.5 = (bf16[1,4,128,256]{3,2,1,0:T(8,128)(2,1)S(1)}, bf16[1,4,128,256]{3,2,1,0:T(8,128)(2,1)S(1)}, u32[]{:S(2)}, u32[]{:S(2)}) collective-permute-start(bf16[1,4,128,256]{3,2,1,0:T(8,128)(2,1)S(1)} %get-tuple-element.29), channel_id=1, source_target_pairs={{0,1},{1,0},{2,3},{3,2},{4,5},{5,4},{6,7},{7,6},{8,9},{9,8},{10,11... | collective-permute-start | bytes 786440 | tf_op jit(solution)/shard_map/ppermute | solution.py:41
  28.6 12.4 %collective-permute-start.1 = (bf16[4,128,256]{2,1,0:T(8,128)(2,1)S(1)}, bf16[4,128,256]{2,1,0:T(8,128)(2,1)S(1)}, u32[]{:S(2)}, u32[]{:S(2)}) collective-permute-start(bf16[4,128,256]{2,1,0:T(8,128)(2,1)S(1)} %get-tuple-element.26), channel_id=1, source_target_pairs={{0,8},{1,121},{8,16},{9,1},{16,24},{17,9},{24,32},{25,17},{32,40},... | collective-permute-start | bytes 786440 | tf_op jit(solution)/shard_map/ppermute | solution.py:36
  33.7 7.4 %collective-permute-start.4 = (bf16[4,192,128]{2,1,0:T(8,128)(2,1)S(1)}, bf16[4,192,128]{2,1,0:T(8,128)(2,1)S(1)}, u32[]{:S(2)}, u32[]{:S(2)}) collective-permute-start(bf16[4,192,128]{2,1,0:T(8,128)(2,1)S(1)} %get-tuple-element.28), channel_id=1, source_target_pairs={{0,2},{2,4},{4,6},{1,3},{3,5},{5,7},{8,10},{10,12},{12,14},{9,11},... | collective-permute-start | bytes 589832 | tf_op jit(solution)/shard_map/ppermute | solution.py:26
  42.4 6.9 %collective-permute-start.6 = (bf16[2,4,128,256]{3,2,1,0:T(8,128)(2,1)S(1)}, bf16[2,4,128,256]{3,2,1,0:T(8,128)(2,1)S(1)}, u32[]{:S(2)}, u32[]{:S(2)}) collective-permute-start(bf16[2,4,128,256]{3,2,1,0:T(8,128)(2,1)S(1)} %work.16), channel_id=1, source_target_pairs={{0,1},{1,0},{2,3},{3,2},{4,5},{5,4},{6,7},{7,6},{8,9},{9,8},{10,11... | collective-permute-start | bytes 1572872 | tf_op jit(solution)/shard_map/ppermute | solution.py:41
  42.6 8.0 %collective-permute-start.10 = (bf16[4,128,256]{2,1,0:T(8,128)(2,1)S(1)}, bf16[4,128,256]{2,1,0:T(8,128)(2,1)S(1)}, u32[]{:S(2)}, u32[]{:S(2)}) collective-permute-start(bf16[4,128,256]{2,1,0:T(8,128)(2,1)S(1)} %work.15.refs_1_), channel_id=1, source_target_pairs={{0,8},{1,121},{8,16},{9,1},{16,24},{17,9},{24,32},{25,17},{32,40},... | collective-permute-start | bytes 786440 | tf_op jit(solution)/shard_map/ppermute | solution.py:36
  44.7 15.5 %collective-permute-start.9 = (bf16[9,192,128]{2,1,0:T(8,128)(2,1)S(1)}, bf16[9,192,128]{2,1,0:T(8,128)(2,1)S(1)}, u32[]{:S(2)}, u32[]{:S(2)}) collective-permute-start(bf16[9,192,128]{2,1,0:T(8,128)(2,1)S(1)} %pack.3), channel_id=1, source_target_pairs={{0,2},{2,4},{4,6},{1,3},{3,5},{5,7},{8,10},{10,12},{12,14},{9,11},... | collective-permute-start | bytes 1327112 | tf_op jit(solution)/shard_map/ppermute | solution.py:26
  48.9 5.5 %collective-permute-start.3 = (bf16[4,128,256]{2,1,0:T(8,128)(2,1)S(1)}, bf16[4,128,256]{2,1,0:T(8,128)(2,1)S(1)}, u32[]{:S(2)}, u32[]{:S(2)}) collective-permute-start(bf16[4,128,256]{2,1,0:T(8,128)(2,1)S(1)} %add_convert_fusion.12.refs_0_), channel_id=1, source_target_pairs={{0,8},{1,121},{8,16},{9,1},{16,24},{17,9},{24,32},{25,17},{32,40},... | collective-permute-start | bytes 786440 | tf_op jit(solution)/shard_map/ppermute | solution.py:36
  50.6 6.7 %collective-permute-start.11 = (bf16[4,128,256]{2,1,0:T(8,128)(2,1)S(1)}, bf16[4,128,256]{2,1,0:T(8,128)(2,1)S(1)}, u32[]{:S(2)}, u32[]{:S(2)}) collective-permute-start(bf16[4,128,256]{2,1,0:T(8,128)(2,1)S(1)} %add_convert_fusion.9), channel_id=1, source_target_pairs={{0,8},{1,121},{8,16},{9,1},{16,24},{17,9},{24,32},{25,17},{32,40},... | collective-permute-start | bytes 786440 | tf_op jit(solution)/shard_map/ppermute | solution.py:36
  54.4 5.7 %collective-permute-start.7 = (bf16[4,128,256]{2,1,0:T(8,128)(2,1)S(1)}, bf16[4,128,256]{2,1,0:T(8,128)(2,1)S(1)}, u32[]{:S(2)}, u32[]{:S(2)}) collective-permute-start(bf16[4,128,256]{2,1,0:T(8,128)(2,1)S(1)} %add_convert_fusion.11), channel_id=1, source_target_pairs={{0,8},{1,121},{8,16},{9,1},{16,24},{17,9},{24,32},{25,17},{32,40},... | collective-permute-start | bytes 786440 | tf_op jit(solution)/shard_map/ppermute | solution.py:36
  61.9 5.1 %collective-permute-start.13 = (bf16[4,4,128,256]{3,2,1,0:T(8,128)(2,1)S(1)}, bf16[4,4,128,256]{3,2,1,0:T(8,128)(2,1)S(1)}, u32[]{:S(2)}, u32[]{:S(2)}) collective-permute-start(bf16[4,4,128,256]{3,2,1,0:T(8,128)(2,1)S(1)} %work.20), channel_id=1, source_target_pairs={{0,1},{1,0},{2,3},{3,2},{4,5},{5,4},{6,7},{7,6},{8,9},{9,8},{10,11... | collective-permute-start | bytes 3145736 | tf_op jit(solution)/shard_map/ppermute | solution.py:41
  64.4 5.5 %collective-permute-start.17 = (bf16[4,128,256]{2,1,0:T(8,128)(2,1)S(1)}, bf16[4,128,256]{2,1,0:T(8,128)(2,1)S(1)}, u32[]{:S(2)}, u32[]{:S(2)}) collective-permute-start(bf16[4,128,256]{2,1,0:T(8,128)(2,1)S(1)} %add_convert_fusion.8.refs_1_), channel_id=1, source_target_pairs={{0,8},{1,121},{8,16},{9,1},{16,24},{17,9},{24,32},{25,17},{32,40},... | collective-permute-start | bytes 786440 | tf_op jit(solution)/shard_map/ppermute | solution.py:36
  64.9 7.8 %collective-permute-start.8 = (bf16[4,128,256]{2,1,0:T(8,128)(2,1)S(1)}, bf16[4,128,256]{2,1,0:T(8,128)(2,1)S(1)}, u32[]{:S(2)}, u32[]{:S(2)}) collective-permute-start(bf16[4,128,256]{2,1,0:T(8,128)(2,1)S(1)} %add_convert_fusion.10.refs_0_), channel_id=1, source_target_pairs={{0,8},{1,121},{8,16},{9,1},{16,24},{17,9},{24,32},{25,17},{32,40},... | collective-permute-start | bytes 786440 | tf_op jit(solution)/shard_map/ppermute | solution.py:36
  69.9 5.6 %collective-permute-start.18 = (bf16[4,128,256]{2,1,0:T(8,128)(2,1)S(1)}, bf16[4,128,256]{2,1,0:T(8,128)(2,1)S(1)}, u32[]{:S(2)}, u32[]{:S(2)}) collective-permute-start(bf16[4,128,256]{2,1,0:T(8,128)(2,1)S(1)} %add_convert_fusion.3), channel_id=1, source_target_pairs={{0,8},{1,121},{8,16},{9,1},{16,24},{17,9},{24,32},{25,17},{32,40},... | collective-permute-start | bytes 786440 | tf_op jit(solution)/shard_map/ppermute | solution.py:36
  72.8 5.6 %collective-permute-start.12 = (bf16[4,128,256]{2,1,0:T(8,128)(2,1)S(1)}, bf16[4,128,256]{2,1,0:T(8,128)(2,1)S(1)}, u32[]{:S(2)}, u32[]{:S(2)}) collective-permute-start(bf16[4,128,256]{2,1,0:T(8,128)(2,1)S(1)} %add_convert_fusion.7), channel_id=1, source_target_pairs={{0,8},{1,121},{8,16},{9,1},{16,24},{17,9},{24,32},{25,17},{32,40},... | collective-permute-start | bytes 786440 | tf_op jit(solution)/shard_map/ppermute | solution.py:36
  75.6 6.5 %collective-permute-start.19 = (bf16[4,128,256]{2,1,0:T(8,128)(2,1)S(1)}, bf16[4,128,256]{2,1,0:T(8,128)(2,1)S(1)}, u32[]{:S(2)}, u32[]{:S(2)}) collective-permute-start(bf16[4,128,256]{2,1,0:T(8,128)(2,1)S(1)} %add_convert_fusion.2), channel_id=1, source_target_pairs={{0,8},{1,121},{8,16},{9,1},{16,24},{17,9},{24,32},{25,17},{32,40},... | collective-permute-start | bytes 786440 | tf_op jit(solution)/shard_map/ppermute | solution.py:36
  78.5 7.5 %collective-permute-start.14 = (bf16[4,128,256]{2,1,0:T(8,128)(2,1)S(1)}, bf16[4,128,256]{2,1,0:T(8,128)(2,1)S(1)}, u32[]{:S(2)}, u32[]{:S(2)}) collective-permute-start(bf16[4,128,256]{2,1,0:T(8,128)(2,1)S(1)} %add_convert_fusion.6), channel_id=1, source_target_pairs={{0,8},{1,121},{8,16},{9,1},{16,24},{17,9},{24,32},{25,17},{32,40},... | collective-permute-start | bytes 786440 | tf_op jit(solution)/shard_map/ppermute | solution.py:36
  82.2 5.8 %collective-permute-start.20 = (bf16[4,128,256]{2,1,0:T(8,128)(2,1)S(1)}, bf16[4,128,256]{2,1,0:T(8,128)(2,1)S(1)}, u32[]{:S(2)}, u32[]{:S(2)}) collective-permute-start(bf16[4,128,256]{2,1,0:T(8,128)(2,1)S(1)} %add_convert_fusion.1), channel_id=1, source_target_pairs={{0,8},{1,121},{8,16},{9,1},{16,24},{17,9},{24,32},{25,17},{32,40},... | collective-permute-start | bytes 786440 | tf_op jit(solution)/shard_map/ppermute | solution.py:36
  86.0 5.3 %collective-permute-start.15 = (bf16[4,128,256]{2,1,0:T(8,128)(2,1)S(1)}, bf16[4,128,256]{2,1,0:T(8,128)(2,1)S(1)}, u32[]{:S(2)}, u32[]{:S(2)}) collective-permute-start(bf16[4,128,256]{2,1,0:T(8,128)(2,1)S(1)} %add_convert_fusion.5), channel_id=1, source_target_pairs={{0,8},{1,121},{8,16},{9,1},{16,24},{17,9},{24,32},{25,17},{32,40},... | collective-permute-start | bytes 786440 | tf_op jit(solution)/shard_map/ppermute | solution.py:36
  88.1 6.5 %collective-permute-start.21 = (bf16[4,128,256]{2,1,0:T(8,128)(2,1)S(1)}, bf16[4,128,256]{2,1,0:T(8,128)(2,1)S(1)}, u32[]{:S(2)}, u32[]{:S(2)}) collective-permute-start(bf16[4,128,256]{2,1,0:T(8,128)(2,1)S(1)} %add_convert_fusion), channel_id=1, source_target_pairs={{0,8},{1,121},{8,16},{9,1},{16,24},{17,9},{24,32},{25,17},{32,40},... | collective-permute-start | bytes 786440 | tf_op jit(solution)/shard_map/ppermute | solution.py:36
  91.4 12.8 %collective-permute-start.16 = (bf16[4,128,256]{2,1,0:T(8,128)(2,1)S(1)}, bf16[4,128,256]{2,1,0:T(8,128)(2,1)S(1)}, u32[]{:S(2)}, u32[]{:S(2)}) collective-permute-start(bf16[4,128,256]{2,1,0:T(8,128)(2,1)S(1)} %add_convert_fusion.4), channel_id=1, source_target_pairs={{0,8},{1,121},{8,16},{9,1},{16,24},{17,9},{24,32},{25,17},{32,40},... | collective-permute-start | bytes 786440 | tf_op jit(solution)/shard_map/ppermute | solution.py:36
  94.6 9.7 %collective-permute-start.22 = (bf16[4,128,256]{2,1,0:T(8,128)(2,1)S(1)}, bf16[4,128,256]{2,1,0:T(8,128)(2,1)S(1)}, u32[]{:S(2)}, u32[]{:S(2)}) collective-permute-start(bf16[4,128,256]{2,1,0:T(8,128)(2,1)S(1)} %collective-permute-done.21), channel_id=1, source_target_pairs={{0,1},{1,0},{2,3},{3,2},{4,5},{5,4},{6,7},{7,6},{8,9},{9,8},{10,11... | collective-permute-start | bytes 786440 | tf_op jit(solution)/shard_map/ppermute | solution.py:41

commit v4 on v3

--- a/solution.py
+++ b/solution.py
@@ -164,18 +164,9 @@
 FILTER, STEER, BOTH = range(3)
 
 
-def work_kernel(jobs, count, rows, names, fetch, *refs):
+def work_kernel(jobs, count, rows, names, *refs):
     held = dict(zip(names, refs))
     outs = refs[len(names) :]
-    copies = []
-    if fetch:
-        *outs, near_ref, sem = outs
-        copies = [
-            pltpu.make_async_copy(held["raw"].at[chunk_index(o, count)], near_ref.at[i], sem.at[i])
-            for i, o in enumerate(fetch)
-        ]
-        for copy in copies:
-            copy.start()
     nt = (((1,), (1,)), ((), ()))
     filters = 0
     for i, (what, offset, place) in enumerate(jobs):
@@ -201,7 +192,7 @@
         if what == BOTH:
             w_ref = held["w"].at[chunk]
         elif what == STEER:
-            w_ref = held["other_w"].at[held["other_w"].shape[0] - offset]
+            w_ref = held["other_w"].at[chunk]
         for q in range(rows):
             if what == STEER:
                 delayed = held["given"][place, q, :, : 2 * w_ref.shape[-2]]
@@ -226,39 +217,29 @@
                 axis=0,
             )
             out[q] = jnp.dot(delayed, steer, preferred_element_type=jnp.float32).astype(out.dtype)
-    for copy in copies:
-        copy.wait()
-
-
-def work(jobs, dtypes, rows, count, length, height, width, fetch=(), **arrays):
+
+
+def work(jobs, dtypes, rows, count, length, height, width, **arrays):
     names = tuple(arrays)
     shapes = [pltpu.VMEM((rows, length, width), dtype) for dtype in dtypes]
     filters = sum(what == FILTER for what, _, _ in jobs)
     if filters:
         lanes = (height + 127) // 128 * 128
         shapes.append(pltpu.VMEM((filters, rows, length, lanes), jnp.bfloat16))
-    if fetch:
-        shapes.append(pltpu.VMEM((len(fetch),) + arrays["raw"].shape[1:], arrays["raw"].dtype))
     flops = 0
     for what, _, _ in jobs:
         flops += 2 * rows * length * height * (
             (0 if what == STEER else length) + (0 if what == FILTER else width)
         )
     return pl.pallas_call(
-        functools.partial(work_kernel, jobs, count, rows, names, fetch),
+        functools.partial(work_kernel, jobs, count, rows, names),
         out_shape=tuple(shapes),
-        in_specs=[{"sets": SMEM, "raw": ANY}.get(name, VMEM) for name in names],
+        in_specs=[SMEM if name == "sets" else VMEM for name in names],
         out_specs=(VMEM,) * len(shapes),
-        scratch_shapes=[pltpu.SemaphoreType.DMA((len(fetch),))] if fetch else [],
         cost_estimate=pl.CostEstimate(flops=flops, bytes_accessed=flops // 256, transcendentals=0),
         compiler_params=PARAMS,
         name="work",
-    )(
-        *[
-            value if name == "raw" else near(value, pltpu.SMEM if name == "sets" else pltpu.VMEM)
-            for name, value in arrays.items()
-        ]
-    )
+    )(*[near(value, pltpu.SMEM if name == "sets" else pltpu.VMEM) for name, value in arrays.items()])
 
 
 def finish_kernel(right_ref, left_ref, own_ref, out_ref):
@@ -325,10 +306,7 @@
     a_got = onward(a)
     given = {1: (across_cores(handed), 0)}
     halo, place = halos[half - 1]
-    own, other_w = work(
-        ((BOTH, half - 1, place),), [wide], *sizes, **common, halo=halo,
-        fetch=tuple(half - s for s in range(1, half)), raw=other_w,
-    )
+    (own,) = work(((BOTH, half - 1, place),), [wide], *sizes, **common, halo=halo)
     second = from_earlier(second)
     packed = pack(near_x, pieces[2], True)
     (b,) = work(

time: 106 us -> 107 us (level)
  starting transfers between devices: 70.3 us -> 72.2 us
  Pallas kernels: 21.3 us -> 19.4 us
  waiting for transfers between devices: 11.7 us -> 13.2 us
    ppermute x3, waiting for transfers between devices: 0.01 us -> 2.34 us  [from_earlier(): lax.ppermute(value, 'tm', [(i, i + 1) for i in range(lax.axis_size('tm')...]
    pallas_call x13, Pallas kernels: 15.1 us -> 13.3 us  [work(): pl.pallas_call(functools.partial(work_kernel, jobs, count, rows, names),...]
    ppermute x5, starting transfers between devices: 32.1 us -> 33.8 us  [across_cores(): lax.ppermute(value, 'chan', [(i, (i + 1) % cores) for i in range(cores)])]
    ppermute x15, waiting for transfers between devices: 11.6 us -> 9.95 us  [onward(): return lax.ppermute(value, ('station', 'chan'), pairs)]
  transfers between devices with their start and end apart: 23 -> 23, of which waited for: 9 -> 10; matrix products, arithmetic and copies ran while one was open for 1% -> 1% of each run, Pallas kernels for 17% -> 15%
where the time goes in v4:
time: 107 us
  starting transfers between devices  72.2 us (67%)
  Pallas kernels  19.4 us (18%)
  waiting for transfers between devices  13.2 us (12%)
    ppermute x5, starting transfers between devices, across_cores(): lax.ppermute(value, 'chan', [(i, (i + 1) % cores) for i in range(cores)])  33.8 us
    ppermute x15, starting transfers between devices, onward(): return lax.ppermute(value, ('station', 'chan'), pairs)  29.2 us
    pallas_call x13, Pallas kernels, work(): pl.pallas_call(functools.partial(work_kernel, jobs, count, rows, names),...  13.3 us
    ppermute x15, waiting for transfers between devices, onward(): return lax.ppermute(value, ('station', 'chan'), pairs)  9.95 us
    ppermute x3, starting transfers between devices, from_earlier(): lax.ppermute(value, 'tm', [(i, i + 1) for i in range(lax.axis_size('tm')...  9.2 us
    pallas_call x1, Pallas kernels, bank(): pl.pallas_call(functools.partial(bank_kernel, offsets, x.shape[0]), out_s...  2.86 us
    ppermute x3, waiting for transfers between devices, from_earlier(): lax.ppermute(value, 'tm', [(i, i + 1) for i in range(lax.axis_size('tm')...  2.34 us
  transfers between devices with their start and end apart: 23, of which 10 were waited for; matrix products, arithmetic and copies ran while one was open for 1% of the time, Pallas kernels for 15%

profile of v4, /device:TPU:33, one launch (start us, length us, event | category | flops | bytes accessed | tf_op | source)
XLA Modules:
  0.0 106.6 jit_solution(11288275201847964465)
XLA Ops:
  0.0 20.4 %collective-permute-start.5 = (bf16[16,4,2,96,128]{4,3,2,1,0:T(8,128)(2,1)}, bf16[16,4,2,96,128]{4,3,2,1,0:T(8,128)(2,1)S(1)}, u32[]{:S(2)}, u32[]{:S(2)}) collective-permute-start(bf16[16,4,2,96,128]{4,3,2,1,0:T(8,128)(2,1)} %bitcast.2), channel_id=1, source_target_pairs={{0,1},{1,0},{2,3},{3,2},{4,5},{5,4},{6,7},{7,6},{8,9},{9,8},{10,11... | collective-permute-start | bytes 9437192 | tf_op jit(solution)/shard_map/ppermute | solution.py:41
  20.4 1.4 %pack.2 = bf16[3,192,128]{2,1,0:T(8,128)(2,1)S(1)} custom-call(bf16[16,4,192,128]{3,2,1,0:T(8,128)(2,1)} %bitcast.14), custom_call_target="tpu_custom_call" | custom-call | tf_op jit(solution)/shard_map/pack/pallas_call | solution.py:84
  21.9 1.3 %collective-permute-start = (bf16[3,192,128]{2,1,0:T(8,128)(2,1)S(1)}, bf16[3,192,128]{2,1,0:T(8,128)(2,1)S(1)}, u32[]{:S(2)}, u32[]{:S(2)}) collective-permute-start(bf16[3,192,128]{2,1,0:T(8,128)(2,1)S(1)} %pack.2), channel_id=1, source_target_pairs={{0,2},{2,4},{4,6},{1,3},{3,5},{5,7},{8,10},{10,12},{12,14},{9,11},... | collective-permute-start | bytes 442376 | tf_op jit(solution)/shard_map/ppermute | solution.py:26
  23.8 2.9 %bank.1 = (bf16[16,128,128]{2,1,0:T(8,128)(2,1)S(1)}, bf16[16,32,128]{2,1,0:T(8,128)(2,1)S(1)}, bf16[16,4,192,128]{3,2,1,0:T(8,128)(2,1)S(1)}, bf16[4,192,128]{2,1,0:T(8,128)(2,1)S(1)}) custom-call(s32[1]{0:T(128)S(6)} %copy.6.delay_ref, bf16[16,16]{1,0:T(8,128)(2,1)S(1)} %copy-done.2, bf16[16,4,192,128]{3,2,1,0:T(8,128)(2,1)} %bitcast.15), custom_call_target="tpu_custom_call" | custom-call | tf_op jit(solution)/shard_map/bank/pallas_call | solution.py:129
  26.7 1.3 %work.13 = (bf16[4,128,256]{2,1,0:T(8,128)(2,1)S(1)}, bf16[1,4,128,256]{3,2,1,0:T(8,128)(2,1)S(1)}) custom-call(s32[1,64]{1,0:T(1,128)S(1)} %copy-done.1, bf16[16,128,128]{2,1,0:T(8,128)(2,1)S(1)} %get-tuple-element.21.refs_1_, bf16[16,32,128]{2,1,0:T(8,128)(2,1)S(1)} %get-tuple-element.22.refs_2_, ...), custom_call_target="tpu_custom_call" | custom-call | flops 100663296 | bytes 393216 | tf_op jit(solution)/shard_map/work/pallas_call | solution.py:234
  28.0 5.2 %collective-permute-start.1 = (bf16[4,128,256]{2,1,0:T(8,128)(2,1)S(1)}, bf16[4,128,256]{2,1,0:T(8,128)(2,1)S(1)}, u32[]{:S(2)}, u32[]{:S(2)}) collective-permute-start(bf16[4,128,256]{2,1,0:T(8,128)(2,1)S(1)} %get-tuple-element.24), channel_id=1, source_target_pairs={{0,8},{1,121},{8,16},{9,1},{16,24},{17,9},{24,32},{25,17},{32,40},... | collective-permute-start | bytes 786440 | tf_op jit(solution)/shard_map/ppermute | solution.py:36
  33.2 3.7 %collective-permute-start.3 = (bf16[4,192,128]{2,1,0:T(8,128)(2,1)S(1)}, bf16[4,192,128]{2,1,0:T(8,128)(2,1)S(1)}, u32[]{:S(2)}, u32[]{:S(2)}) collective-permute-start(bf16[4,192,128]{2,1,0:T(8,128)(2,1)S(1)} %get-tuple-element.25), channel_id=1, source_target_pairs={{0,2},{2,4},{4,6},{1,3},{3,5},{5,7},{8,10},{10,12},{12,14},{9,11},... | collective-permute-start | bytes 589832 | tf_op jit(solution)/shard_map/ppermute | solution.py:26
  37.0 1.0 work.14
  38.1 0.2 work.15.refs_1_
  38.4 2.3 %collective-permute-done.3.value_ref = bf16[4,192,128]{2,1,0:T(8,128)(2,1)S(1)} collective-permute-done((bf16[4,192,128]{2,1,0:T(8,128)(2,1)S(1)}, bf16[4,192,128]{2,1,0:T(8,128)(2,1)S(1)}, u32[]{:S(2)}, u32[]{:S(2)}) %collective-permute-start.3) | collective-permute-done | bytes 196640 | tf_op jit(solution)/shard_map/ppermute | solution.py:26
  40.7 0.2 settle.4.refs_5_
  40.9 1.0 work.16
  41.9 1.5 %collective-permute-start.6 = (bf16[2,4,128,256]{3,2,1,0:T(8,128)(2,1)S(1)}, bf16[2,4,128,256]{3,2,1,0:T(8,128)(2,1)S(1)}, u32[]{:S(2)}, u32[]{:S(2)}) collective-permute-start(bf16[2,4,128,256]{3,2,1,0:T(8,128)(2,1)S(1)} %work.16), channel_id=1, source_target_pairs={{0,1},{1,0},{2,3},{3,2},{4,5},{5,4},{6,7},{7,6},{8,9},{9,8},{10,11... | collective-permute-start | bytes 1572872 | tf_op jit(solution)/shard_map/ppermute | solution.py:41
  43.4 1.0 collective-permute-start.10
  44.5 0.4 pack.3
  44.9 4.2 %collective-permute-start.9 = (bf16[9,192,128]{2,1,0:T(8,128)(2,1)S(1)}, bf16[9,192,128]{2,1,0:T(8,128)(2,1)S(1)}, u32[]{:S(2)}, u32[]{:S(2)}) collective-permute-start(bf16[9,192,128]{2,1,0:T(8,128)(2,1)S(1)} %pack.3), channel_id=1, source_target_pairs={{0,2},{2,4},{4,6},{1,3},{3,5},{5,7},{8,10},{10,12},{12,14},{9,11},... | collective-permute-start | bytes 1327112 | tf_op jit(solution)/shard_map/ppermute | solution.py:26
  49.0 1.7 %collective-permute-start.2 = (bf16[4,128,256]{2,1,0:T(8,128)(2,1)S(1)}, bf16[4,128,256]{2,1,0:T(8,128)(2,1)S(1)}, u32[]{:S(2)}, u32[]{:S(2)}) collective-permute-start(bf16[4,128,256]{2,1,0:T(8,128)(2,1)S(1)} %add_convert_fusion.12.refs_0_), channel_id=1, source_target_pairs={{0,8},{1,121},{8,16},{9,1},{16,24},{17,9},{24,32},{25,17},{32,40},... | collective-permute-start | bytes 786440 | tf_op jit(solution)/shard_map/ppermute | solution.py:36
  50.8 1.2 %work.17 = (f32[4,128,256]{2,1,0:T(8,128)S(1)}, f32[4,128,256]{2,1,0:T(8,128)S(1)}) custom-call(s32[1,64]{1,0:T(1,128)S(1)} %copy-done.1, bf16[16,128,128]{2,1,0:T(8,128)(2,1)S(1)} %get-tuple-element.21.refs_1_, bf16[16,32,128]{2,1,0:T(8,128)(2,1)S(1)} %get-tuple-element.22.refs_2_, bf16[16,4,192,128]{3,2,1,0:T(8,128)(2,1)S(1)} %get-tuple-element.23.refs_3_.x_ref, ...), custom_call_target="tpu_custom_call" | custom-call | flops 125829120 | bytes 491520 | tf_op jit(solution)/shard_map/work/pallas_call | solution.py:234
  52.3 2.4 %collective-permute-done.2 = bf16[4,128,256]{2,1,0:T(8,128)(2,1)S(1)} collective-permute-done((bf16[4,128,256]{2,1,0:T(8,128)(2,1)S(1)}, bf16[4,128,256]{2,1,0:T(8,128)(2,1)S(1)}, u32[]{:S(2)}, u32[]{:S(2)}) %collective-permute-start.2) | collective-permute-done | bytes 262176 | tf_op jit(solution)/shard_map/ppermute | solution.py:36
  54.7 2.6 %collective-permute-start.7 = (bf16[4,128,256]{2,1,0:T(8,128)(2,1)S(1)}, bf16[4,128,256]{2,1,0:T(8,128)(2,1)S(1)}, u32[]{:S(2)}, u32[]{:S(2)}) collective-permute-start(bf16[4,128,256]{2,1,0:T(8,128)(2,1)S(1)} %add_convert_fusion.11), channel_id=1, source_target_pairs={{0,8},{1,121},{8,16},{9,1},{16,24},{17,9},{24,32},{25,17},{32,40},... | collective-permute-start | bytes 786440 | tf_op jit(solution)/shard_map/ppermute | solution.py:36
  57.4 1.2 %work.18 = (f32[4,128,256]{2,1,0:T(8,128)S(1)}, f32[4,128,256]{2,1,0:T(8,128)S(1)}) custom-call(s32[1,64]{1,0:T(1,128)S(1)} %copy-done.1, bf16[16,128,128]{2,1,0:T(8,128)(2,1)S(1)} %get-tuple-element.21.refs_1_, bf16[16,32,128]{2,1,0:T(8,128)(2,1)S(1)} %get-tuple-element.22.refs_2_, bf16[16,4,192,128]{3,2,1,0:T(8,128)(2,1)S(1)} %get-tuple-element.23.refs_3_.x_ref, ...), custom_call_target="tpu_custom_call" | custom-call | flops 125829120 | bytes 491520 | tf_op jit(solution)/shard_map/work/pallas_call | solution.py:234
  58.7 2.0 %collective-permute-done.7 = bf16[4,128,256]{2,1,0:T(8,128)(2,1)S(1)} collective-permute-done((bf16[4,128,256]{2,1,0:T(8,128)(2,1)S(1)}, bf16[4,128,256]{2,1,0:T(8,128)(2,1)S(1)}, u32[]{:S(2)}, u32[]{:S(2)}) %collective-permute-start.7) | collective-permute-done | bytes 262176 | tf_op jit(solution)/shard_map/ppermute | solution.py:36
  60.8 0.3 settle.6.refs_5_
  61.0 1.3 %work.20 = bf16[4,4,128,256]{3,2,1,0:T(8,128)(2,1)S(1)} custom-call(s32[1,64]{1,0:T(1,128)S(1)} %copy-done.1, bf16[16,128,128]{2,1,0:T(8,128)(2,1)S(1)} %get-tuple-element.21.refs_1_, bf16[16,32,128]{2,1,0:T(8,128)(2,1)S(1)} %get-tuple-element.22.refs_2_, bf16[16,4,192,128]{3,2,1,0:T(8,128)(2,1)S(1)} %get-tuple-element.23.refs_3_.x_ref, ...), custom_call_target="tpu_custom_call" | custom-call | flops 100663296 | bytes 393216 | tf_op jit(solution)/shard_map/work/pallas_call | solution.py:234
  62.4 3.4 %collective-permute-start.13 = (bf16[4,4,128,256]{3,2,1,0:T(8,128)(2,1)S(1)}, bf16[4,4,128,256]{3,2,1,0:T(8,128)(2,1)S(1)}, u32[]{:S(2)}, u32[]{:S(2)}) collective-permute-start(bf16[4,4,128,256]{3,2,1,0:T(8,128)(2,1)S(1)} %work.20), channel_id=1, source_target_pairs={{0,1},{1,0},{2,3},{3,2},{4,5},{5,4},{6,7},{7,6},{8,9},{9,8},{10,11... | collective-permute-start | bytes 3145736 | tf_op jit(solution)/shard_map/ppermute | solution.py:41
  65.8 0.5 collective-permute-start.17
  66.3 1.0 work.19
  67.3 0.7 collective-permute-done.13.value_ref
  68.1 0.2 work.24
  68.4 2.9 %collective-permute-done.17 = bf16[4,128,256]{2,1,0:T(8,128)(2,1)S(1)} collective-permute-done((bf16[4,128,256]{2,1,0:T(8,128)(2,1)S(1)}, bf16[4,128,256]{2,1,0:T(8,128)(2,1)S(1)}, u32[]{:S(2)}, u32[]{:S(2)}) %collective-permute-start.17) | collective-permute-done | bytes 262176 | tf_op jit(solution)/shard_map/ppermute | solution.py:36
  71.4 1.5 %collective-permute-start.18 = (bf16[4,128,256]{2,1,0:T(8,128)(2,1)S(1)}, bf16[4,128,256]{2,1,0:T(8,128)(2,1)S(1)}, u32[]{:S(2)}, u32[]{:S(2)}) collective-permute-start(bf16[4,128,256]{2,1,0:T(8,128)(2,1)S(1)} %add_convert_fusion.3), channel_id=1, source_target_pairs={{0,8},{1,121},{8,16},{9,1},{16,24},{17,9},{24,32},{25,17},{32,40},... | collective-permute-start | bytes 786440 | tf_op jit(solution)/shard_map/ppermute | solution.py:36
  72.9 1.2 %collective-permute-done.8 = bf16[4,128,256]{2,1,0:T(8,128)(2,1)S(1)} collective-permute-done((bf16[4,128,256]{2,1,0:T(8,128)(2,1)S(1)}, bf16[4,128,256]{2,1,0:T(8,128)(2,1)S(1)}, u32[]{:S(2)}, u32[]{:S(2)}) %collective-permute-start.8) | collective-permute-done | bytes 262176 | tf_op jit(solution)/shard_map/ppermute | solution.py:36
  74.2 1.5 %collective-permute-start.12 = (bf16[4,128,256]{2,1,0:T(8,128)(2,1)S(1)}, bf16[4,128,256]{2,1,0:T(8,128)(2,1)S(1)}, u32[]{:S(2)}, u32[]{:S(2)}) collective-permute-start(bf16[4,128,256]{2,1,0:T(8,128)(2,1)S(1)} %add_convert_fusion.7), channel_id=1, source_target_pairs={{0,8},{1,121},{8,16},{9,1},{16,24},{17,9},{24,32},{25,17},{32,40},... | collective-permute-start | bytes 786440 | tf_op jit(solution)/shard_map/ppermute | solution.py:36
  75.7 1.2 %work.21 = (f32[4,128,256]{2,1,0:T(8,128)S(1)}, f32[4,128,256]{2,1,0:T(8,128)S(1)}) custom-call(s32[1,64]{1,0:T(1,128)S(1)} %copy-done.1, bf16[16,128,128]{2,1,0:T(8,128)(2,1)S(1)} %get-tuple-element.21.refs_1_, bf16[16,32,128]{2,1,0:T(8,128)(2,1)S(1)} %get-tuple-element.22.refs_2_, bf16[16,4,192,128]{3,2,1,0:T(8,128)(2,1)S(1)} %get-tuple-element.23.refs_3_.x_ref, ...), custom_call_target="tpu_custom_call" | custom-call | flops 125829120 | bytes 491520 | tf_op jit(solution)/shard_map/work/pallas_call | solution.py:234
  77.0 2.5 %collective-permute-start.19 = (bf16[4,128,256]{2,1,0:T(8,128)(2,1)S(1)}, bf16[4,128,256]{2,1,0:T(8,128)(2,1)S(1)}, u32[]{:S(2)}, u32[]{:S(2)}) collective-permute-start(bf16[4,128,256]{2,1,0:T(8,128)(2,1)S(1)} %add_convert_fusion.2), channel_id=1, source_target_pairs={{0,8},{1,121},{8,16},{9,1},{16,24},{17,9},{24,32},{25,17},{32,40},... | collective-permute-start | bytes 786440 | tf_op jit(solution)/shard_map/ppermute | solution.py:36
  79.5 0.3 collective-permute-done.12
  79.9 2.4 %collective-permute-start.14 = (bf16[4,128,256]{2,1,0:T(8,128)(2,1)S(1)}, bf16[4,128,256]{2,1,0:T(8,128)(2,1)S(1)}, u32[]{:S(2)}, u32[]{:S(2)}) collective-permute-start(bf16[4,128,256]{2,1,0:T(8,128)(2,1)S(1)} %add_convert_fusion.6), channel_id=1, source_target_pairs={{0,8},{1,121},{8,16},{9,1},{16,24},{17,9},{24,32},{25,17},{32,40},... | collective-permute-start | bytes 786440 | tf_op jit(solution)/shard_map/ppermute | solution.py:36
  82.3 1.2 %work.22 = (f32[4,128,256]{2,1,0:T(8,128)S(1)}, f32[4,128,256]{2,1,0:T(8,128)S(1)}) custom-call(s32[1,64]{1,0:T(1,128)S(1)} %copy-done.1, bf16[16,128,128]{2,1,0:T(8,128)(2,1)S(1)} %get-tuple-element.21.refs_1_, bf16[16,32,128]{2,1,0:T(8,128)(2,1)S(1)} %get-tuple-element.22.refs_2_, bf16[16,4,192,128]{3,2,1,0:T(8,128)(2,1)S(1)} %get-tuple-element.23.refs_3_.x_ref, ...), custom_call_target="tpu_custom_call" | custom-call | flops 125829120 | bytes 491520 | tf_op jit(solution)/shard_map/work/pallas_call | solution.py:234
  83.6 2.5 %collective-permute-start.20 = (bf16[4,128,256]{2,1,0:T(8,128)(2,1)S(1)}, bf16[4,128,256]{2,1,0:T(8,128)(2,1)S(1)}, u32[]{:S(2)}, u32[]{:S(2)}) collective-permute-start(bf16[4,128,256]{2,1,0:T(8,128)(2,1)S(1)} %add_convert_fusion.1), channel_id=1, source_target_pairs={{0,8},{1,121},{8,16},{9,1},{16,24},{17,9},{24,32},{25,17},{32,40},... | collective-permute-start | bytes 786440 | tf_op jit(solution)/shard_map/ppermute | solution.py:36
  86.1 1.2 %work.23 = (f32[4,128,256]{2,1,0:T(8,128)S(1)}, f32[4,128,256]{2,1,0:T(8,128)S(1)}) custom-call(s32[1,64]{1,0:T(1,128)S(1)} %copy-done.1, bf16[16,128,128]{2,1,0:T(8,128)(2,1)S(1)} %get-tuple-element.21.refs_1_, bf16[16,32,128]{2,1,0:T(8,128)(2,1)S(1)} %get-tuple-element.22.refs_2_, bf16[16,4,192,128]{3,2,1,0:T(8,128)(2,1)S(1)} %get-tuple-element.23.refs_3_.x_ref, ...), custom_call_target="tpu_custom_call" | custom-call | flops 125829120 | bytes 491520 | tf_op jit(solution)/shard_map/work/pallas_call | solution.py:234
  87.4 1.5 %collective-permute-start.15 = (bf16[4,128,256]{2,1,0:T(8,128)(2,1)S(1)}, bf16[4,128,256]{2,1,0:T(8,128)(2,1)S(1)}, u32[]{:S(2)}, u32[]{:S(2)}) collective-permute-start(bf16[4,128,256]{2,1,0:T(8,128)(2,1)S(1)} %add_convert_fusion.5), channel_id=1, source_target_pairs={{0,8},{1,121},{8,16},{9,1},{16,24},{17,9},{24,32},{25,17},{32,40},... | collective-permute-start | bytes 786440 | tf_op jit(solution)/shard_map/ppermute | solution.py:36
  88.9 0.5 collective-permute-done.20
  89.5 3.2 %collective-permute-start.21 = (bf16[4,128,256]{2,1,0:T(8,128)(2,1)S(1)}, bf16[4,128,256]{2,1,0:T(8,128)(2,1)S(1)}, u32[]{:S(2)}, u32[]{:S(2)}) collective-permute-start(bf16[4,128,256]{2,1,0:T(8,128)(2,1)S(1)} %add_convert_fusion), channel_id=1, source_target_pairs={{0,8},{1,121},{8,16},{9,1},{16,24},{17,9},{24,32},{25,17},{32,40},... | collective-permute-start | bytes 786440 | tf_op jit(solution)/shard_map/ppermute | solution.py:36
  92.8 2.7 %collective-permute-start.16 = (bf16[4,128,256]{2,1,0:T(8,128)(2,1)S(1)}, bf16[4,128,256]{2,1,0:T(8,128)(2,1)S(1)}, u32[]{:S(2)}, u32[]{:S(2)}) collective-permute-start(bf16[4,128,256]{2,1,0:T(8,128)(2,1)S(1)} %add_convert_fusion.4), channel_id=1, source_target_pairs={{0,8},{1,121},{8,16},{9,1},{16,24},{17,9},{24,32},{25,17},{32,40},... | collective-permute-start | bytes 786440 | tf_op jit(solution)/shard_map/ppermute | solution.py:36
  95.5 0.5 collective-permute-done.21
  96.0 8.5 %collective-permute-start.22 = (bf16[4,128,256]{2,1,0:T(8,128)(2,1)S(1)}, bf16[4,128,256]{2,1,0:T(8,128)(2,1)S(1)}, u32[]{:S(2)}, u32[]{:S(2)}) collective-permute-start(bf16[4,128,256]{2,1,0:T(8,128)(2,1)S(1)} %collective-permute-done.21), channel_id=1, source_target_pairs={{0,1},{1,0},{2,3},{3,2},{4,5},{5,4},{6,7},{7,6},{8,9},{9,8},{10,11... | collective-permute-start | bytes 786440 | tf_op jit(solution)/shard_map/ppermute | solution.py:41
  104.5 1.0 work.25.own_ref
  105.7 0.9 finish.1
  (38 shorter events, 1.3 us)
Async XLA Ops:
  0.0 23.8 %copy-start.2 = (bf16[16,16]{1,0:T(8,128)(2,1)S(1)}, bf16[16,16]{1,0:T(8,128)(2,1)}, u32[]{:S(2)}) copy-start(bf16[16,16]{1,0:T(8,128)(2,1)} %table_ref.1) | copy-start | bytes 1540
  0.0 38.1 %collective-permute-start.5 = (bf16[16,4,2,96,128]{4,3,2,1,0:T(8,128)(2,1)}, bf16[16,4,2,96,128]{4,3,2,1,0:T(8,128)(2,1)S(1)}, u32[]{:S(2)}, u32[]{:S(2)}) collective-permute-start(bf16[16,4,2,96,128]{4,3,2,1,0:T(8,128)(2,1)} %bitcast.2), channel_id=1, source_target_pairs={{0,1},{1,0},{2,3},{3,2},{4,5},{5,4},{6,7},{7,6},{8,9},{9,8},{10,11... | collective-permute-start | bytes 9437192 | tf_op jit(solution)/shard_map/ppermute | solution.py:41
  20.4 6.3 %copy-start = (bf16[1,64,2,96,128]{4,3,2,1,0:T(8,128)(2,1)S(1)}, bf16[1,64,2,96,128]{4,3,2,1,0:T(8,128)(2,1)}, u32[]{:S(2)}) copy-start(bf16[1,64,2,96,128]{4,3,2,1,0:T(8,128)(2,1)} %param.9) | copy-start | bytes 9437188
  20.4 6.3 %copy-start.1 = (s32[1,64]{1,0:T(1,128)S(1)}, s32[1,64]{1,0:T(1,128)}, u32[]{:S(2)}) copy-start(s32[1,64]{1,0:T(1,128)} %refs_0_.21) | copy-start | bytes 772
  21.9 4.9 %collective-permute-start = (bf16[3,192,128]{2,1,0:T(8,128)(2,1)S(1)}, bf16[3,192,128]{2,1,0:T(8,128)(2,1)S(1)}, u32[]{:S(2)}, u32[]{:S(2)}) collective-permute-start(bf16[3,192,128]{2,1,0:T(8,128)(2,1)S(1)} %pack.2), channel_id=1, source_target_pairs={{0,2},{2,4},{4,6},{1,3},{3,5},{5,7},{8,10},{10,12},{12,14},{9,11},... | collective-permute-start | bytes 442376 | tf_op jit(solution)/shard_map/ppermute | solution.py:26
  28.0 10.0 %collective-permute-start.1 = (bf16[4,128,256]{2,1,0:T(8,128)(2,1)S(1)}, bf16[4,128,256]{2,1,0:T(8,128)(2,1)S(1)}, u32[]{:S(2)}, u32[]{:S(2)}) collective-permute-start(bf16[4,128,256]{2,1,0:T(8,128)(2,1)S(1)} %get-tuple-element.24), channel_id=1, source_target_pairs={{0,8},{1,121},{8,16},{9,1},{16,24},{17,9},{24,32},{25,17},{32,40},... | collective-permute-start | bytes 786440 | tf_op jit(solution)/shard_map/ppermute | solution.py:36
  33.2 4.9 %collective-permute-start.4 = (bf16[1,4,128,256]{3,2,1,0:T(8,128)(2,1)S(1)}, bf16[1,4,128,256]{3,2,1,0:T(8,128)(2,1)S(1)}, u32[]{:S(2)}, u32[]{:S(2)}) collective-permute-start(bf16[1,4,128,256]{3,2,1,0:T(8,128)(2,1)S(1)} %get-tuple-element.26), channel_id=1, source_target_pairs={{0,1},{1,0},{2,3},{3,2},{4,5},{5,4},{6,7},{7,6},{8,9},{9,8},{10,11... | collective-permute-start | bytes 786440 | tf_op jit(solution)/shard_map/ppermute | solution.py:41
  33.2 7.5 %collective-permute-start.3 = (bf16[4,192,128]{2,1,0:T(8,128)(2,1)S(1)}, bf16[4,192,128]{2,1,0:T(8,128)(2,1)S(1)}, u32[]{:S(2)}, u32[]{:S(2)}) collective-permute-start(bf16[4,192,128]{2,1,0:T(8,128)(2,1)S(1)} %get-tuple-element.25), channel_id=1, source_target_pairs={{0,2},{2,4},{4,6},{1,3},{3,5},{5,7},{8,10},{10,12},{12,14},{9,11},... | collective-permute-start | bytes 589832 | tf_op jit(solution)/shard_map/ppermute | solution.py:26
  41.9 8.8 %collective-permute-start.6 = (bf16[2,4,128,256]{3,2,1,0:T(8,128)(2,1)S(1)}, bf16[2,4,128,256]{3,2,1,0:T(8,128)(2,1)S(1)}, u32[]{:S(2)}, u32[]{:S(2)}) collective-permute-start(bf16[2,4,128,256]{3,2,1,0:T(8,128)(2,1)S(1)} %work.16), channel_id=1, source_target_pairs={{0,1},{1,0},{2,3},{3,2},{4,5},{5,4},{6,7},{7,6},{8,9},{9,8},{10,11... | collective-permute-start | bytes 1572872 | tf_op jit(solution)/shard_map/ppermute | solution.py:41
  43.4 8.6 %collective-permute-start.10 = (bf16[4,128,256]{2,1,0:T(8,128)(2,1)S(1)}, bf16[4,128,256]{2,1,0:T(8,128)(2,1)S(1)}, u32[]{:S(2)}, u32[]{:S(2)}) collective-permute-start(bf16[4,128,256]{2,1,0:T(8,128)(2,1)S(1)} %work.15.refs_1_), channel_id=1, source_target_pairs={{0,8},{1,121},{8,16},{9,1},{16,24},{17,9},{24,32},{25,17},{32,40},... | collective-permute-start | bytes 786440 | tf_op jit(solution)/shard_map/ppermute | solution.py:36
  44.9 15.9 %collective-permute-start.9 = (bf16[9,192,128]{2,1,0:T(8,128)(2,1)S(1)}, bf16[9,192,128]{2,1,0:T(8,128)(2,1)S(1)}, u32[]{:S(2)}, u32[]{:S(2)}) collective-permute-start(bf16[9,192,128]{2,1,0:T(8,128)(2,1)S(1)} %pack.3), channel_id=1, source_target_pairs={{0,2},{2,4},{4,6},{1,3},{3,5},{5,7},{8,10},{10,12},{12,14},{9,11},... | collective-permute-start | bytes 1327112 | tf_op jit(solution)/shard_map/ppermute | solution.py:26
  49.0 5.6 %collective-permute-start.2 = (bf16[4,128,256]{2,1,0:T(8,128)(2,1)S(1)}, bf16[4,128,256]{2,1,0:T(8,128)(2,1)S(1)}, u32[]{:S(2)}, u32[]{:S(2)}) collective-permute-start(bf16[4,128,256]{2,1,0:T(8,128)(2,1)S(1)} %add_convert_fusion.12.refs_0_), channel_id=1, source_target_pairs={{0,8},{1,121},{8,16},{9,1},{16,24},{17,9},{24,32},{25,17},{32,40},... | collective-permute-start | bytes 786440 | tf_op jit(solution)/shard_map/ppermute | solution.py:36
  52.1 6.5 %collective-permute-start.11 = (bf16[4,128,256]{2,1,0:T(8,128)(2,1)S(1)}, bf16[4,128,256]{2,1,0:T(8,128)(2,1)S(1)}, u32[]{:S(2)}, u32[]{:S(2)}) collective-permute-start(bf16[4,128,256]{2,1,0:T(8,128)(2,1)S(1)} %add_convert_fusion.9), channel_id=1, source_target_pairs={{0,8},{1,121},{8,16},{9,1},{16,24},{17,9},{24,32},{25,17},{32,40},... | collective-permute-start | bytes 786440 | tf_op jit(solution)/shard_map/ppermute | solution.py:36
  54.7 6.0 %collective-permute-start.7 = (bf16[4,128,256]{2,1,0:T(8,128)(2,1)S(1)}, bf16[4,128,256]{2,1,0:T(8,128)(2,1)S(1)}, u32[]{:S(2)}, u32[]{:S(2)}) collective-permute-start(bf16[4,128,256]{2,1,0:T(8,128)(2,1)S(1)} %add_convert_fusion.11), channel_id=1, source_target_pairs={{0,8},{1,121},{8,16},{9,1},{16,24},{17,9},{24,32},{25,17},{32,40},... | collective-permute-start | bytes 786440 | tf_op jit(solution)/shard_map/ppermute | solution.py:36
  62.4 5.7 %collective-permute-start.13 = (bf16[4,4,128,256]{3,2,1,0:T(8,128)(2,1)S(1)}, bf16[4,4,128,256]{3,2,1,0:T(8,128)(2,1)S(1)}, u32[]{:S(2)}, u32[]{:S(2)}) collective-permute-start(bf16[4,4,128,256]{3,2,1,0:T(8,128)(2,1)S(1)} %work.20), channel_id=1, source_target_pairs={{0,1},{1,0},{2,3},{3,2},{4,5},{5,4},{6,7},{7,6},{8,9},{9,8},{10,11... | collective-permute-start | bytes 3145736 | tf_op jit(solution)/shard_map/ppermute | solution.py:41
  65.8 5.5 %collective-permute-start.17 = (bf16[4,128,256]{2,1,0:T(8,128)(2,1)S(1)}, bf16[4,128,256]{2,1,0:T(8,128)(2,1)S(1)}, u32[]{:S(2)}, u32[]{:S(2)}) collective-permute-start(bf16[4,128,256]{2,1,0:T(8,128)(2,1)S(1)} %add_convert_fusion.8.refs_1_), channel_id=1, source_target_pairs={{0,8},{1,121},{8,16},{9,1},{16,24},{17,9},{24,32},{25,17},{32,40},... | collective-permute-start | bytes 786440 | tf_op jit(solution)/shard_map/ppermute | solution.py:36
  66.2 7.8 %collective-permute-start.8 = (bf16[4,128,256]{2,1,0:T(8,128)(2,1)S(1)}, bf16[4,128,256]{2,1,0:T(8,128)(2,1)S(1)}, u32[]{:S(2)}, u32[]{:S(2)}) collective-permute-start(bf16[4,128,256]{2,1,0:T(8,128)(2,1)S(1)} %add_convert_fusion.10.refs_0_), channel_id=1, source_target_pairs={{0,8},{1,121},{8,16},{9,1},{16,24},{17,9},{24,32},{25,17},{32,40},... | collective-permute-start | bytes 786440 | tf_op jit(solution)/shard_map/ppermute | solution.py:36
  71.4 5.5 %collective-permute-start.18 = (bf16[4,128,256]{2,1,0:T(8,128)(2,1)S(1)}, bf16[4,128,256]{2,1,0:T(8,128)(2,1)S(1)}, u32[]{:S(2)}, u32[]{:S(2)}) collective-permute-start(bf16[4,128,256]{2,1,0:T(8,128)(2,1)S(1)} %add_convert_fusion.3), channel_id=1, source_target_pairs={{0,8},{1,121},{8,16},{9,1},{16,24},{17,9},{24,32},{25,17},{32,40},... | collective-permute-start | bytes 786440 | tf_op jit(solution)/shard_map/ppermute | solution.py:36
  74.2 5.6 %collective-permute-start.12 = (bf16[4,128,256]{2,1,0:T(8,128)(2,1)S(1)}, bf16[4,128,256]{2,1,0:T(8,128)(2,1)S(1)}, u32[]{:S(2)}, u32[]{:S(2)}) collective-permute-start(bf16[4,128,256]{2,1,0:T(8,128)(2,1)S(1)} %add_convert_fusion.7), channel_id=1, source_target_pairs={{0,8},{1,121},{8,16},{9,1},{16,24},{17,9},{24,32},{25,17},{32,40},... | collective-permute-start | bytes 786440 | tf_op jit(solution)/shard_map/ppermute | solution.py:36
  77.0 6.5 %collective-permute-start.19 = (bf16[4,128,256]{2,1,0:T(8,128)(2,1)S(1)}, bf16[4,128,256]{2,1,0:T(8,128)(2,1)S(1)}, u32[]{:S(2)}, u32[]{:S(2)}) collective-permute-start(bf16[4,128,256]{2,1,0:T(8,128)(2,1)S(1)} %add_convert_fusion.2), channel_id=1, source_target_pairs={{0,8},{1,121},{8,16},{9,1},{16,24},{17,9},{24,32},{25,17},{32,40},... | collective-permute-start | bytes 786440 | tf_op jit(solution)/shard_map/ppermute | solution.py:36
  79.9 7.4 %collective-permute-start.14 = (bf16[4,128,256]{2,1,0:T(8,128)(2,1)S(1)}, bf16[4,128,256]{2,1,0:T(8,128)(2,1)S(1)}, u32[]{:S(2)}, u32[]{:S(2)}) collective-permute-start(bf16[4,128,256]{2,1,0:T(8,128)(2,1)S(1)} %add_convert_fusion.6), channel_id=1, source_target_pairs={{0,8},{1,121},{8,16},{9,1},{16,24},{17,9},{24,32},{25,17},{32,40},... | collective-permute-start | bytes 786440 | tf_op jit(solution)/shard_map/ppermute | solution.py:36
  83.6 5.8 %collective-permute-start.20 = (bf16[4,128,256]{2,1,0:T(8,128)(2,1)S(1)}, bf16[4,128,256]{2,1,0:T(8,128)(2,1)S(1)}, u32[]{:S(2)}, u32[]{:S(2)}) collective-permute-start(bf16[4,128,256]{2,1,0:T(8,128)(2,1)S(1)} %add_convert_fusion.1), channel_id=1, source_target_pairs={{0,8},{1,121},{8,16},{9,1},{16,24},{17,9},{24,32},{25,17},{32,40},... | collective-permute-start | bytes 786440 | tf_op jit(solution)/shard_map/ppermute | solution.py:36
  87.4 5.3 %collective-permute-start.15 = (bf16[4,128,256]{2,1,0:T(8,128)(2,1)S(1)}, bf16[4,128,256]{2,1,0:T(8,128)(2,1)S(1)}, u32[]{:S(2)}, u32[]{:S(2)}) collective-permute-start(bf16[4,128,256]{2,1,0:T(8,128)(2,1)S(1)} %add_convert_fusion.5), channel_id=1, source_target_pairs={{0,8},{1,121},{8,16},{9,1},{16,24},{17,9},{24,32},{25,17},{32,40},... | collective-permute-start | bytes 786440 | tf_op jit(solution)/shard_map/ppermute | solution.py:36
  89.5 6.5 %collective-permute-start.21 = (bf16[4,128,256]{2,1,0:T(8,128)(2,1)S(1)}, bf16[4,128,256]{2,1,0:T(8,128)(2,1)S(1)}, u32[]{:S(2)}, u32[]{:S(2)}) collective-permute-start(bf16[4,128,256]{2,1,0:T(8,128)(2,1)S(1)} %add_convert_fusion), channel_id=1, source_target_pairs={{0,8},{1,121},{8,16},{9,1},{16,24},{17,9},{24,32},{25,17},{32,40},... | collective-permute-start | bytes 786440 | tf_op jit(solution)/shard_map/ppermute | solution.py:36
  92.8 12.8 %collective-permute-start.16 = (bf16[4,128,256]{2,1,0:T(8,128)(2,1)S(1)}, bf16[4,128,256]{2,1,0:T(8,128)(2,1)S(1)}, u32[]{:S(2)}, u32[]{:S(2)}) collective-permute-start(bf16[4,128,256]{2,1,0:T(8,128)(2,1)S(1)} %add_convert_fusion.4), channel_id=1, source_target_pairs={{0,8},{1,121},{8,16},{9,1},{16,24},{17,9},{24,32},{25,17},{32,40},... | collective-permute-start | bytes 786440 | tf_op jit(solution)/shard_map/ppermute | solution.py:36
  96.0 9.7 %collective-permute-start.22 = (bf16[4,128,256]{2,1,0:T(8,128)(2,1)S(1)}, bf16[4,128,256]{2,1,0:T(8,128)(2,1)S(1)}, u32[]{:S(2)}, u32[]{:S(2)}) collective-permute-start(bf16[4,128,256]{2,1,0:T(8,128)(2,1)S(1)} %collective-permute-done.21), channel_id=1, source_target_pairs={{0,1},{1,0},{2,3},{3,2},{4,5},{5,4},{6,7},{7,6},{8,9},{9,8},{10,11... | collective-permute-start | bytes 786440 | tf_op jit(solution)/shard_map/ppermute | solution.py:41
